TPU v7x, 512 devices: a whole 4x8x8 slice. The times are simulated.
512 devices in a mesh: acq: 16 (over z, y_lo), line: 32 (over y_hi, x, core).
Axes of the slice: x: 4, y: 8 (y_hi: 4, y_lo: 2; y = y_hi * 2 + y_lo), z: 8, core: 2. Of those that a mesh axis runs over, the one named last changes fastest.
Arguments:
- slc_stack: float32 [2, 64, 256, 2048], P(None, 'acq', 'line'), may hold values from -6 to 6
- wavenumbers: float32 [64], replicated, may hold values from -0.8 to 0.8
Outputs:
- spectrum: bfloat16 [256, 256, 2048], P(None, 'line', 'acq')
All inputs are finite; a program needn't handle non-finite values.
Results may differ from a plain program's by a relative error of at most 0.001.
Values sent between devices are 32-bit elements; how exact they have to be, the bound alone decides.
No kernel may reach another device: no remote copies, remote signals or barrier semaphores. Data moves between devices by JAX's collectives and lax.ppermute only.
A program may use at most 64 MiB of HBM per device.

v0:
```python
import jax
import jax.numpy as jnp
from jax import lax
from jax.sharding import PartitionSpec as P

HEIGHTS = 256


epsilon = 1e-06


def in_blocks(x, dim, size):
    lengths = x.shape
    tiles = x.reshape(*lengths[:dim], size, lengths[dim] // size, *lengths[dim + 1 :])
    return jnp.moveaxis(tiles, dim, 0)


def edges_of(length, count):
    step = length // count
    if step >= 8:
        step -= step % 8
    return [step * k for k in range(1, count)]


def joined_along(tiles, dim):
    tiles = jnp.moveaxis(tiles, 0, dim)
    lengths = tiles.shape
    return tiles.reshape(*lengths[:dim], lengths[dim] * lengths[dim + 1], *lengths[dim + 2 :])


def cut_exchange(x, axis, pieces, split_dim, concat_dim):
    tiles = in_blocks(x, split_dim, lax.axis_size(axis))
    widest = max(range(1, max(2, tiles.ndim - 1)), key=lambda d: tiles.shape[d])
    outs = []
    for slab in jnp.split(tiles, edges_of(tiles.shape[widest], pieces), axis=widest):
        if slab.size:
            outs.append(lax.all_to_all(slab, axis, split_axis=0, concat_axis=0, tiled=True))
    return joined_along(jnp.concatenate(outs, axis=widest), concat_dim)


def with_halo(x, sides, width):
    for axis, dim in sides:
        size, length = (lax.axis_size(axis), x.shape[dim])
        up = [(i, (i + 1) % size) for i in range(size - 1)]
        down = [(j, i) for i, j in up]
        last = lax.slice_in_dim(x, length - width, length, axis=dim)
        first = lax.slice_in_dim(x, 0, width, axis=dim)
        before = lax.ppermute(last, axis, up)
        after = lax.ppermute(first, axis, down)
        x = jnp.concatenate([before, x, after], axis=dim)
    return x


def steering(wavenumbers, count):
    heights = jnp.arange(count, dtype=jnp.int32).astype(jnp.float32) - jnp.float32(count // 2)
    phases = wavenumbers[:, None] * heights[None, :]
    cosine_part = jnp.cos(phases).T
    sine_part = jnp.sin(phases).T
    upper = jnp.concatenate([cosine_part, sine_part], axis=1)
    lower = jnp.concatenate([-sine_part, cosine_part], axis=1)
    return jnp.concatenate([upper, lower], axis=0)


def beamform(stack_block, wavenumbers, count):
    matrix = steering(wavenumbers, count)
    channels = stack_block.shape[0] * stack_block.shape[1]
    flat = stack_block.reshape(channels, -1)
    beams = jnp.dot(
        matrix, flat, precision=lax.Precision.HIGHEST, preferred_element_type=jnp.float32
    )
    beam_power = beams[:count] * beams[:count] + beams[count:] * beams[count:]
    energy = jnp.sum(flat * flat, axis=0)
    shape = stack_block.shape[2:]
    return (beam_power.reshape((count,) + shape), energy.reshape((1,) + shape))


def sum_range(field, count):
    total = field[..., 0:count]
    for offset in range(1, 7):
        total = total + field[..., offset : offset + count]
    return total


def sum_lines(field, count):
    total = field[..., 0:count, :]
    for offset in range(1, 7):
        total = total + field[..., offset : offset + count, :]
    return total


def body(slc_stack, wavenumbers):
    regrouped = cut_exchange(slc_stack, "acq", 2, 3, 1)
    line_count = regrouped.shape[2]
    range_count = regrouped.shape[3]
    beam_power, energy = beamform(regrouped, wavenumbers, HEIGHTS)
    wide_power, wide_energy = (
        with_halo(beam_power, (("line", 1), ("acq", 2)), 3),
        with_halo(energy, (("line", 1), ("acq", 2)), 3),
    )
    box_power = sum_lines(sum_range(wide_power, range_count), line_count)
    box_energy = sum_lines(sum_range(wide_energy, range_count), line_count)
    return (box_power / (box_energy + epsilon)).astype(jnp.bfloat16)


def solution(mesh):
    placed = (P(None, "acq", "line", None), P())
    return jax.shard_map(
        body, mesh=mesh, in_specs=placed, out_specs=P(None, "line", "acq"), check_vma=False
    )
```

profile of v0, /device:TPU:40, one launch (start us, length us, event | category | flops | bytes accessed | tf_op | source)
XLA Modules:
  0.0 84.7 jit_solution(15488452211770101416)
XLA Ops:
  0.0 0.0 copy-start
  0.0 1.1 %copy.76 = f32[8,8,16,128]{3,2,1,0:T(8,128)S(1)} copy(f32[8,8,16,128]{3,1,2,0:T(8,128)} %bitcast.27) | data formatting | bytes 1048576
  1.2 0.8 copy.61
  2.0 11.8 %all-to-all-start = ((f32[16,2,4,4,128]{4,3,2,1,0:T(4,128)}), f32[16,2,4,4,128]{4,3,2,1,0:T(4,128)S(1)}, u32[]{:S(2)}, u32[]{:S(2)}) async-start(f32[16,2,4,4,128]{4,3,2,1,0:T(4,128)} %copy.61), calls=%async_computation | async-start | bytes 524288 | tf_op jit(solution)/shard_map/all_to_all | solution.py:37
  13.8 0.8 copy.62
  14.6 9.7 %all-to-all-done = f32[16,2,4,4,128]{4,3,2,1,0:T(4,128)S(1)} async-done(((f32[16,2,4,4,128]{4,3,2,1,0:T(4,128)}), f32[16,2,4,4,128]{4,3,2,1,0:T(4,128)S(1)}, u32[]{:S(2)}, u32[]{:S(2)}) %all-to-all-start) | async-done | bytes 262176 | tf_op jit(solution)/shard_map/all_to_all | solution.py:37
  24.3 4.5 %all-to-all-start.1 = ((f32[16,2,4,4,128]{4,3,2,1,0:T(4,128)}), f32[16,2,4,4,128]{4,3,2,1,0:T(4,128)S(1)}, u32[]{:S(2)}, u32[]{:S(2)}) async-start(f32[16,2,4,4,128]{4,3,2,1,0:T(4,128)} %copy.62), calls=%async_computation.1 | async-start | bytes 524288 | tf_op jit(solution)/shard_map/all_to_all | solution.py:37
  28.8 0.0 copy-done
  28.8 0.5 multiply_sine_fusion
  29.3 9.8 %all-to-all-done.1 = f32[16,2,4,4,128]{4,3,2,1,0:T(4,128)S(1)} async-done(((f32[16,2,4,4,128]{4,3,2,1,0:T(4,128)}), f32[16,2,4,4,128]{4,3,2,1,0:T(4,128)S(1)}, u32[]{:S(2)}, u32[]{:S(2)}) %all-to-all-start.1) | async-done | bytes 262176 | tf_op jit(solution)/shard_map/all_to_all | solution.py:37
  39.1 0.1 maximum_bitcast_fusion
  39.2 0.1 multiply_reduce_fusion
  39.4 1.9 %collective-permute-start.4 = (f32[1,3,128]{2,1,0:T(4,128)S(1)}, f32[1,3,128]{2,1,0:T(4,128)S(1)}, u32[]{:S(2)}, u32[]{:S(2)}) collective-permute-start(f32[1,3,128]{2,1,0:T(4,128)S(1)} %get-tuple-element.17), channel_id=1, source_target_pairs={{0,1},{1,2},{2,3},{3,4},{4,5},{5,6},{6,7},{7,8},{8,9},{9,10},{10,1... | collective-permute-start | bytes 4616 | tf_op jit(solution)/shard_map/ppermute | solution.py:48
  41.3 7.9 %collective-permute-start.5 = (f32[1,3,128]{2,1,0:T(4,128)S(1)}, f32[1,3,128]{2,1,0:T(4,128)S(1)}, u32[]{:S(2)}, u32[]{:S(2)}) collective-permute-start(f32[1,3,128]{2,1,0:T(4,128)S(1)} %get-tuple-element.18), channel_id=1, source_target_pairs={{1,0},{2,1},{3,2},{4,3},{5,4},{6,5},{7,6},{8,7},{9,8},{10,9},{11,1... | collective-permute-start | bytes 4616 | tf_op jit(solution)/shard_map/ppermute | solution.py:49
  49.2 1.9 %fusion.5 = f32[512,1024]{1,0:T(8,128)S(1)} fusion(f32[16,8,8,128]{3,2,1,0:T(8,128)S(1)} %bitcast.26, f32[256,64]{1,0:T(8,128)S(1)} %get-tuple-element.21, f32[256,64]{1,0:T(8,128)S(1)} %get-tuple-element.20, f32[256,64]{1,0:T(8,128)S(1)} %get-tuple-element.19), kind=kOutput, calls=%fused_computation.21 | convolution fusion | flops 805502976 | bytes 2818048 | tf_op jit(solution)/shard_map/dot_general | solution.py:68
  51.0 0.2 fusion.4
  51.3 0.2 copy.78
  51.5 0.2 fusion.20
  51.7 1.9 %collective-permute-start.1 = (f32[256,3,128]{2,0,1:T(8,128)S(1)}, f32[256,3,128]{2,0,1:T(8,128)}, u32[]{:S(2)}, u32[]{:S(2)}) collective-permute-start(f32[256,3,128]{2,0,1:T(8,128)S(1)} %copy.75), channel_id=1, source_target_pairs={{1,0},{2,1},{3,2},{4,3},{5,4},{6,5},{7,6},{8,7},{9,8},{10,9},{11,1... | collective-permute-start | bytes 1179656 | tf_op jit(solution)/shard_map/ppermute | solution.py:49
  53.7 2.4 %collective-permute-start = (f32[256,3,128]{2,0,1:T(8,128)S(1)}, f32[256,3,128]{2,0,1:T(8,128)S(1)}, u32[]{:S(2)}, u32[]{:S(2)}) collective-permute-start(f32[256,3,128]{2,0,1:T(8,128)S(1)} %copy.74), channel_id=1, source_target_pairs={{0,1},{1,2},{2,3},{3,4},{4,5},{5,6},{6,7},{7,8},{8,9},{9,10},{10,1... | collective-permute-start | bytes 1179656 | tf_op jit(solution)/shard_map/ppermute | solution.py:48
  56.1 0.0 collective-permute-done.4
  56.1 0.0 collective-permute-done.5
  56.1 0.1 fusion.22
  56.2 2.7 %collective-permute-start.6 = (f32[1,14,3]{2,0,1:T(1,128)S(1)}, f32[1,14,3]{2,0,1:T(1,128)S(1)}, u32[]{:S(2)}, u32[]{:S(2)}) collective-permute-start(f32[1,14,3]{2,0,1:T(1,128)S(1)} %get-tuple-element.15), channel_id=1, source_target_pairs={{0,32},{32,64},{64,96},{96,128},{128,160},{160,192},{192,224},{224... | collective-permute-start | bytes 512 | tf_op jit(solution)/shard_map/ppermute | solution.py:48
  58.9 3.1 %collective-permute-start.7 = (f32[1,14,3]{2,0,1:T(1,128)S(1)}, f32[1,14,3]{2,0,1:T(1,128)S(1)}, u32[]{:S(2)}, u32[]{:S(2)}) collective-permute-start(f32[1,14,3]{2,0,1:T(1,128)S(1)} %get-tuple-element.16), channel_id=1, source_target_pairs={{32,0},{64,32},{96,64},{128,96},{160,128},{192,160},{224,192},{256... | collective-permute-start | bytes 512 | tf_op jit(solution)/shard_map/ppermute | solution.py:49
  62.1 0.6 copy.67
  62.6 0.4 collective-permute-done.6
  63.0 2.4 %collective-permute-done.7 = f32[1,14,3]{2,0,1:T(1,128)S(1)} collective-permute-done((f32[1,14,3]{2,0,1:T(1,128)S(1)}, f32[1,14,3]{2,0,1:T(1,128)S(1)}, u32[]{:S(2)}, u32[]{:S(2)}) %collective-permute-start.7) | collective-permute-done | bytes 200 | tf_op jit(solution)/shard_map/ppermute | solution.py:49
  65.4 0.1 maximum_maximum_fusion.1
  65.5 0.1 slice_add_fusion.11
  65.6 0.0 collective-permute-done.1
  65.6 1.2 %copy.68 = f32[256,3,128]{0,1,2:T(4,128)S(1)} copy(f32[256,3,128]{2,0,1:T(8,128)} %collective-permute-done.1) | data formatting | bytes 786432 | tf_op jit(solution)/shard_map/ppermute | solution.py:49
  66.9 2.7 %collective-permute-done = f32[256,3,128]{2,0,1:T(8,128)S(1)} collective-permute-done((f32[256,3,128]{2,0,1:T(8,128)S(1)}, f32[256,3,128]{2,0,1:T(8,128)S(1)}, u32[]{:S(2)}, u32[]{:S(2)}) %collective-permute-start) | collective-permute-done | bytes 393248 | tf_op jit(solution)/shard_map/ppermute | solution.py:48
  69.6 0.2 copy.66
  69.8 0.4 pad_maximum_fusion.1
  70.2 4.1 %collective-permute-start.2 = (f32[256,14,3]{0,1,2:T(8,128)S(1)}, f32[256,14,3]{0,1,2:T(8,128)S(1)}, u32[]{:S(2)}, u32[]{:S(2)}) collective-permute-start(f32[256,14,3]{0,1,2:T(8,128)S(1)} %get-tuple-element.7), channel_id=1, source_target_pairs={{0,32},{32,64},{64,96},{96,128},{128,160},{160,192},{192,224},{224... | collective-permute-start | bytes 129032 | tf_op jit(solution)/shard_map/ppermute | solution.py:48
  74.3 1.9 %collective-permute-start.3 = (f32[256,14,3]{0,1,2:T(8,128)S(1)}, f32[256,14,3]{0,1,2:T(8,128)S(1)}, u32[]{:S(2)}, u32[]{:S(2)}) collective-permute-start(f32[256,14,3]{0,1,2:T(8,128)S(1)} %get-tuple-element.8), channel_id=1, source_target_pairs={{32,0},{64,32},{96,64},{128,96},{160,128},{192,160},{224,192},{256... | collective-permute-start | bytes 129032 | tf_op jit(solution)/shard_map/ppermute | solution.py:49
  76.3 0.1 copy.72
  76.4 0.0 collective-permute-done.2
  76.4 4.8 %collective-permute-done.3 = f32[256,14,3]{0,1,2:T(8,128)S(1)} collective-permute-done((f32[256,14,3]{0,1,2:T(8,128)S(1)}, f32[256,14,3]{0,1,2:T(8,128)S(1)}, u32[]{:S(2)}, u32[]{:S(2)}) %collective-permute-start.3) | collective-permute-done | bytes 43040 | tf_op jit(solution)/shard_map/ppermute | solution.py:49
  81.2 0.6 maximum_maximum_fusion
  81.8 0.8 slice_add_fusion
  82.6 0.7 fusion.2
  83.3 1.3 %copy.73 = bf16[256,8,128]{2,1,0:T(8,128)(2,1)} copy(bf16[256,8,128]{0,1,2:T(8,128)(2,1)S(1)} %fusion.2) | data formatting | bytes 1048576 | tf_op jit(solution)/shard_map/convert_element_type | solution.py:102
  (11 shorter events, 0.2 us)
Async XLA Ops:
  0.0 28.8 %copy-start = (f32[64]{0:T(128)S(1)}, f32[64]{0:T(128)}, u32[]{:S(2)}) copy-start(f32[64]{0:T(128)} %param.3) | copy-start | bytes 772
  2.0 22.2 %all-to-all-start = ((f32[16,2,4,4,128]{4,3,2,1,0:T(4,128)}), f32[16,2,4,4,128]{4,3,2,1,0:T(4,128)S(1)}, u32[]{:S(2)}, u32[]{:S(2)}) async-start(f32[16,2,4,4,128]{4,3,2,1,0:T(4,128)} %copy.61), calls=%async_computation | async-start | bytes 524288 | tf_op jit(solution)/shard_map/all_to_all | solution.py:37
  24.3 14.8 %all-to-all-start.1 = ((f32[16,2,4,4,128]{4,3,2,1,0:T(4,128)}), f32[16,2,4,4,128]{4,3,2,1,0:T(4,128)S(1)}, u32[]{:S(2)}, u32[]{:S(2)}) async-start(f32[16,2,4,4,128]{4,3,2,1,0:T(4,128)} %copy.62), calls=%async_computation.1 | async-start | bytes 524288 | tf_op jit(solution)/shard_map/all_to_all | solution.py:37
  39.4 16.7 %collective-permute-start.4 = (f32[1,3,128]{2,1,0:T(4,128)S(1)}, f32[1,3,128]{2,1,0:T(4,128)S(1)}, u32[]{:S(2)}, u32[]{:S(2)}) collective-permute-start(f32[1,3,128]{2,1,0:T(4,128)S(1)} %get-tuple-element.17), channel_id=1, source_target_pairs={{0,1},{1,2},{2,3},{3,4},{4,5},{5,6},{6,7},{7,8},{8,9},{9,10},{10,1... | collective-permute-start | bytes 4616 | tf_op jit(solution)/shard_map/ppermute | solution.py:48
  41.3 14.8 %collective-permute-start.5 = (f32[1,3,128]{2,1,0:T(4,128)S(1)}, f32[1,3,128]{2,1,0:T(4,128)S(1)}, u32[]{:S(2)}, u32[]{:S(2)}) collective-permute-start(f32[1,3,128]{2,1,0:T(4,128)S(1)} %get-tuple-element.18), channel_id=1, source_target_pairs={{1,0},{2,1},{3,2},{4,3},{5,4},{6,5},{7,6},{8,7},{9,8},{10,9},{11,1... | collective-permute-start | bytes 4616 | tf_op jit(solution)/shard_map/ppermute | solution.py:49
  51.7 13.9 %collective-permute-start.1 = (f32[256,3,128]{2,0,1:T(8,128)S(1)}, f32[256,3,128]{2,0,1:T(8,128)}, u32[]{:S(2)}, u32[]{:S(2)}) collective-permute-start(f32[256,3,128]{2,0,1:T(8,128)S(1)} %copy.75), channel_id=1, source_target_pairs={{1,0},{2,1},{3,2},{4,3},{5,4},{6,5},{7,6},{8,7},{9,8},{10,9},{11,1... | collective-permute-start | bytes 1179656 | tf_op jit(solution)/shard_map/ppermute | solution.py:49
  53.7 15.9 %collective-permute-start = (f32[256,3,128]{2,0,1:T(8,128)S(1)}, f32[256,3,128]{2,0,1:T(8,128)S(1)}, u32[]{:S(2)}, u32[]{:S(2)}) collective-permute-start(f32[256,3,128]{2,0,1:T(8,128)S(1)} %copy.74), channel_id=1, source_target_pairs={{0,1},{1,2},{2,3},{3,4},{4,5},{5,6},{6,7},{7,8},{8,9},{9,10},{10,1... | collective-permute-start | bytes 1179656 | tf_op jit(solution)/shard_map/ppermute | solution.py:48
  56.2 6.8 %collective-permute-start.6 = (f32[1,14,3]{2,0,1:T(1,128)S(1)}, f32[1,14,3]{2,0,1:T(1,128)S(1)}, u32[]{:S(2)}, u32[]{:S(2)}) collective-permute-start(f32[1,14,3]{2,0,1:T(1,128)S(1)} %get-tuple-element.15), channel_id=1, source_target_pairs={{0,32},{32,64},{64,96},{96,128},{128,160},{160,192},{192,224},{224... | collective-permute-start | bytes 512 | tf_op jit(solution)/shard_map/ppermute | solution.py:48
  58.9 6.4 %collective-permute-start.7 = (f32[1,14,3]{2,0,1:T(1,128)S(1)}, f32[1,14,3]{2,0,1:T(1,128)S(1)}, u32[]{:S(2)}, u32[]{:S(2)}) collective-permute-start(f32[1,14,3]{2,0,1:T(1,128)S(1)} %get-tuple-element.16), channel_id=1, source_target_pairs={{32,0},{64,32},{96,64},{128,96},{160,128},{192,160},{224,192},{256... | collective-permute-start | bytes 512 | tf_op jit(solution)/shard_map/ppermute | solution.py:49
  70.2 6.2 %collective-permute-start.2 = (f32[256,14,3]{0,1,2:T(8,128)S(1)}, f32[256,14,3]{0,1,2:T(8,128)S(1)}, u32[]{:S(2)}, u32[]{:S(2)}) collective-permute-start(f32[256,14,3]{0,1,2:T(8,128)S(1)} %get-tuple-element.7), channel_id=1, source_target_pairs={{0,32},{32,64},{64,96},{96,128},{128,160},{160,192},{192,224},{224... | collective-permute-start | bytes 129032 | tf_op jit(solution)/shard_map/ppermute | solution.py:48
  74.3 6.9 %collective-permute-start.3 = (f32[256,14,3]{0,1,2:T(8,128)S(1)}, f32[256,14,3]{0,1,2:T(8,128)S(1)}, u32[]{:S(2)}, u32[]{:S(2)}) collective-permute-start(f32[256,14,3]{0,1,2:T(8,128)S(1)} %get-tuple-element.8), channel_id=1, source_target_pairs={{32,0},{64,32},{96,64},{128,96},{160,128},{192,160},{224,192},{256... | collective-permute-start | bytes 129032 | tf_op jit(solution)/shard_map/ppermute | solution.py:49
where the time goes:
time: 85.2 us; the launch traced here: 84.7 us
  starting transfers between devices  42.2 us (50%)
  waiting for transfers between devices  29.7 us (35%)
  local copies, waits for them, and re-layouts  6.81 us (8%)
  other arithmetic  3.76 us (4%)
  matrix products  1.86 us (2%)
    all_to_all x2, waiting for transfers between devices, cut_exchange(): lax.all_to_all(slab, axis, split_axis=0, concat_axis=0, tiled=True)  19.4 us
    all_to_all x2, starting transfers between devices, cut_exchange(): lax.all_to_all(slab, axis, split_axis=0, concat_axis=0, tiled=True)  16.3 us
    ppermute x4, starting transfers between devices, with_halo(): after = lax.ppermute(first, axis, down)  14.8 us
    ppermute x4, starting transfers between devices, with_halo(): before = lax.ppermute(last, axis, up)  11.1 us
    ppermute x4, waiting for transfers between devices, with_halo(): after = lax.ppermute(first, axis, down)  7.19 us
    ppermute x4, waiting for transfers between devices, with_halo(): before = lax.ppermute(last, axis, up)  3.13 us
    dot_general x1, matrix products, beamform(): jnp.dot(matrix, flat, precision=lax.Precision.HIGHEST, preferred_element_...  1.86 us
  transfers between devices with their start and end apart: 10, of which 6 were waited for; matrix products, arithmetic and copies ran while one was open for 7% of the time, Pallas kernels for 0%

commit v1 on v0

v1 whole, which is shorter than its diff:
```python
import jax
import jax.numpy as jnp
import numpy as np
from jax import lax
from jax.experimental import pallas as pl
from jax.experimental.pallas import tpu as pltpu
from jax.sharding import PartitionSpec as P


HEIGHTS = 256
ROWS = HEIGHTS + 8
LANES = 128
epsilon = 1e-06

SLOT = {0: 0, 1: 1, 2: 2, 7: 4, 6: 5, 5: 6, 3: 7, 4: 8}
HALO = 3

PACK_VMEM = 4 << 20
OWN_VMEM = 10 << 20
BOX_VMEM = 16 << 20


def parity():
    return lax.rem(lax.axis_index("line"), 2)


def pack_kernel(x_ref, out_ref):
    blocks = x_ref.shape[0] // 64
    odd = parity()
    lane = lax.broadcasted_iota(jnp.int32, (8, LANES), 1)
    halo = [jnp.zeros((8, LANES), jnp.float32) for _ in range(blocks)]
    for m in range(8):
        line = m + odd * (7 - 2 * m)
        left = (lane >= 6 * m) & (lane < 6 * m + 3)
        right = (lane >= 6 * m + 3) & (lane < 6 * m + 6)
        for j in range(blocks):
            tile = x_ref[pl.ds(8 * j + line, 8, stride=8 * blocks), :]
            out_ref[j, SLOT[m]] = tile
            moved = pltpu.roll(tile, 3 + 6 * m, 1)
            if j + 1 < blocks:
                halo[j + 1] = jnp.where(left, moved, halo[j + 1])
            if j >= 1:
                halo[j - 1] = jnp.where(right, moved, halo[j - 1])
    for j in range(blocks):
        out_ref[j, HALO] = halo[j]


def beam_pair(first, second, steer_ref, beams_ref):
    both = jnp.concatenate([first.reshape(LANES, LANES), second.reshape(LANES, LANES)], axis=1)
    high = both.astype(jnp.bfloat16)
    low = (both - high.astype(jnp.float32)).astype(jnp.bfloat16)
    stacked = jnp.concatenate([high, low, high], axis=0)
    beams_ref[...] = jnp.dot(steer_ref[...], stacked, preferred_element_type=jnp.float32)
    re, im = beams_ref[:HEIGHTS], beams_ref[HEIGHTS:]
    power = re * re + im * im
    squares = (both * both).reshape(16, 8, 2 * LANES).sum(axis=0)
    return jnp.concatenate([power, squares], axis=0)


def own_kernel(r_ref, steer_ref, out_ref, beams_ref):
    for s in (0, 2, 4, 6, 8):
        t = min(s + 1, 8)
        both = beam_pair(r_ref[:, s], r_ref[:, t], steer_ref, beams_ref)
        out_ref[s] = both[:, :LANES]
        if t != s:
            out_ref[t] = both[:, LANES:]


def halves(field):
    high = field.astype(jnp.bfloat16)
    low = (field - high.astype(jnp.float32)).astype(jnp.bfloat16)
    return jnp.concatenate([high, low], axis=1)


def box_kernel(own_ref, o_ref, e_ref, steer_ref, mid_ref, mo_ref, me_ref, out_ref, beams_ref, side_ref, cor_ref, flat_ref):
    odd = parity()
    for k, ref in ((0, o_ref), (4, e_ref)):
        for s in (0, 2):
            both = beam_pair(ref[:, s], ref[:, s + 1], steer_ref, beams_ref)
            side_ref[k + s] = both[:, :LANES]
            side_ref[k + s + 1] = both[:, LANES:]
    cor_ref[...] = jnp.dot(halves(own_ref[HALO]), mid_ref[...], preferred_element_type=jnp.float32)
    cor_ref[:, : 3 * LANES] += jnp.dot(halves(side_ref[3]), mo_ref[...], preferred_element_type=jnp.float32)
    cor_ref[:, 5 * LANES :] += jnp.dot(halves(side_ref[4]), me_ref[...], preferred_element_type=jnp.float32)

    def rows_of(position, rows):
        if position < 0:
            return side_ref[-1 - position, rows]
        if position > 7:
            return side_ref[position - 3, rows]
        return own_ref[SLOT[position], rows]

    def boxed(m, rows, count):
        lane = lax.broadcasted_iota(jnp.int32, (count, LANES), 1)
        total = rows_of(m - 3, rows)
        for d in range(-2, 4):
            total = total + rows_of(m + d, rows)
        box = total + cor_ref[rows, m * LANES : (m + 1) * LANES]
        for d in (1, 2, 3):
            box = box + jnp.where(lane >= d, pltpu.roll(total, d, 1), 0.0)
            box = box + jnp.where(lane < LANES - d, pltpu.roll(total, LANES - d, 1), 0.0)
        return box

    for m in range(8):
        line = m + odd * (7 - 2 * m)
        energy = boxed(m, slice(HEIGHTS, ROWS), 8).sum(axis=0, keepdims=True)
        inverse = 1.0 / (energy + epsilon)
        for k in range(0, HEIGHTS, 64):
            box = boxed(m, slice(k, k + 64), 64) * inverse
            flat_ref[pl.ds(8 * k + line, 64, stride=8), :] = box
    for k in range(0, HEIGHTS, 16):
        out_ref[k : k + 16] = flat_ref[8 * k : 8 * k + 128].reshape(16, 8, LANES).astype(jnp.bfloat16)


def spread():
    column = np.array([-3, -2, -1, 128, 129, 130])
    near = np.abs(column[:, None] - np.arange(LANES)[None, :]) <= 3

    def matrix(position_of, lines, used):
        full = np.zeros((LANES, len(lines), LANES), np.float32)
        for n in used:
            for i, m in enumerate(lines):
                if abs(position_of(n) - m) <= 3:
                    full[6 * n : 6 * n + 6, i] = near
        full = full.reshape(LANES, -1)
        return jnp.asarray(np.concatenate([full, full], axis=0), jnp.bfloat16)

    mid = matrix(lambda n: n, range(8), range(8))
    mo = matrix(lambda n: -1 - n, (0, 1, 2), (0, 1, 2))
    me = matrix(lambda n: 15 - n, (5, 6, 7), (5, 6, 7))
    return mid, mo, me


def steering(wavenumbers):
    waves = jnp.broadcast_to(wavenumbers.reshape(16, 1, 4), (16, 2, 4)).reshape(LANES)
    real = (jnp.arange(LANES) // 4) % 2 == 0
    heights = jnp.arange(HEIGHTS, dtype=jnp.int32).astype(jnp.float32) - jnp.float32(HEIGHTS // 2)
    phases = heights[:, None] * waves[None, :]
    cosine, sine = jnp.cos(phases), jnp.sin(phases)
    full = jnp.concatenate([jnp.where(real, cosine, sine), jnp.where(real, -sine, cosine)], axis=0)
    high = lax.reduce_precision(full, 8, 7)
    low = (full - high).astype(jnp.bfloat16)
    high = high.astype(jnp.bfloat16)
    return jnp.concatenate([high, high, low], axis=1)


VMEM = pl.BlockSpec(memory_space=pltpu.VMEM)


def spectrum(slc_stack, wavenumbers):
    lines = lax.axis_size("line")
    outer = [pair for i in range(1, lines - 1, 2) for pair in ((i, i + 1), (i + 1, i))]
    inner = [pair for i in range(0, lines, 2) for pair in ((i, i + 1), (i + 1, i))]
    packed = pl.pallas_call(
        pack_kernel,
        out_shape=jax.ShapeDtypeStruct((16, 9, 8, LANES), jnp.float32),
        in_specs=[VMEM],
        out_specs=VMEM,
        name="pack",
        compiler_params=pltpu.CompilerParams(vmem_limit_bytes=PACK_VMEM),
        cost_estimate=pl.CostEstimate(flops=1000000, bytes_accessed=1100000, transcendentals=0),
    )(slc_stack.reshape(8, 8, -1, LANES).transpose(0, 2, 1, 3).reshape(-1, LANES))
    gathered = lax.all_to_all(packed, "acq", 0, 0, tiled=True)
    steer = steering(wavenumbers)
    mid, mo, me = spread()
    side_o = lax.ppermute(gathered[:, 0:4], "line", outer)
    side_e = lax.ppermute(gathered[:, 3:7], "line", inner)
    own = pl.pallas_call(
        own_kernel,
        out_shape=jax.ShapeDtypeStruct((9, ROWS, LANES), jnp.float32),
        in_specs=[VMEM] * 2,
        out_specs=VMEM,
        scratch_shapes=[pltpu.VMEM((2 * HEIGHTS, 2 * LANES), jnp.float32)],
        name="own",
        compiler_params=pltpu.CompilerParams(vmem_limit_bytes=OWN_VMEM),
        cost_estimate=pl.CostEstimate(flops=1000000000, bytes_accessed=2000000, transcendentals=0),
    )(gathered, steer)
    return pl.pallas_call(
        box_kernel,
        out_shape=jax.ShapeDtypeStruct((HEIGHTS, 8, LANES), jnp.bfloat16),
        in_specs=[VMEM] * 7,
        out_specs=VMEM,
        scratch_shapes=[
            pltpu.VMEM((2 * HEIGHTS, 2 * LANES), jnp.float32),
            pltpu.VMEM((8, ROWS, LANES), jnp.float32),
            pltpu.VMEM((ROWS, 8 * LANES), jnp.float32),
            pltpu.VMEM((8 * HEIGHTS, LANES), jnp.float32),
        ],
        name="box",
        compiler_params=pltpu.CompilerParams(vmem_limit_bytes=BOX_VMEM),
        cost_estimate=pl.CostEstimate(flops=1000000000, bytes_accessed=2000000, transcendentals=0),
    )(own, side_o, side_e, steer, mid, mo, me)


def solution(mesh):
    placed = (P(None, "acq", "line", None), P())
    return jax.shard_map(spectrum, mesh=mesh, in_specs=placed, out_specs=P(None, "line", "acq"), check_vma=False)
```

time: 85.2 us -> 53 us (0.62)
  the two profiles are of different devices: /device:TPU:40 before, /device:TPU:23 now
where the time goes in v1:
time: 53 us; the launch traced here: 52.7 us
  waiting for transfers between devices  24.8 us (47%)
  starting transfers between devices  20.5 us (39%)
  Pallas kernels  5.35 us (10%)
  local copies, waits for them, and re-layouts  1.33 us (3%)
  other arithmetic  0.65 us (1%)
    all_to_all x1, waiting for transfers between devices, spectrum(): gathered = lax.all_to_all(packed, 'acq', 0, 0, tiled=True)  15.4 us
    all_to_all x1, starting transfers between devices, spectrum(): gathered = lax.all_to_all(packed, 'acq', 0, 0, tiled=True)  11.2 us
    ppermute x1, waiting for transfers between devices, spectrum(): side_o = lax.ppermute(gathered[:, 0:4], 'line', outer)  9.36 us
    ppermute x1, starting transfers between devices, spectrum(): side_e = lax.ppermute(gathered[:, 3:7], 'line', inner)  4.97 us
    ppermute x1, starting transfers between devices, spectrum(): side_o = lax.ppermute(gathered[:, 0:4], 'line', outer)  4.34 us
    pallas_call x1, Pallas kernels, spectrum(): pl.pallas_call(box_kernel, out_shape=jax.ShapeDtypeStruct((HEIGHTS, 8, LA...  3.3 us
    pallas_call x1, Pallas kernels, spectrum(): pl.pallas_call(pack_kernel, out_shape=jax.ShapeDtypeStruct((16, 9, 8, LAN...  1.21 us
    unnamed x10, local copies, waits for them, and re-layouts  1.08 us
  transfers between devices with their start and end apart: 3, of which 2 were waited for; matrix products, arithmetic and copies ran while one was open for 2% of the time, Pallas kernels for 2%

profile of v1, /device:TPU:23, one launch (start us, length us, event | category | flops | bytes accessed | tf_op | source)
XLA Modules:
  0.0 52.7 jit_solution(5990130766292071055)
XLA Ops:
  0.0 0.0 copy-start.4
  0.0 0.0 copy-start
  0.0 1.1 %copy-done = f32[2,4,8,2048]{3,2,1,0:T(8,128)S(1)} copy-done((f32[2,4,8,2048]{3,2,1,0:T(8,128)S(1)}, f32[2,4,8,2048]{3,2,1,0:T(8,128)}, u32[]{:S(2)}) %copy-start) | copy-done | bytes 524312
  1.1 1.2 %pack.1 = f32[16,9,8,128]{3,2,1,0:T(8,128)} custom-call(f32[1024,128]{1,0:T(8,128)S(1)} %bitcast.5), custom_call_target="tpu_custom_call" | custom-call | flops 1000000 | bytes 1100000 | tf_op jit(solution)/shard_map/pack/pallas_call | solution.py:154
  2.3 11.2 %all-to-all-start = ((f32[16,9,8,128]{3,2,1,0:T(8,128)}), f32[16,9,8,128]{3,2,1,0:T(8,128)S(1)}, u32[]{:S(2)}, u32[]{:S(2)}) async-start(f32[16,9,8,128]{3,2,1,0:T(8,128)} %pack.1), calls=%async_computation | async-start | bytes 1179648 | tf_op jit(solution)/shard_map/all_to_all | solution.py:163
  13.4 0.0 copy-done.4
  13.4 0.1 broadcast_in_dim.16
  13.5 0.1 mul.16
  13.7 0.5 %fusion.2 = (f32[256,128]{1,0:T(8,128)S(1)}, f32[256,128]{1,0:T(8,128)S(1)}) fusion(f32[128]{0:T(128)S(1)} %mul.16, f32[256]{0:T(256)S(1)} %convert_add_fusion, pred[128]{0:T(512)(128)(4,1)S(1)} %fusion.4), kind=kLoop, calls=%fused_computation.8 | loop fusion | flops 131072 | bytes 263808 | tf_op jit(solution)/shard_map/jit(_where)/select_n | solution.py:140
  14.2 15.4 %all-to-all-done.r_ref = f32[16,9,8,128]{3,2,1,0:T(8,128)S(1)} async-done(((f32[16,9,8,128]{3,2,1,0:T(8,128)}), f32[16,9,8,128]{3,2,1,0:T(8,128)S(1)}, u32[]{:S(2)}, u32[]{:S(2)}) %all-to-all-start) | async-done | bytes 589856 | tf_op jit(solution)/shard_map/all_to_all | solution.py:163
  29.7 5.0 %collective-permute-start.1 = (f32[16,4,8,128]{3,2,1,0:T(8,128)S(1)}, f32[16,4,8,128]{3,2,1,0:T(8,128)S(1)}, u32[]{:S(2)}, u32[]{:S(2)}) collective-permute-start(f32[16,4,8,128]{3,2,1,0:T(8,128)S(1)} %get-tuple-element.5), channel_id=1, source_target_pairs={{0,1},{1,0},{2,3},{3,2},{4,5},{5,4},{6,7},{7,6},{8,9},{9,8},{10,11... | collective-permute-start | bytes 786440 | tf_op jit(solution)/shard_map/ppermute | solution.py:167
  34.7 4.3 %collective-permute-start = (f32[16,4,8,128]{3,2,1,0:T(8,128)S(1)}, f32[16,4,8,128]{3,2,1,0:T(8,128)S(1)}, u32[]{:S(2)}, u32[]{:S(2)}) collective-permute-start(f32[16,4,8,128]{3,2,1,0:T(8,128)S(1)} %get-tuple-element.6), channel_id=1, source_target_pairs={{1,2},{2,1},{3,4},{4,3},{5,6},{6,5},{7,8},{8,7},{9,10},{10,9},{11,... | collective-permute-start | bytes 786440 | tf_op jit(solution)/shard_map/ppermute | solution.py:166
  39.1 0.0 copy-start.1
  39.1 0.0 copy-start.2
  39.2 0.0 copy-start.3
  39.2 0.8 %own.1.own_ref = f32[9,264,128]{2,1,0:T(8,128)S(1)} custom-call(f32[16,9,8,128]{3,2,1,0:T(8,128)S(1)} %all-to-all-done.r_ref, bf16[512,384]{1,0:T(8,128)(2,1)S(1)} %pad_maximum_fusion.steer_ref), custom_call_target="tpu_custom_call" | custom-call | flops 1000000000 | bytes 2000000 | tf_op jit(solution)/shard_map/own/pallas_call | solution.py:168
  40.0 0.0 collective-permute-done.1.e_ref
  40.0 9.4 %collective-permute-done.o_ref = f32[16,4,8,128]{3,2,1,0:T(8,128)S(1)} collective-permute-done((f32[16,4,8,128]{3,2,1,0:T(8,128)S(1)}, f32[16,4,8,128]{3,2,1,0:T(8,128)S(1)}, u32[]{:S(2)}, u32[]{:S(2)}) %collective-permute-start) | collective-permute-done | bytes 262176 | tf_op jit(solution)/shard_map/ppermute | solution.py:166
  49.4 0.0 copy-done.1
  49.4 0.0 copy-done.2
  49.4 0.0 copy-done.3
  49.4 3.3 %box.1 = bf16[256,8,128]{2,1,0:T(8,128)(2,1)} custom-call(f32[9,264,128]{2,1,0:T(8,128)S(1)} %own.1.own_ref, f32[16,4,8,128]{3,2,1,0:T(8,128)S(1)} %collective-permute-done.o_ref, f32[16,4,8,128]{3,2,1,0:T(8,128)S(1)} %collective-permute-done.1.e_ref, bf16[512,384]{1,0:T(8,128)(2,1)S(1)} %pad_maximum_fusion.steer_ref, bf16[256,1024]{1,0:T(8,128)(2,1)S(1)} %copy-done.1, ...), custom_call_target="tpu_custom_call" | custom-call | flops 1000000000 | bytes 2000000 | tf_op jit(solution)/shard_map/box/pallas_call | solution.py:178
  (6 shorter events, 0.2 us)
Async XLA Ops:
  0.0 13.4 %copy-start.4 = (f32[64]{0:T(128)S(1)}, f32[64]{0:T(128)}, u32[]{:S(2)}) copy-start(f32[64]{0:T(128)} %param.6) | copy-start | bytes 772
  0.0 1.1 %copy-start = (f32[2,4,8,2048]{3,2,1,0:T(8,128)S(1)}, f32[2,4,8,2048]{3,2,1,0:T(8,128)}, u32[]{:S(2)}) copy-start(f32[2,4,8,2048]{3,2,1,0:T(8,128)} %param.5) | copy-start | bytes 1572868
  2.3 27.4 %all-to-all-start = ((f32[16,9,8,128]{3,2,1,0:T(8,128)}), f32[16,9,8,128]{3,2,1,0:T(8,128)S(1)}, u32[]{:S(2)}, u32[]{:S(2)}) async-start(f32[16,9,8,128]{3,2,1,0:T(8,128)} %pack.1), calls=%async_computation | async-start | bytes 1179648 | tf_op jit(solution)/shard_map/all_to_all | solution.py:163
  29.7 10.3 %collective-permute-start.1 = (f32[16,4,8,128]{3,2,1,0:T(8,128)S(1)}, f32[16,4,8,128]{3,2,1,0:T(8,128)S(1)}, u32[]{:S(2)}, u32[]{:S(2)}) collective-permute-start(f32[16,4,8,128]{3,2,1,0:T(8,128)S(1)} %get-tuple-element.5), channel_id=1, source_target_pairs={{0,1},{1,0},{2,3},{3,2},{4,5},{5,4},{6,7},{7,6},{8,9},{9,8},{10,11... | collective-permute-start | bytes 786440 | tf_op jit(solution)/shard_map/ppermute | solution.py:167
  34.7 14.7 %collective-permute-start = (f32[16,4,8,128]{3,2,1,0:T(8,128)S(1)}, f32[16,4,8,128]{3,2,1,0:T(8,128)S(1)}, u32[]{:S(2)}, u32[]{:S(2)}) collective-permute-start(f32[16,4,8,128]{3,2,1,0:T(8,128)S(1)} %get-tuple-element.6), channel_id=1, source_target_pairs={{1,2},{2,1},{3,4},{4,3},{5,6},{6,5},{7,8},{8,7},{9,10},{10,9},{11,... | collective-permute-start | bytes 786440 | tf_op jit(solution)/shard_map/ppermute | solution.py:166
  39.1 10.3 %copy-start.1 = (bf16[256,1024]{1,0:T(8,128)(2,1)S(1)}, bf16[256,1024]{1,0:T(8,128)(2,1)}, u32[]{:S(2)}) copy-start(bf16[256,1024]{1,0:T(8,128)(2,1)} %constant.40.clone.mid_ref) | copy-start | bytes 1572868
  39.1 10.3 %copy-start.2 = (bf16[256,384]{1,0:T(8,128)(2,1)S(1)}, bf16[256,384]{1,0:T(8,128)(2,1)}, u32[]{:S(2)}) copy-start(bf16[256,384]{1,0:T(8,128)(2,1)} %constant.42.clone.me_ref) | copy-start | bytes 589828
  39.2 10.2 %copy-start.3 = (bf16[256,384]{1,0:T(8,128)(2,1)S(1)}, bf16[256,384]{1,0:T(8,128)(2,1)}, u32[]{:S(2)}) copy-start(bf16[256,384]{1,0:T(8,128)(2,1)} %constant.41.clone.mo_ref) | copy-start | bytes 589828

commit v2 on v1

--- a/solution.py
+++ b/solution.py
@@ -14,6 +14,7 @@
 
 SLOT = {0: 0, 1: 1, 2: 2, 7: 4, 6: 5, 5: 6, 3: 7, 4: 8}
 HALO = 3
+FIRST = 4
 
 PACK_VMEM = 4 << 20
 OWN_VMEM = 10 << 20
@@ -24,18 +25,23 @@
     return lax.rem(lax.axis_index("line"), 2)
 
 
-def pack_kernel(x_ref, out_ref):
+def tile_of(x_ref, m, odd, j):
+    blocks = x_ref.shape[0] // 64
+    return x_ref[pl.ds(8 * j + m + odd * (7 - 2 * m), 8, stride=8 * blocks), :]
+
+
+def pack_edge(x_ref, out_ref):
     blocks = x_ref.shape[0] // 64
     odd = parity()
     lane = lax.broadcasted_iota(jnp.int32, (8, LANES), 1)
     halo = [jnp.zeros((8, LANES), jnp.float32) for _ in range(blocks)]
     for m in range(8):
-        line = m + odd * (7 - 2 * m)
         left = (lane >= 6 * m) & (lane < 6 * m + 3)
         right = (lane >= 6 * m + 3) & (lane < 6 * m + 6)
         for j in range(blocks):
-            tile = x_ref[pl.ds(8 * j + line, 8, stride=8 * blocks), :]
-            out_ref[j, SLOT[m]] = tile
+            tile = tile_of(x_ref, m, odd, j)
+            if SLOT[m] < FIRST:
+                out_ref[j, SLOT[m]] = tile
             moved = pltpu.roll(tile, 3 + 6 * m, 1)
             if j + 1 < blocks:
                 halo[j + 1] = jnp.where(left, moved, halo[j + 1])
@@ -43,6 +49,13 @@
                 halo[j - 1] = jnp.where(right, moved, halo[j - 1])
     for j in range(blocks):
         out_ref[j, HALO] = halo[j]
+
+
+def pack_rest(x_ref, steer_ref, out_ref):
+    odd = parity()
+    for m in range(3, 8):
+        for j in range(x_ref.shape[0] // 64):
+            out_ref[j, SLOT[m] - FIRST] = tile_of(x_ref, m, odd, j)
 
 
 def beam_pair(first, second, steer_ref, beams_ref):
@@ -58,8 +71,9 @@
 
 
 def own_kernel(r_ref, steer_ref, out_ref, beams_ref):
-    for s in (0, 2, 4, 6, 8):
-        t = min(s + 1, 8)
+    count = r_ref.shape[1]
+    for s in range(0, count, 2):
+        t = min(s + 1, count - 1)
         both = beam_pair(r_ref[:, s], r_ref[:, t], steer_ref, beams_ref)
         out_ref[s] = both[:, :LANES]
         if t != s:
@@ -72,14 +86,14 @@
     return jnp.concatenate([high, low], axis=1)
 
 
-def box_kernel(own_ref, o_ref, e_ref, steer_ref, mid_ref, mo_ref, me_ref, out_ref, beams_ref, side_ref, cor_ref, flat_ref):
+def box_kernel(edge_ref, rest_ref, o_ref, e_ref, steer_ref, mid_ref, mo_ref, me_ref, out_ref, beams_ref, side_ref, cor_ref, flat_ref):
     odd = parity()
     for k, ref in ((0, o_ref), (4, e_ref)):
         for s in (0, 2):
             both = beam_pair(ref[:, s], ref[:, s + 1], steer_ref, beams_ref)
             side_ref[k + s] = both[:, :LANES]
             side_ref[k + s + 1] = both[:, LANES:]
-    cor_ref[...] = jnp.dot(halves(own_ref[HALO]), mid_ref[...], preferred_element_type=jnp.float32)
+    cor_ref[...] = jnp.dot(halves(edge_ref[HALO]), mid_ref[...], preferred_element_type=jnp.float32)
     cor_ref[:, : 3 * LANES] += jnp.dot(halves(side_ref[3]), mo_ref[...], preferred_element_type=jnp.float32)
     cor_ref[:, 5 * LANES :] += jnp.dot(halves(side_ref[4]), me_ref[...], preferred_element_type=jnp.float32)
 
@@ -88,7 +102,8 @@
             return side_ref[-1 - position, rows]
         if position > 7:
             return side_ref[position - 3, rows]
-        return own_ref[SLOT[position], rows]
+        slot = SLOT[position]
+        return edge_ref[slot, rows] if slot < FIRST else rest_ref[slot - FIRST, rows]
 
     def boxed(m, rows, count):
         lane = lax.broadcasted_iota(jnp.int32, (count, LANES), 1)
@@ -147,38 +162,41 @@
 VMEM = pl.BlockSpec(memory_space=pltpu.VMEM)
 
 
+def run(kernel, shape, vmem, flops, scratch=()):
+    def call(*operands):
+        return pl.pallas_call(
+            kernel,
+            out_shape=jax.ShapeDtypeStruct(shape, jnp.float32),
+            in_specs=[VMEM] * len(operands),
+            out_specs=VMEM,
+            scratch_shapes=list(scratch),
+            compiler_params=pltpu.CompilerParams(vmem_limit_bytes=vmem),
+            cost_estimate=pl.CostEstimate(flops=flops, bytes_accessed=1000000, transcendentals=0),
+        )(*operands)
+
+    return call
+
+
 def spectrum(slc_stack, wavenumbers):
     lines = lax.axis_size("line")
     outer = [pair for i in range(1, lines - 1, 2) for pair in ((i, i + 1), (i + 1, i))]
     inner = [pair for i in range(0, lines, 2) for pair in ((i, i + 1), (i + 1, i))]
-    packed = pl.pallas_call(
-        pack_kernel,
-        out_shape=jax.ShapeDtypeStruct((16, 9, 8, LANES), jnp.float32),
-        in_specs=[VMEM],
-        out_specs=VMEM,
-        name="pack",
-        compiler_params=pltpu.CompilerParams(vmem_limit_bytes=PACK_VMEM),
-        cost_estimate=pl.CostEstimate(flops=1000000, bytes_accessed=1100000, transcendentals=0),
-    )(slc_stack.reshape(8, 8, -1, LANES).transpose(0, 2, 1, 3).reshape(-1, LANES))
-    gathered = lax.all_to_all(packed, "acq", 0, 0, tiled=True)
     steer = steering(wavenumbers)
+    stack = slc_stack.reshape(8, 8, -1, LANES).transpose(0, 2, 1, 3).reshape(-1, LANES)
+    edge = run(pack_edge, (16, FIRST, 8, LANES), PACK_VMEM, 1000000)(stack)
+    rest = run(pack_rest, (16, 9 - FIRST, 8, LANES), PACK_VMEM, 1000000)(stack, steer)
+    edge = lax.all_to_all(edge, "acq", 0, 0, tiled=True)
+    rest = lax.all_to_all(rest, "acq", 0, 0, tiled=True)
     mid, mo, me = spread()
-    side_o = lax.ppermute(gathered[:, 0:4], "line", outer)
-    side_e = lax.ppermute(gathered[:, 3:7], "line", inner)
-    own = pl.pallas_call(
-        own_kernel,
-        out_shape=jax.ShapeDtypeStruct((9, ROWS, LANES), jnp.float32),
-        in_specs=[VMEM] * 2,
-        out_specs=VMEM,
-        scratch_shapes=[pltpu.VMEM((2 * HEIGHTS, 2 * LANES), jnp.float32)],
-        name="own",
-        compiler_params=pltpu.CompilerParams(vmem_limit_bytes=OWN_VMEM),
-        cost_estimate=pl.CostEstimate(flops=1000000000, bytes_accessed=2000000, transcendentals=0),
-    )(gathered, steer)
+    side_o = lax.ppermute(edge, "line", outer)
+    side_e = lax.ppermute(jnp.concatenate([edge[:, HALO:], rest[:, :3]], axis=1), "line", inner)
+    beams = [pltpu.VMEM((2 * HEIGHTS, 2 * LANES), jnp.float32)]
+    edge = run(own_kernel, (FIRST, ROWS, LANES), OWN_VMEM, 1000000000, beams)(edge, steer)
+    rest = run(own_kernel, (9 - FIRST, ROWS, LANES), OWN_VMEM, 1000000000, beams)(rest, steer)
     return pl.pallas_call(
         box_kernel,
         out_shape=jax.ShapeDtypeStruct((HEIGHTS, 8, LANES), jnp.bfloat16),
-        in_specs=[VMEM] * 7,
+        in_specs=[VMEM] * 8,
         out_specs=VMEM,
         scratch_shapes=[
             pltpu.VMEM((2 * HEIGHTS, 2 * LANES), jnp.float32),
@@ -189,7 +207,7 @@
         name="box",
         compiler_params=pltpu.CompilerParams(vmem_limit_bytes=BOX_VMEM),
         cost_estimate=pl.CostEstimate(flops=1000000000, bytes_accessed=2000000, transcendentals=0),
-    )(own, side_o, side_e, steer, mid, mo, me)
+    )(edge, rest, side_o, side_e, steer, mid, mo, me)
 
 
 def solution(mesh):

time: 53 us -> 50 us (0.943)
  the two profiles are of different devices: /device:TPU:23 before, /device:TPU:1 now
where the time goes in v2:
time: 50 us; the launch traced here: 49.5 us
  starting transfers between devices  26.5 us (53%)
  waiting for transfers between devices  12.6 us (25%)
  Pallas kernels  6.32 us (13%)
  local copies, waits for them, and re-layouts  3.32 us (7%)
  other arithmetic  0.67 us (1%)
    all_to_all x1, starting transfers between devices, spectrum(): edge = lax.all_to_all(edge, 'acq', 0, 0, tiled=True)  12 us
    all_to_all x1, waiting for transfers between devices, spectrum(): rest = lax.all_to_all(rest, 'acq', 0, 0, tiled=True)  7.03 us
    all_to_all x1, starting transfers between devices, spectrum(): rest = lax.all_to_all(rest, 'acq', 0, 0, tiled=True)  5.89 us
    all_to_all x1, waiting for transfers between devices, spectrum(): edge = lax.all_to_all(edge, 'acq', 0, 0, tiled=True)  5.49 us
    ppermute x1, starting transfers between devices, spectrum(): lax.ppermute(jnp.concatenate([edge[:, HALO:], rest[:, :3]], axis=1), 'lin...  4.38 us
    ppermute x1, starting transfers between devices, spectrum(): side_o = lax.ppermute(edge, 'line', outer)  4.23 us
    pallas_call x1, Pallas kernels, spectrum(): pl.pallas_call(box_kernel, out_shape=jax.ShapeDtypeStruct((HEIGHTS, 8, LA...  3.28 us
    unnamed x12, local copies, waits for them, and re-layouts  3.09 us
  transfers between devices with their start and end apart: 4, of which 2 were waited for; matrix products, arithmetic and copies ran while one was open for 2% of the time, Pallas kernels for 4%

profile of v2, /device:TPU:1, one launch (start us, length us, event | category | flops | bytes accessed | tf_op | source)
XLA Modules:
  0.0 49.5 jit_solution(16549710140483557473)
XLA Ops:
  0.0 0.0 copy-start
  0.0 1.0 %copy-done = f32[2,4,8,2048]{3,2,1,0:T(8,128)S(1)} copy-done((f32[2,4,8,2048]{3,2,1,0:T(8,128)S(1)}, f32[2,4,8,2048]{3,2,1,0:T(8,128)}, u32[]{:S(2)}) %copy-start) | copy-done | bytes 524312
  1.0 1.1 %shard_map.55 = f32[16,4,8,128]{3,2,1,0:T(8,128)} custom-call(f32[1024,128]{1,0:T(8,128)S(1)} %bitcast.5), custom_call_target="tpu_custom_call" | custom-call | flops 1000000 | bytes 1000000 | tf_op jit(solution)/shard_map/pallas_call | solution.py:167
  2.1 12.0 %all-to-all-start = ((f32[16,4,8,128]{3,2,1,0:T(8,128)}), f32[16,4,8,128]{3,2,1,0:T(8,128)S(1)}, u32[]{:S(2)}, u32[]{:S(2)}) async-start(f32[16,4,8,128]{3,2,1,0:T(8,128)} %shard_map.55), calls=%async_computation | async-start | bytes 524288 | tf_op jit(solution)/shard_map/all_to_all | solution.py:188
  14.1 0.0 copy-start.5
  14.1 0.6 %copy-done.5 = f32[64]{0:T(128)S(1)} copy-done((f32[64]{0:T(128)S(1)}, f32[64]{0:T(128)}, u32[]{:S(2)}) %copy-start.5) | copy-done | bytes 280
  14.8 0.1 broadcast_in_dim.16
  14.9 0.1 mul.16
  15.0 0.5 %fusion.2 = (f32[256,128]{1,0:T(8,128)S(1)}, f32[256,128]{1,0:T(8,128)S(1)}) fusion(f32[128]{0:T(128)S(1)} %mul.16, f32[256]{0:T(256)S(1)} %convert_add_fusion, pred[128]{0:T(512)(128)(4,1)S(1)} %fusion.4), kind=kLoop, calls=%fused_computation.9 | loop fusion | flops 131072 | bytes 263808 | tf_op jit(solution)/shard_map/jit(_where)/select_n | solution.py:155
  15.5 0.0 copy-start.1
  15.7 0.9 %copy-done.1 = f32[2,4,8,2048]{3,2,1,0:T(8,128)S(1)} copy-done((f32[2,4,8,2048]{3,2,1,0:T(8,128)S(1)}, f32[2,4,8,2048]{3,2,1,0:T(8,128)}, u32[]{:S(2)}) %copy-start.1) | copy-done | bytes 524312
  16.6 0.9 %shard_map.57 = f32[16,5,8,128]{3,2,1,0:T(8,128)} custom-call(f32[1024,128]{1,0:T(8,128)S(1)} %bitcast.6, bf16[512,384]{1,0:T(8,128)(2,1)S(1)} %pad_maximum_fusion.steer_ref), custom_call_target="tpu_custom_call" | custom-call | flops 1000000 | bytes 1000000 | tf_op jit(solution)/shard_map/pallas_call | solution.py:167
  17.5 5.5 %all-to-all-done.r_ref = f32[16,4,8,128]{3,2,1,0:T(8,128)S(1)} async-done(((f32[16,4,8,128]{3,2,1,0:T(8,128)}), f32[16,4,8,128]{3,2,1,0:T(8,128)S(1)}, u32[]{:S(2)}, u32[]{:S(2)}) %all-to-all-start) | async-done | bytes 262176 | tf_op jit(solution)/shard_map/all_to_all | solution.py:188
  23.0 5.9 %all-to-all-start.1 = ((f32[16,5,8,128]{3,2,1,0:T(8,128)}), f32[16,5,8,128]{3,2,1,0:T(8,128)S(1)}, u32[]{:S(2)}, u32[]{:S(2)}) async-start(f32[16,5,8,128]{3,2,1,0:T(8,128)} %shard_map.57), calls=%async_computation.1 | async-start | bytes 655360 | tf_op jit(solution)/shard_map/all_to_all | solution.py:189
  28.9 4.2 %collective-permute-start = (f32[16,4,8,128]{3,2,1,0:T(8,128)S(1)}, f32[16,4,8,128]{3,2,1,0:T(8,128)S(1)}, u32[]{:S(2)}, u32[]{:S(2)}) collective-permute-start(f32[16,4,8,128]{3,2,1,0:T(8,128)S(1)} %all-to-all-done.r_ref), channel_id=1, source_target_pairs={{1,2},{2,1},{3,4},{4,3},{5,6},{6,5},{7,8},{8,7},{9,10},{10,9},{11,... | collective-permute-start | bytes 786440 | tf_op jit(solution)/shard_map/ppermute | solution.py:191
  33.2 7.0 %all-to-all-done.1.r_ref = f32[16,5,8,128]{3,2,1,0:T(8,128)S(1)} async-done(((f32[16,5,8,128]{3,2,1,0:T(8,128)}), f32[16,5,8,128]{3,2,1,0:T(8,128)S(1)}, u32[]{:S(2)}, u32[]{:S(2)}) %all-to-all-start.1) | async-done | bytes 327712 | tf_op jit(solution)/shard_map/all_to_all | solution.py:189
  40.2 4.4 %collective-permute-start.1 = (f32[16,4,8,128]{3,2,1,0:T(8,128)S(1)}, f32[16,4,8,128]{3,2,1,0:T(8,128)S(1)}, u32[]{:S(2)}, u32[]{:S(2)}) collective-permute-start(f32[16,4,8,128]{3,2,1,0:T(8,128)S(1)} %pad_maximum_fusion.2), channel_id=1, source_target_pairs={{0,1},{1,0},{2,3},{3,2},{4,5},{5,4},{6,7},{7,6},{8,9},{9,8},{10,11... | collective-permute-start | bytes 786440 | tf_op jit(solution)/shard_map/ppermute | solution.py:192
  44.6 0.4 shard_map.56.edge_ref
  45.1 0.0 copy-start.2
  45.1 0.0 copy-start.3
  45.1 0.0 copy-start.4
  45.1 0.6 %shard_map.58.rest_ref = f32[5,264,128]{2,1,0:T(8,128)S(1)} custom-call(f32[16,5,8,128]{3,2,1,0:T(8,128)S(1)} %all-to-all-done.1.r_ref, bf16[512,384]{1,0:T(8,128)(2,1)S(1)} %pad_maximum_fusion.steer_ref), custom_call_target="tpu_custom_call" | custom-call | flops 1000000000 | bytes 1000000 | tf_op jit(solution)/shard_map/pallas_call | solution.py:167
  45.7 0.0 collective-permute-done.o_ref
  45.7 0.0 collective-permute-done.1.e_ref
  45.8 0.4 copy-done.2
  46.1 0.0 copy-done.3
  46.2 0.1 copy-done.4
  46.2 3.3 %box.1 = bf16[256,8,128]{2,1,0:T(8,128)(2,1)} custom-call(f32[4,264,128]{2,1,0:T(8,128)S(1)} %shard_map.56.edge_ref, f32[5,264,128]{2,1,0:T(8,128)S(1)} %shard_map.58.rest_ref, f32[16,4,8,128]{3,2,1,0:T(8,128)S(1)} %collective-permute-done.o_ref, f32[16,4,8,128]{3,2,1,0:T(8,128)S(1)} %collective-permute-done.1.e_ref, ...), custom_call_target="tpu_custom_call" | custom-call | flops 1000000000 | bytes 2000000 | tf_op jit(solution)/shard_map/box/pallas_call | solution.py:196
  (8 shorter events, 0.2 us)
Async XLA Ops:
  0.0 1.0 %copy-start = (f32[2,4,8,2048]{3,2,1,0:T(8,128)S(1)}, f32[2,4,8,2048]{3,2,1,0:T(8,128)}, u32[]{:S(2)}) copy-start(f32[2,4,8,2048]{3,2,1,0:T(8,128)} %param.5) | copy-start | bytes 1572868
  2.1 20.9 %all-to-all-start = ((f32[16,4,8,128]{3,2,1,0:T(8,128)}), f32[16,4,8,128]{3,2,1,0:T(8,128)S(1)}, u32[]{:S(2)}, u32[]{:S(2)}) async-start(f32[16,4,8,128]{3,2,1,0:T(8,128)} %shard_map.55), calls=%async_computation | async-start | bytes 524288 | tf_op jit(solution)/shard_map/all_to_all | solution.py:188
  14.1 0.7 %copy-start.5 = (f32[64]{0:T(128)S(1)}, f32[64]{0:T(128)}, u32[]{:S(2)}) copy-start(f32[64]{0:T(128)} %param.6) | copy-start | bytes 772
  15.5 1.0 %copy-start.1 = (f32[2,4,8,2048]{3,2,1,0:T(8,128)S(1)}, f32[2,4,8,2048]{3,2,1,0:T(8,128)}, u32[]{:S(2)}) copy-start(f32[2,4,8,2048]{3,2,1,0:T(8,128)} %param.5) | copy-start | bytes 1572868
  23.0 17.2 %all-to-all-start.1 = ((f32[16,5,8,128]{3,2,1,0:T(8,128)}), f32[16,5,8,128]{3,2,1,0:T(8,128)S(1)}, u32[]{:S(2)}, u32[]{:S(2)}) async-start(f32[16,5,8,128]{3,2,1,0:T(8,128)} %shard_map.57), calls=%async_computation.1 | async-start | bytes 655360 | tf_op jit(solution)/shard_map/all_to_all | solution.py:189
  28.9 16.8 %collective-permute-start = (f32[16,4,8,128]{3,2,1,0:T(8,128)S(1)}, f32[16,4,8,128]{3,2,1,0:T(8,128)S(1)}, u32[]{:S(2)}, u32[]{:S(2)}) collective-permute-start(f32[16,4,8,128]{3,2,1,0:T(8,128)S(1)} %all-to-all-done.r_ref), channel_id=1, source_target_pairs={{1,2},{2,1},{3,4},{4,3},{5,6},{6,5},{7,8},{8,7},{9,10},{10,9},{11,... | collective-permute-start | bytes 786440 | tf_op jit(solution)/shard_map/ppermute | solution.py:191
  40.2 5.5 %collective-permute-start.1 = (f32[16,4,8,128]{3,2,1,0:T(8,128)S(1)}, f32[16,4,8,128]{3,2,1,0:T(8,128)S(1)}, u32[]{:S(2)}, u32[]{:S(2)}) collective-permute-start(f32[16,4,8,128]{3,2,1,0:T(8,128)S(1)} %pad_maximum_fusion.2), channel_id=1, source_target_pairs={{0,1},{1,0},{2,3},{3,2},{4,5},{5,4},{6,7},{7,6},{8,9},{9,8},{10,11... | collective-permute-start | bytes 786440 | tf_op jit(solution)/shard_map/ppermute | solution.py:192
  45.1 1.0 %copy-start.2 = (bf16[256,1024]{1,0:T(8,128)(2,1)S(1)}, bf16[256,1024]{1,0:T(8,128)(2,1)}, u32[]{:S(2)}) copy-start(bf16[256,1024]{1,0:T(8,128)(2,1)} %constant.40.clone.mid_ref) | copy-start | bytes 1572868
  45.1 1.1 %copy-start.3 = (bf16[256,384]{1,0:T(8,128)(2,1)S(1)}, bf16[256,384]{1,0:T(8,128)(2,1)}, u32[]{:S(2)}) copy-start(bf16[256,384]{1,0:T(8,128)(2,1)} %constant.42.clone.me_ref) | copy-start | bytes 589828
  45.1 1.1 %copy-start.4 = (bf16[256,384]{1,0:T(8,128)(2,1)S(1)}, bf16[256,384]{1,0:T(8,128)(2,1)}, u32[]{:S(2)}) copy-start(bf16[256,384]{1,0:T(8,128)(2,1)} %constant.41.clone.mo_ref) | copy-start | bytes 589828

commit v3 on v1

v3 whole, which is shorter than its diff:
```python
import jax
import jax.numpy as jnp
import numpy as np
from jax import lax
from jax.experimental import pallas as pl
from jax.experimental.pallas import tpu as pltpu
from jax.sharding import PartitionSpec as P


HEIGHTS = 256
ROWS = HEIGHTS + 8
LANES = 128
epsilon = 1e-06

SLOT = {0: 0, 1: 1, 2: 2, 7: 4, 6: 5, 5: 6, 3: 7, 4: 8}
HALO = 3
OWN_LANES = 48
EDGE_LANES = 18
MERGED = 4
EDGE_TILES = 48 + 16 // MERGED


def parity():
    return lax.rem(lax.axis_index("line"), 2)


def pack_kernel(x_ref, out_ref):
    blocks = x_ref.shape[0] // 64
    odd = parity()
    place = OWN_LANES + EDGE_LANES * lax.rem(lax.axis_index("acq"), MERGED)
    lane = lax.broadcasted_iota(jnp.int32, (8, LANES), 1)
    halo = [jnp.zeros((8, LANES), jnp.float32) for _ in range(blocks)]
    for m in range(8):
        line = m + odd * (7 - 2 * m)
        for start in (6 * m, place + 6 * m)[: 2 if m < 3 else 1]:
            left = (lane >= start) & (lane < start + 3)
            right = (lane >= start + 3) & (lane < start + 6)
            for j in range(blocks):
                tile = x_ref[pl.ds(8 * j + line, 8, stride=8 * blocks), :]
                if isinstance(start, int):
                    out_ref[blocks - 1 - j, SLOT[m]] = tile
                moved = pltpu.roll(tile, start + 3, 1)
                if j + 1 < blocks:
                    halo[j + 1] = jnp.where(left, moved, halo[j + 1])
                if j >= 1:
                    halo[j - 1] = jnp.where(right, moved, halo[j - 1])
    for j in range(blocks):
        out_ref[blocks - 1 - j, HALO] = halo[j]


def edge_kernel(r_ref, o_ref, e_ref):
    lane = lax.broadcasted_iota(jnp.int32, (8, LANES), 1)
    for j in range(16):
        for s in range(3):
            o_ref[3 * j + s] = r_ref[j, s]
        for s in range(4):
            e_ref[j, s] = r_ref[j, HALO + s]
    for g in range(16 // MERGED):
        total = r_ref[MERGED * g, HALO]
        for j in range(1, MERGED):
            total = total + r_ref[MERGED * g + j, HALO]
        o_ref[48 + g] = jnp.where(lane < OWN_LANES, 0.0, total)


def beam_pair(first, second, steer_ref, beams_ref):
    both = jnp.concatenate([first.reshape(LANES, LANES), second.reshape(LANES, LANES)], axis=1)
    high = both.astype(jnp.bfloat16)
    low = (both - high.astype(jnp.float32)).astype(jnp.bfloat16)
    stacked = jnp.concatenate([high, low, high], axis=0)
    beams_ref[...] = jnp.dot(steer_ref[...], stacked, preferred_element_type=jnp.float32)
    re, im = beams_ref[:HEIGHTS], beams_ref[HEIGHTS:]
    power = re * re + im * im
    squares = (both * both).reshape(16, 8, 2 * LANES).sum(axis=0)
    return jnp.concatenate([power, squares], axis=0)


def own_kernel(r_ref, steer_ref, out_ref, beams_ref):
    for s in (0, 2, 4, 6, 8):
        t = min(s + 1, 8)
        both = beam_pair(r_ref[:, s], r_ref[:, t], steer_ref, beams_ref)
        out_ref[s] = both[:, :LANES]
        if t != s:
            out_ref[t] = both[:, LANES:]


def halves(field):
    high = field.astype(jnp.bfloat16)
    low = (field - high.astype(jnp.float32)).astype(jnp.bfloat16)
    return jnp.concatenate([high, low], axis=1)


def boxed(total, correction):
    lane = lax.broadcasted_iota(jnp.int32, total.shape, 1)
    box = total + correction
    for d in (1, 2, 3):
        box = box + jnp.where(lane >= d, pltpu.roll(total, d, 1), 0.0)
        box = box + jnp.where(lane < LANES - d, pltpu.roll(total, LANES - d, 1), 0.0)
    return box


def normalize(m, odd, box_of, flat_ref):
    line = m + odd * (7 - 2 * m)
    energy = box_of(m, slice(HEIGHTS, ROWS)).sum(axis=0, keepdims=True)
    inverse = 1.0 / (energy + epsilon)
    for k in range(0, HEIGHTS, 64):
        flat_ref[pl.ds(8 * k + line, 64, stride=8), :] = box_of(m, slice(k, k + 64)) * inverse


def inner_kernel(own_ref, e_ref, steer_ref, mid_ref, me_ref, flat_ref, part_ref, cor_ref, beams_ref, side_ref, all_ref):
    for s in (0, 2):
        both = beam_pair(e_ref[:, s], e_ref[:, s + 1], steer_ref, beams_ref)
        side_ref[s] = both[:, :LANES]
        side_ref[s + 1] = both[:, LANES:]
    all_ref[...] = jnp.dot(halves(own_ref[HALO]), mid_ref[...], preferred_element_type=jnp.float32)
    all_ref[:, 5 * LANES :] += jnp.dot(halves(side_ref[0]), me_ref[...], preferred_element_type=jnp.float32)
    cor_ref[...] = all_ref[:, : 3 * LANES]

    def summed(m, rows):
        total = None
        for position in range(max(m - 3, 0), m + 4):
            term = side_ref[position - 7, rows] if position > 7 else own_ref[SLOT[position], rows]
            total = term if total is None else total + term
        return total

    for m in range(3):
        for k in range(0, ROWS, 88):
            part_ref[m, k : k + 88] = summed(m, slice(k, k + 88))
    odd = parity()
    for m in range(3, 8):
        normalize(m, odd, lambda m, rows: boxed(summed(m, rows), all_ref[rows, m * LANES : (m + 1) * LANES]), flat_ref)


def outer_kernel(o_ref, part_ref, cor_ref, flat_ref, steer_ref, mo_ref, out_ref, beams_ref, side_ref, halo_ref, all_ref, edge_ref, done_ref, sems):
    lane = lax.broadcasted_iota(jnp.int32, (8, LANES), 1)
    for j in range(16):
        start = OWN_LANES + EDGE_LANES * ((15 - j) % MERGED)
        halo_ref[j] = jnp.where(lane < EDGE_LANES, pltpu.roll(o_ref[48 + j // MERGED], LANES - start, 1), 0.0)
    lines = o_ref[:48].reshape(16, 3, 8, LANES)
    for s in (0, 2):
        both = beam_pair(lines[:, s], lines[:, 1] if s == 0 else halo_ref[...], steer_ref, beams_ref)
        side_ref[s] = both[:, :LANES]
        side_ref[s + 1] = both[:, LANES:]
    all_ref[...] = cor_ref[...] + jnp.dot(halves(side_ref[3]), mo_ref[...], preferred_element_type=jnp.float32)

    def box_of(m, rows):
        total = part_ref[m, rows]
        for i in range(3 - m):
            total = total + side_ref[i, rows]
        return boxed(total, all_ref[rows, m * LANES : (m + 1) * LANES])

    odd = parity()
    for m in range(3):
        normalize(m, odd, box_of, edge_ref)
    sub = lax.broadcasted_iota(jnp.int32, (16, 8, LANES), 1)
    edge = jnp.where(odd == 1, 7 - sub, sub) < 3
    copies = []
    for q in range(4):
        for k in range(64 * q, 64 * q + 64, 16):
            rows = slice(8 * k, 8 * k + 128)
            merged = jnp.where(edge, edge_ref[rows].reshape(16, 8, LANES), flat_ref[rows].reshape(16, 8, LANES))
            done_ref[k : k + 16] = merged.astype(jnp.bfloat16)
        copy = pltpu.make_async_copy(done_ref.at[pl.ds(64 * q, 64)], out_ref.at[pl.ds(64 * q, 64)], sems.at[q])
        copy.start()
        copies.append(copy)
    for copy in copies:
        copy.wait()


def spread():
    column = np.array([-3, -2, -1, 128, 129, 130])
    near = np.abs(column[:, None] - np.arange(LANES)[None, :]) <= 3

    def matrix(position_of, lines, used):
        full = np.zeros((LANES, len(lines), LANES), np.float32)
        for n in used:
            for i, m in enumerate(lines):
                if abs(position_of(n) - m) <= 3:
                    full[6 * n : 6 * n + 6, i] = near
        full = full.reshape(LANES, -1)
        return jnp.asarray(np.concatenate([full, full], axis=0), jnp.bfloat16)

    mid = matrix(lambda n: n, range(8), range(8))
    mo = matrix(lambda n: -1 - n, (0, 1, 2), (0, 1, 2))
    me = matrix(lambda n: 15 - n, (5, 6, 7), (5, 6, 7))
    return mid, mo, me


def steering(wavenumbers):
    waves = jnp.broadcast_to(wavenumbers.reshape(16, 1, 4)[::-1], (16, 2, 4)).reshape(LANES)
    real = (jnp.arange(LANES) // 4) % 2 == 0
    heights = jnp.arange(HEIGHTS, dtype=jnp.int32).astype(jnp.float32) - jnp.float32(HEIGHTS // 2)
    phases = heights[:, None] * waves[None, :]
    cosine, sine = jnp.cos(phases), jnp.sin(phases)
    full = jnp.concatenate([jnp.where(real, cosine, sine), jnp.where(real, -sine, cosine)], axis=0)
    high = lax.reduce_precision(full, 8, 7)
    low = (full - high).astype(jnp.bfloat16)
    high = high.astype(jnp.bfloat16)
    return jnp.concatenate([high, high, low], axis=1)


VMEM = pl.BlockSpec(memory_space=pltpu.VMEM)
ANY = pl.BlockSpec(memory_space=pl.ANY)


def call(kernel, shapes, vmem, flops, scratch=(), out=VMEM, dtype=jnp.float32):
    def on(*operands):
        return pl.pallas_call(
            kernel,
            out_shape=[jax.ShapeDtypeStruct(shape, dtype) for shape in shapes],
            in_specs=[VMEM] * len(operands),
            out_specs=[out] * len(shapes),
            scratch_shapes=list(scratch),
            compiler_params=pltpu.CompilerParams(vmem_limit_bytes=vmem << 20),
            cost_estimate=pl.CostEstimate(flops=flops, bytes_accessed=1000000, transcendentals=0),
        )(*operands)

    return on


def spectrum(slc_stack, wavenumbers):
    lines, acqs = lax.axis_size("line"), lax.axis_size("acq")
    outer = [pair for i in range(1, lines - 1, 2) for pair in ((i, i + 1), (i + 1, i))]
    inner = [pair for i in range(0, lines, 2) for pair in ((i, i + 1), (i + 1, i))]
    beams = pltpu.VMEM((2 * HEIGHTS, 2 * LANES), jnp.float32)
    stack = slc_stack.reshape(8, 8, -1, LANES).transpose(0, 2, 1, 3).reshape(-1, LANES)
    (packed,) = call(pack_kernel, [(16, 9, 8, LANES)], 4, 1000000)(stack)
    gathered = lax.all_to_all(packed, "acq", 0, 0, tiled=True, axis_index_groups=[list(range(acqs))[::-1]])
    steer = steering(wavenumbers)
    mid, mo, me = spread()
    to_o, to_e = call(edge_kernel, [(EDGE_TILES, 8, LANES), (16, 4, 8, LANES)], 4, 1000000)(gathered)
    side_o = lax.ppermute(to_o, "line", outer)
    side_e = lax.ppermute(to_e, "line", inner)
    (own,) = call(own_kernel, [(9, ROWS, LANES)], 10, 1000000000, [beams])(gathered, steer)
    flat, part, cor = call(
        inner_kernel,
        [(8 * HEIGHTS, LANES), (3, ROWS, LANES), (ROWS, 3 * LANES)],
        14,
        1000000000,
        [beams, pltpu.VMEM((4, ROWS, LANES), jnp.float32), pltpu.VMEM((ROWS, 8 * LANES), jnp.float32)],
    )(own, side_e, steer, mid, me)
    (result,) = call(
        outer_kernel,
        [(HEIGHTS, 8, LANES)],
        12,
        1000000000,
        [
            beams,
            pltpu.VMEM((4, ROWS, LANES), jnp.float32),
            pltpu.VMEM((16, 8, LANES), jnp.float32),
            pltpu.VMEM((ROWS, 3 * LANES), jnp.float32),
            pltpu.VMEM((8 * HEIGHTS, LANES), jnp.float32),
            pltpu.VMEM((HEIGHTS, 8, LANES), jnp.bfloat16),
            pltpu.SemaphoreType.DMA((4,)),
        ],
        out=ANY,
        dtype=jnp.bfloat16,
    )(side_o, part, cor, flat, steer, mo)
    return result


def solution(mesh):
    placed = (P(None, "acq", "line", None), P())
    return jax.shard_map(spectrum, mesh=mesh, in_specs=placed, out_specs=P(None, "line", "acq"), check_vma=False)
```

time: 53 us -> 48.9 us (0.923)
  waiting for transfers between devices: 24.8 us -> 19.5 us
  starting transfers between devices: 20.5 us -> 21.4 us
    ppermute x2, waiting for transfers between devices: 9.36 us -> 6.51 us  [the longest x1 6.5 us: spectrum(): side_o = lax.ppermute(to_o, 'line', outer)]
    all_to_all x1, waiting for transfers between devices: 15.4 us -> 13 us  [spectrum(): lax.all_to_all(packed, 'acq', 0, 0, tiled=True, axis_index_groups=[list(r...]
    all_to_all x1, starting transfers between devices: 11.2 us -> 13.2 us  [spectrum(): lax.all_to_all(packed, 'acq', 0, 0, tiled=True, axis_index_groups=[list(r...]
    ppermute x2, starting transfers between devices: 9.31 us -> 8.13 us  [the longest x1 4.34 us: spectrum(): side_o = lax.ppermute(to_o, 'line', outer)]
    pallas_call x3 -> x5, Pallas kernels: 5.35 us -> 5.47 us  [on(): pl.pallas_call(kernel, out_shape=[jax.ShapeDtypeStruct(shape, dtype) for...]
  transfers between devices with their start and end apart: 3 -> 3, of which waited for: 2 -> 2; matrix products, arithmetic and copies ran while one was open for 2% -> 2% of each run, Pallas kernels for 2% -> 5%
where the time goes in v3:
time: 48.9 us; the launch traced here: 48.6 us
  starting transfers between devices  21.4 us (44%)
  waiting for transfers between devices  19.5 us (40%)
  Pallas kernels  5.47 us (11%)
  local copies, waits for them, and re-layouts  1.48 us (3%)
  other arithmetic  0.65 us (1%)
    all_to_all x1, starting transfers between devices, spectrum(): lax.all_to_all(packed, 'acq', 0, 0, tiled=True, axis_index_groups=[list(r...  13.2 us
    all_to_all x1, waiting for transfers between devices, spectrum(): lax.all_to_all(packed, 'acq', 0, 0, tiled=True, axis_index_groups=[list(r...  13 us
    ppermute x1, waiting for transfers between devices, spectrum(): side_o = lax.ppermute(to_o, 'line', outer)  6.5 us
    pallas_call x5, Pallas kernels, on(): pl.pallas_call(kernel, out_shape=[jax.ShapeDtypeStruct(shape, dtype) for...  5.47 us
    ppermute x1, starting transfers between devices, spectrum(): side_o = lax.ppermute(to_o, 'line', outer)  4.34 us
    ppermute x1, starting transfers between devices, spectrum(): side_e = lax.ppermute(to_e, 'line', inner)  3.79 us
    unnamed x10, local copies, waits for them, and re-layouts  1.25 us
  transfers between devices with their start and end apart: 3, of which 2 were waited for; matrix products, arithmetic and copies ran while one was open for 2% of the time, Pallas kernels for 5%

profile of v3, /device:TPU:23, one launch (start us, length us, event | category | flops | bytes accessed | tf_op | source)
XLA Modules:
  0.0 48.6 jit_solution(9774649601085212923)
XLA Ops:
  0.0 0.0 copy-start.4
  0.0 0.0 copy-start
  0.0 1.1 %copy-done = f32[2,4,8,2048]{3,2,1,0:T(8,128)S(1)} copy-done((f32[2,4,8,2048]{3,2,1,0:T(8,128)S(1)}, f32[2,4,8,2048]{3,2,1,0:T(8,128)}, u32[]{:S(2)}) %copy-start) | copy-done | bytes 524312
  1.1 1.2 %shard_map.55 = f32[16,9,8,128]{3,2,1,0:T(8,128)} custom-call(f32[1024,128]{1,0:T(8,128)S(1)} %bitcast.6), custom_call_target="tpu_custom_call" | custom-call | flops 1000000 | bytes 1000000 | tf_op jit(solution)/shard_map/pallas_call | solution.py:207
  2.3 13.2 %all-to-all-start = ((f32[16,9,8,128]{3,2,1,0:T(8,128)}), f32[16,9,8,128]{3,2,1,0:T(8,128)S(1)}, u32[]{:S(2)}, u32[]{:S(2)}) async-start(f32[16,9,8,128]{3,2,1,0:T(8,128)} %shard_map.55), calls=%async_computation | async-start | bytes 1179648 | tf_op jit(solution)/shard_map/all_to_all | solution.py:227
  15.5 0.0 copy-done.4
  15.5 0.1 reshape.17
  15.6 0.1 mul.16
  15.8 0.5 %fusion.2 = (f32[256,128]{1,0:T(8,128)S(1)}, f32[256,128]{1,0:T(8,128)S(1)}) fusion(f32[128]{0:T(128)S(1)} %mul.16, f32[256]{0:T(256)S(1)} %convert_add_fusion, pred[128]{0:T(512)(128)(4,1)S(1)} %fusion.4), kind=kLoop, calls=%fused_computation.8 | loop fusion | flops 131072 | bytes 263808 | tf_op jit(solution)/shard_map/jit(_where)/select_n | solution.py:194
  16.3 13.0 %all-to-all-done.r_ref = f32[16,9,8,128]{3,2,1,0:T(8,128)S(1)} async-done(((f32[16,9,8,128]{3,2,1,0:T(8,128)}), f32[16,9,8,128]{3,2,1,0:T(8,128)S(1)}, u32[]{:S(2)}, u32[]{:S(2)}) %all-to-all-start) | async-done | bytes 589856 | tf_op jit(solution)/shard_map/all_to_all | solution.py:227
  29.4 3.8 %collective-permute-start.1 = (f32[16,4,8,128]{3,2,1,0:T(8,128)S(1)}, f32[16,4,8,128]{3,2,1,0:T(8,128)S(1)}, u32[]{:S(2)}, u32[]{:S(2)}) collective-permute-start(f32[16,4,8,128]{3,2,1,0:T(8,128)S(1)} %get-tuple-element.11), channel_id=1, source_target_pairs={{0,1},{1,0},{2,3},{3,2},{4,5},{5,4},{6,7},{7,6},{8,9},{9,8},{10,11... | collective-permute-start | bytes 786440 | tf_op jit(solution)/shard_map/ppermute | solution.py:232
  33.3 4.3 %collective-permute-start = (f32[52,8,128]{2,1,0:T(8,128)S(1)}, f32[52,8,128]{2,1,0:T(8,128)S(1)}, u32[]{:S(2)}, u32[]{:S(2)}) collective-permute-start(f32[52,8,128]{2,1,0:T(8,128)S(1)} %get-tuple-element.10), channel_id=1, source_target_pairs={{1,2},{2,1},{3,4},{4,3},{5,6},{6,5},{7,8},{8,7},{9,10},{10,9},{11,... | collective-permute-start | bytes 638984 | tf_op jit(solution)/shard_map/ppermute | solution.py:231
  37.7 0.0 copy-start.1
  37.7 0.0 copy-start.3
  37.7 0.9 %shard_map.57.own_ref = f32[9,264,128]{2,1,0:T(8,128)S(1)} custom-call(f32[16,9,8,128]{3,2,1,0:T(8,128)S(1)} %all-to-all-done.r_ref, bf16[512,384]{1,0:T(8,128)(2,1)S(1)} %pad_maximum_fusion.steer_ref), custom_call_target="tpu_custom_call" | custom-call | flops 1000000000 | bytes 1000000 | tf_op jit(solution)/shard_map/pallas_call | solution.py:207
  38.5 0.0 copy-start.2
  38.5 0.0 collective-permute-done.1.e_ref
  38.6 0.1 copy-done.1
  38.7 0.0 copy-done.3
  38.7 1.5 %shard_map.58 = (f32[2048,128]{1,0:T(8,128)S(1)}, f32[3,264,128]{2,1,0:T(8,128)S(1)}, f32[264,384]{1,0:T(8,128)S(1)}) custom-call(f32[9,264,128]{2,1,0:T(8,128)S(1)} %shard_map.57.own_ref, f32[16,4,8,128]{3,2,1,0:T(8,128)S(1)} %collective-permute-done.1.e_ref, bf16[512,384]{1,0:T(8,128)(2,1)S(1)} %pad_maximum_fusion.steer_ref, ...), custom_call_target="tpu_custom_call" | custom-call | flops 1000000000 | bytes 1000000 | tf_op jit(solution)/shard_map/pallas_call | solution.py:207
  40.2 6.5 %collective-permute-done.o_ref = f32[52,8,128]{2,1,0:T(8,128)S(1)} collective-permute-done((f32[52,8,128]{2,1,0:T(8,128)S(1)}, f32[52,8,128]{2,1,0:T(8,128)S(1)}, u32[]{:S(2)}, u32[]{:S(2)}) %collective-permute-start) | collective-permute-done | bytes 213024 | tf_op jit(solution)/shard_map/ppermute | solution.py:231
  46.7 0.0 copy-done.2
  46.7 1.9 %shard_map.59 = bf16[256,8,128]{2,1,0:T(8,128)(2,1)} custom-call(f32[52,8,128]{2,1,0:T(8,128)S(1)} %collective-permute-done.o_ref, f32[3,264,128]{2,1,0:T(8,128)S(1)} %get-tuple-element.12.part_ref, f32[264,384]{1,0:T(8,128)S(1)} %get-tuple-element.13.cor_ref, f32[2048,128]{1,0:T(8,128)S(1)} %get-tuple-element.14.flat_ref, ...), custom_call_target="tpu_custom_call" | custom-call | flops 1000000000 | bytes 1000000 | tf_op jit(solution)/shard_map/pallas_call | solution.py:207
  (7 shorter events, 0.2 us)
Async XLA Ops:
  0.0 15.5 %copy-start.4 = (f32[64]{0:T(128)S(1)}, f32[64]{0:T(128)}, u32[]{:S(2)}) copy-start(f32[64]{0:T(128)} %param.6) | copy-start | bytes 772
  0.0 1.1 %copy-start = (f32[2,4,8,2048]{3,2,1,0:T(8,128)S(1)}, f32[2,4,8,2048]{3,2,1,0:T(8,128)}, u32[]{:S(2)}) copy-start(f32[2,4,8,2048]{3,2,1,0:T(8,128)} %param.5) | copy-start | bytes 1572868
  2.3 27.1 %all-to-all-start = ((f32[16,9,8,128]{3,2,1,0:T(8,128)}), f32[16,9,8,128]{3,2,1,0:T(8,128)S(1)}, u32[]{:S(2)}, u32[]{:S(2)}) async-start(f32[16,9,8,128]{3,2,1,0:T(8,128)} %shard_map.55), calls=%async_computation | async-start | bytes 1179648 | tf_op jit(solution)/shard_map/all_to_all | solution.py:227
  29.4 9.2 %collective-permute-start.1 = (f32[16,4,8,128]{3,2,1,0:T(8,128)S(1)}, f32[16,4,8,128]{3,2,1,0:T(8,128)S(1)}, u32[]{:S(2)}, u32[]{:S(2)}) collective-permute-start(f32[16,4,8,128]{3,2,1,0:T(8,128)S(1)} %get-tuple-element.11), channel_id=1, source_target_pairs={{0,1},{1,0},{2,3},{3,2},{4,5},{5,4},{6,7},{7,6},{8,9},{9,8},{10,11... | collective-permute-start | bytes 786440 | tf_op jit(solution)/shard_map/ppermute | solution.py:232
  33.3 13.5 %collective-permute-start = (f32[52,8,128]{2,1,0:T(8,128)S(1)}, f32[52,8,128]{2,1,0:T(8,128)S(1)}, u32[]{:S(2)}, u32[]{:S(2)}) collective-permute-start(f32[52,8,128]{2,1,0:T(8,128)S(1)} %get-tuple-element.10), channel_id=1, source_target_pairs={{1,2},{2,1},{3,4},{4,3},{5,6},{6,5},{7,8},{8,7},{9,10},{10,9},{11,... | collective-permute-start | bytes 638984 | tf_op jit(solution)/shard_map/ppermute | solution.py:231
  37.7 1.0 %copy-start.1 = (bf16[256,1024]{1,0:T(8,128)(2,1)S(1)}, bf16[256,1024]{1,0:T(8,128)(2,1)}, u32[]{:S(2)}) copy-start(bf16[256,1024]{1,0:T(8,128)(2,1)} %constant.40.clone.mid_ref) | copy-start | bytes 1572868
  37.7 1.1 %copy-start.3 = (bf16[256,384]{1,0:T(8,128)(2,1)S(1)}, bf16[256,384]{1,0:T(8,128)(2,1)}, u32[]{:S(2)}) copy-start(bf16[256,384]{1,0:T(8,128)(2,1)} %constant.42.clone.me_ref) | copy-start | bytes 589828
  38.5 8.2 %copy-start.2 = (bf16[256,384]{1,0:T(8,128)(2,1)S(1)}, bf16[256,384]{1,0:T(8,128)(2,1)}, u32[]{:S(2)}) copy-start(bf16[256,384]{1,0:T(8,128)(2,1)} %constant.41.clone.mo_ref) | copy-start | bytes 589828

commit v4 on v3

--- a/solution.py
+++ b/solution.py
@@ -18,34 +18,52 @@
 EDGE_LANES = 18
 MERGED = 4
 EDGE_TILES = 48 + 16 // MERGED
+PIECES = 4
+PLACE = [2 * z + y for z in (4, 3, 5, 2, 6, 1, 7, 0) for y in (0, 1)]
+MERGE = [acq % MERGED for acq in PLACE]
 
 
 def parity():
     return lax.rem(lax.axis_index("line"), 2)
 
 
-def pack_kernel(x_ref, out_ref):
+def pack_kernel(x_hbm, out_hbm, x_ref, out_ref, in_sems, out_sems):
     blocks = x_ref.shape[0] // 64
+    step = blocks // PIECES
+    wide = x_ref.reshape(8, 8 * blocks, LANES)
+    loads = []
+    for q in range(PIECES):
+        rows = pl.ds(8 * step * q, 8 * step)
+        loads.append(pltpu.make_async_copy(x_hbm.at[:, rows], wide.at[:, rows], in_sems.at[q]))
+        loads[q].start()
     odd = parity()
     place = OWN_LANES + EDGE_LANES * lax.rem(lax.axis_index("acq"), MERGED)
     lane = lax.broadcasted_iota(jnp.int32, (8, LANES), 1)
-    halo = [jnp.zeros((8, LANES), jnp.float32) for _ in range(blocks)]
-    for m in range(8):
-        line = m + odd * (7 - 2 * m)
-        for start in (6 * m, place + 6 * m)[: 2 if m < 3 else 1]:
-            left = (lane >= start) & (lane < start + 3)
-            right = (lane >= start + 3) & (lane < start + 6)
-            for j in range(blocks):
+    zero = jnp.zeros((8, LANES), jnp.float32)
+    halo = [zero, zero]
+    stores = []
+    for q in range(PIECES):
+        loads[q].wait()
+        for j in range(step * q, step * q + step):
+            halo.append(zero)
+            for m in range(8):
+                line = m + odd * (7 - 2 * m)
                 tile = x_ref[pl.ds(8 * j + line, 8, stride=8 * blocks), :]
-                if isinstance(start, int):
-                    out_ref[blocks - 1 - j, SLOT[m]] = tile
-                moved = pltpu.roll(tile, start + 3, 1)
-                if j + 1 < blocks:
-                    halo[j + 1] = jnp.where(left, moved, halo[j + 1])
-                if j >= 1:
-                    halo[j - 1] = jnp.where(right, moved, halo[j - 1])
-    for j in range(blocks):
-        out_ref[blocks - 1 - j, HALO] = halo[j]
+                out_ref[PLACE.index(j), SLOT[m]] = tile
+                for start in (6 * m, place + 6 * m)[: 2 if m < 3 else 1]:
+                    left = (lane >= start) & (lane < start + 3)
+                    right = (lane >= start + 3) & (lane < start + 6)
+                    moved = pltpu.roll(tile, start + 3, 1)
+                    halo[j + 2] = jnp.where(left, moved, halo[j + 2])
+                    halo[j] = jnp.where(right, moved, halo[j])
+        ready = range(max(step * q - 1, 0), step * q + step - 1 if q < PIECES - 1 else blocks)
+        for j in ready:
+            n = PLACE.index(j)
+            out_ref[n, HALO] = halo[j + 1]
+            stores.append(pltpu.make_async_copy(out_ref.at[n], out_hbm.at[n], out_sems.at[j]))
+            stores[-1].start()
+    for store in stores:
+        store.wait()
 
 
 def edge_kernel(r_ref, o_ref, e_ref):
@@ -133,7 +151,7 @@
 def outer_kernel(o_ref, part_ref, cor_ref, flat_ref, steer_ref, mo_ref, out_ref, beams_ref, side_ref, halo_ref, all_ref, edge_ref, done_ref, sems):
     lane = lax.broadcasted_iota(jnp.int32, (8, LANES), 1)
     for j in range(16):
-        start = OWN_LANES + EDGE_LANES * ((15 - j) % MERGED)
+        start = OWN_LANES + EDGE_LANES * MERGE[j]
         halo_ref[j] = jnp.where(lane < EDGE_LANES, pltpu.roll(o_ref[48 + j // MERGED], LANES - start, 1), 0.0)
     lines = o_ref[:48].reshape(16, 3, 8, LANES)
     for s in (0, 2):
@@ -186,7 +204,9 @@
 
 
 def steering(wavenumbers):
-    waves = jnp.broadcast_to(wavenumbers.reshape(16, 1, 4)[::-1], (16, 2, 4)).reshape(LANES)
+    planes = wavenumbers.reshape(8, 8)
+    ordered = jnp.stack([planes[4:], planes[:4][::-1]], axis=1).reshape(16, 1, 4)
+    waves = jnp.broadcast_to(ordered, (16, 2, 4)).reshape(LANES)
     real = (jnp.arange(LANES) // 4) % 2 == 0
     heights = jnp.arange(HEIGHTS, dtype=jnp.int32).astype(jnp.float32) - jnp.float32(HEIGHTS // 2)
     phases = heights[:, None] * waves[None, :]
@@ -202,12 +222,12 @@
 ANY = pl.BlockSpec(memory_space=pl.ANY)
 
 
-def call(kernel, shapes, vmem, flops, scratch=(), out=VMEM, dtype=jnp.float32):
+def call(kernel, shapes, vmem, flops, scratch=(), out=VMEM, dtype=jnp.float32, into=VMEM):
     def on(*operands):
         return pl.pallas_call(
             kernel,
             out_shape=[jax.ShapeDtypeStruct(shape, dtype) for shape in shapes],
-            in_specs=[VMEM] * len(operands),
+            in_specs=[into] * len(operands),
             out_specs=[out] * len(shapes),
             scratch_shapes=list(scratch),
             compiler_params=pltpu.CompilerParams(vmem_limit_bytes=vmem << 20),
@@ -218,13 +238,26 @@
 
 
 def spectrum(slc_stack, wavenumbers):
-    lines, acqs = lax.axis_size("line"), lax.axis_size("acq")
+    lines = lax.axis_size("line")
     outer = [pair for i in range(1, lines - 1, 2) for pair in ((i, i + 1), (i + 1, i))]
     inner = [pair for i in range(0, lines, 2) for pair in ((i, i + 1), (i + 1, i))]
     beams = pltpu.VMEM((2 * HEIGHTS, 2 * LANES), jnp.float32)
-    stack = slc_stack.reshape(8, 8, -1, LANES).transpose(0, 2, 1, 3).reshape(-1, LANES)
-    (packed,) = call(pack_kernel, [(16, 9, 8, LANES)], 4, 1000000)(stack)
-    gathered = lax.all_to_all(packed, "acq", 0, 0, tiled=True, axis_index_groups=[list(range(acqs))[::-1]])
+    stack = slc_stack.reshape(8, 8, -1, LANES).transpose(0, 2, 1, 3).reshape(8, -1, LANES)
+    (packed,) = call(
+        pack_kernel,
+        [(16, 9, 8, LANES)],
+        60,
+        1000000,
+        [
+            pltpu.VMEM((1024, LANES), jnp.float32),
+            pltpu.VMEM((16, 9, 8, LANES), jnp.float32),
+            pltpu.SemaphoreType.DMA((PIECES,)),
+            pltpu.SemaphoreType.DMA((16,)),
+        ],
+        out=ANY,
+        into=ANY,
+    )(stack)
+    gathered = lax.all_to_all(packed, "acq", 0, 0, tiled=True, axis_index_groups=[PLACE])
     steer = steering(wavenumbers)
     mid, mo, me = spread()
     to_o, to_e = call(edge_kernel, [(EDGE_TILES, 8, LANES), (16, 4, 8, LANES)], 4, 1000000)(gathered)

time: 48.9 us -> 49 us (level)
  Pallas kernels: 5.47 us -> 6.58 us
  local copies, waits for them, and re-layouts: 1.48 us -> 0.69 us
    pallas_call x5, Pallas kernels: 5.47 us -> 6.58 us  [on(): pl.pallas_call(kernel, out_shape=[jax.ShapeDtypeStruct(shape, dtype) for...]
    unnamed x10 -> x8, local copies, waits for them, and re-layouts: 1.25 us -> 0.21 us
    ppermute x1, starting transfers between devices: 3.79 us -> 2.83 us  [spectrum(): side_e = lax.ppermute(to_e, 'line', inner)]
    all_to_all x1, starting transfers between devices: 13.2 us -> 14.1 us  [spectrum(): lax.all_to_all(packed, 'acq', 0, 0, tiled=True, axis_index_groups=[PLACE])]
where the time goes in v4:
time: 49 us; the launch traced here: 48.7 us
  starting transfers between devices  21.2 us (43%)
  waiting for transfers between devices  19.4 us (40%)
  Pallas kernels  6.58 us (13%)
  local copies, waits for them, and re-layouts  0.69 us (1%)
  other arithmetic  0.65 us (1%)
    all_to_all x1, starting transfers between devices, spectrum(): lax.all_to_all(packed, 'acq', 0, 0, tiled=True, axis_index_groups=[PLACE])  14.1 us
    all_to_all x1, waiting for transfers between devices, spectrum(): lax.all_to_all(packed, 'acq', 0, 0, tiled=True, axis_index_groups=[PLACE])  12.8 us
    ppermute x1, waiting for transfers between devices, spectrum(): side_o = lax.ppermute(to_o, 'line', outer)  6.65 us
    pallas_call x5, Pallas kernels, on(): pl.pallas_call(kernel, out_shape=[jax.ShapeDtypeStruct(shape, dtype) for...  6.58 us
    ppermute x1, starting transfers between devices, spectrum(): side_o = lax.ppermute(to_o, 'line', outer)  4.34 us
    ppermute x1, starting transfers between devices, spectrum(): side_e = lax.ppermute(to_e, 'line', inner)  2.83 us
  transfers between devices with their start and end apart: 3, of which 2 were waited for; matrix products, arithmetic and copies ran while one was open for 2% of the time, Pallas kernels for 5%

profile of v4, /device:TPU:23, one launch (start us, length us, event | category | flops | bytes accessed | tf_op | source)
XLA Modules:
  0.0 48.7 jit_solution(5183048632666954488)
XLA Ops:
  0.0 0.0 copy-start.3
  0.0 2.3 %shard_map.55 = f32[16,9,8,128]{3,2,1,0:T(8,128)} custom-call(f32[8,128,128]{2,1,0:T(8,128)} %bitcast.6), custom_call_target="tpu_custom_call" | custom-call | flops 1000000 | bytes 1000000 | tf_op jit(solution)/shard_map/pallas_call | solution.py:227
  2.3 14.1 %all-to-all-start = ((f32[16,9,8,128]{3,2,1,0:T(8,128)}), f32[16,9,8,128]{3,2,1,0:T(8,128)S(1)}, u32[]{:S(2)}, u32[]{:S(2)}) async-start(f32[16,9,8,128]{3,2,1,0:T(8,128)} %shard_map.55), calls=%async_computation | async-start | bytes 1179648 | tf_op jit(solution)/shard_map/all_to_all | solution.py:260
  16.4 0.0 copy-done.3
  16.4 0.1 fusion.6
  16.5 0.1 stack.9
  16.6 0.1 slice.28
  16.7 0.1 broadcast_in_dim.16
  16.8 0.1 mul.16
  16.9 0.5 %fusion.2 = (f32[256,128]{1,0:T(8,128)S(1)}, f32[256,128]{1,0:T(8,128)S(1)}) fusion(f32[128]{0:T(128)S(1)} %mul.16, f32[256]{0:T(256)S(1)} %convert_add_fusion, pred[128]{0:T(512)(128)(4,1)S(1)} %fusion.4), kind=kLoop, calls=%fused_computation.8 | loop fusion | flops 131072 | bytes 263808 | tf_op jit(solution)/shard_map/jit(_where)/select_n | solution.py:214
  17.5 12.8 %all-to-all-done.r_ref = f32[16,9,8,128]{3,2,1,0:T(8,128)S(1)} async-done(((f32[16,9,8,128]{3,2,1,0:T(8,128)}), f32[16,9,8,128]{3,2,1,0:T(8,128)S(1)}, u32[]{:S(2)}, u32[]{:S(2)}) %all-to-all-start) | async-done | bytes 589856 | tf_op jit(solution)/shard_map/all_to_all | solution.py:260
  30.3 2.8 %collective-permute-start.1 = (f32[16,4,8,128]{3,2,1,0:T(8,128)S(1)}, f32[16,4,8,128]{3,2,1,0:T(8,128)S(1)}, u32[]{:S(2)}, u32[]{:S(2)}) collective-permute-start(f32[16,4,8,128]{3,2,1,0:T(8,128)S(1)} %get-tuple-element.11), channel_id=1, source_target_pairs={{0,1},{1,0},{2,3},{3,2},{4,5},{5,4},{6,7},{7,6},{8,9},{9,8},{10,11... | collective-permute-start | bytes 786440 | tf_op jit(solution)/shard_map/ppermute | solution.py:265
  33.2 4.3 %collective-permute-start = (f32[52,8,128]{2,1,0:T(8,128)S(1)}, f32[52,8,128]{2,1,0:T(8,128)S(1)}, u32[]{:S(2)}, u32[]{:S(2)}) collective-permute-start(f32[52,8,128]{2,1,0:T(8,128)S(1)} %get-tuple-element.10), channel_id=1, source_target_pairs={{1,2},{2,1},{3,4},{4,3},{5,6},{6,5},{7,8},{8,7},{9,10},{10,9},{11,... | collective-permute-start | bytes 638984 | tf_op jit(solution)/shard_map/ppermute | solution.py:264
  37.6 0.0 copy-start
  37.6 0.0 copy-start.2
  37.6 0.8 %shard_map.57.own_ref = f32[9,264,128]{2,1,0:T(8,128)S(1)} custom-call(f32[16,9,8,128]{3,2,1,0:T(8,128)S(1)} %all-to-all-done.r_ref, bf16[512,384]{1,0:T(8,128)(2,1)S(1)} %pad_maximum_fusion.steer_ref), custom_call_target="tpu_custom_call" | custom-call | flops 1000000000 | bytes 1000000 | tf_op jit(solution)/shard_map/pallas_call | solution.py:227
  38.4 0.0 copy-start.1
  38.5 0.0 collective-permute-done.1.e_ref
  38.5 0.1 copy-done
  38.6 0.0 copy-done.2
  38.7 1.5 %shard_map.58 = (f32[2048,128]{1,0:T(8,128)S(1)}, f32[3,264,128]{2,1,0:T(8,128)S(1)}, f32[264,384]{1,0:T(8,128)S(1)}) custom-call(f32[9,264,128]{2,1,0:T(8,128)S(1)} %shard_map.57.own_ref, f32[16,4,8,128]{3,2,1,0:T(8,128)S(1)} %collective-permute-done.1.e_ref, bf16[512,384]{1,0:T(8,128)(2,1)S(1)} %pad_maximum_fusion.steer_ref, ...), custom_call_target="tpu_custom_call" | custom-call | flops 1000000000 | bytes 1000000 | tf_op jit(solution)/shard_map/pallas_call | solution.py:227
  40.2 6.7 %collective-permute-done.o_ref = f32[52,8,128]{2,1,0:T(8,128)S(1)} collective-permute-done((f32[52,8,128]{2,1,0:T(8,128)S(1)}, f32[52,8,128]{2,1,0:T(8,128)S(1)}, u32[]{:S(2)}, u32[]{:S(2)}) %collective-permute-start) | collective-permute-done | bytes 213024 | tf_op jit(solution)/shard_map/ppermute | solution.py:264
  46.8 0.0 copy-done.1
  46.8 1.8 %shard_map.59 = bf16[256,8,128]{2,1,0:T(8,128)(2,1)} custom-call(f32[52,8,128]{2,1,0:T(8,128)S(1)} %collective-permute-done.o_ref, f32[3,264,128]{2,1,0:T(8,128)S(1)} %get-tuple-element.12.part_ref, f32[264,384]{1,0:T(8,128)S(1)} %get-tuple-element.13.cor_ref, f32[2048,128]{1,0:T(8,128)S(1)} %get-tuple-element.14.flat_ref, ...), custom_call_target="tpu_custom_call" | custom-call | flops 1000000000 | bytes 1000000 | tf_op jit(solution)/shard_map/pallas_call | solution.py:227
  (9 shorter events, 0.2 us)
Async XLA Ops:
  0.0 16.4 %copy-start.3 = (f32[64]{0:T(128)S(1)}, f32[64]{0:T(128)}, u32[]{:S(2)}) copy-start(f32[64]{0:T(128)} %param.6) | copy-start | bytes 772
  2.3 27.9 %all-to-all-start = ((f32[16,9,8,128]{3,2,1,0:T(8,128)}), f32[16,9,8,128]{3,2,1,0:T(8,128)S(1)}, u32[]{:S(2)}, u32[]{:S(2)}) async-start(f32[16,9,8,128]{3,2,1,0:T(8,128)} %shard_map.55), calls=%async_computation | async-start | bytes 1179648 | tf_op jit(solution)/shard_map/all_to_all | solution.py:260
  30.3 8.2 %collective-permute-start.1 = (f32[16,4,8,128]{3,2,1,0:T(8,128)S(1)}, f32[16,4,8,128]{3,2,1,0:T(8,128)S(1)}, u32[]{:S(2)}, u32[]{:S(2)}) collective-permute-start(f32[16,4,8,128]{3,2,1,0:T(8,128)S(1)} %get-tuple-element.11), channel_id=1, source_target_pairs={{0,1},{1,0},{2,3},{3,2},{4,5},{5,4},{6,7},{7,6},{8,9},{9,8},{10,11... | collective-permute-start | bytes 786440 | tf_op jit(solution)/shard_map/ppermute | solution.py:265
  33.2 13.7 %collective-permute-start = (f32[52,8,128]{2,1,0:T(8,128)S(1)}, f32[52,8,128]{2,1,0:T(8,128)S(1)}, u32[]{:S(2)}, u32[]{:S(2)}) collective-permute-start(f32[52,8,128]{2,1,0:T(8,128)S(1)} %get-tuple-element.10), channel_id=1, source_target_pairs={{1,2},{2,1},{3,4},{4,3},{5,6},{6,5},{7,8},{8,7},{9,10},{10,9},{11,... | collective-permute-start | bytes 638984 | tf_op jit(solution)/shard_map/ppermute | solution.py:264
  37.6 1.0 %copy-start = (bf16[256,1024]{1,0:T(8,128)(2,1)S(1)}, bf16[256,1024]{1,0:T(8,128)(2,1)}, u32[]{:S(2)}) copy-start(bf16[256,1024]{1,0:T(8,128)(2,1)} %constant.40.clone.mid_ref) | copy-start | bytes 1572868
  37.6 1.1 %copy-start.2 = (bf16[256,384]{1,0:T(8,128)(2,1)S(1)}, bf16[256,384]{1,0:T(8,128)(2,1)}, u32[]{:S(2)}) copy-start(bf16[256,384]{1,0:T(8,128)(2,1)} %constant.42.clone.me_ref) | copy-start | bytes 589828
  38.4 8.4 %copy-start.1 = (bf16[256,384]{1,0:T(8,128)(2,1)S(1)}, bf16[256,384]{1,0:T(8,128)(2,1)}, u32[]{:S(2)}) copy-start(bf16[256,384]{1,0:T(8,128)(2,1)} %constant.41.clone.mo_ref) | copy-start | bytes 589828

commit v5 on v3

--- a/solution.py
+++ b/solution.py
@@ -18,6 +18,8 @@
 EDGE_LANES = 18
 MERGED = 4
 EDGE_TILES = 48 + 16 // MERGED
+PLACE = [2 * z + y for z in (4, 3, 5, 2, 6, 1, 7, 0) for y in (0, 1)]
+MERGE = [acq % MERGED for acq in PLACE]
 
 
 def parity():
@@ -29,23 +31,22 @@
     odd = parity()
     place = OWN_LANES + EDGE_LANES * lax.rem(lax.axis_index("acq"), MERGED)
     lane = lax.broadcasted_iota(jnp.int32, (8, LANES), 1)
-    halo = [jnp.zeros((8, LANES), jnp.float32) for _ in range(blocks)]
-    for m in range(8):
-        line = m + odd * (7 - 2 * m)
-        for start in (6 * m, place + 6 * m)[: 2 if m < 3 else 1]:
-            left = (lane >= start) & (lane < start + 3)
-            right = (lane >= start + 3) & (lane < start + 6)
-            for j in range(blocks):
-                tile = x_ref[pl.ds(8 * j + line, 8, stride=8 * blocks), :]
-                if isinstance(start, int):
-                    out_ref[blocks - 1 - j, SLOT[m]] = tile
+    zero = jnp.zeros((8, LANES), jnp.float32)
+    halo = [zero, zero]
+    for j in range(blocks):
+        halo.append(zero)
+        for m in range(8):
+            line = m + odd * (7 - 2 * m)
+            tile = x_ref[pl.ds(8 * j + line, 8, stride=8 * blocks), :]
+            out_ref[PLACE.index(j), SLOT[m]] = tile
+            for start in (6 * m, place + 6 * m)[: 2 if m < 3 else 1]:
+                left = (lane >= start) & (lane < start + 3)
+                right = (lane >= start + 3) & (lane < start + 6)
                 moved = pltpu.roll(tile, start + 3, 1)
-                if j + 1 < blocks:
-                    halo[j + 1] = jnp.where(left, moved, halo[j + 1])
-                if j >= 1:
-                    halo[j - 1] = jnp.where(right, moved, halo[j - 1])
+                halo[j + 2] = jnp.where(left, moved, halo[j + 2])
+                halo[j] = jnp.where(right, moved, halo[j])
     for j in range(blocks):
-        out_ref[blocks - 1 - j, HALO] = halo[j]
+        out_ref[PLACE.index(j), HALO] = halo[j + 1]
 
 
 def edge_kernel(r_ref, o_ref, e_ref):
@@ -133,7 +134,7 @@
 def outer_kernel(o_ref, part_ref, cor_ref, flat_ref, steer_ref, mo_ref, out_ref, beams_ref, side_ref, halo_ref, all_ref, edge_ref, done_ref, sems):
     lane = lax.broadcasted_iota(jnp.int32, (8, LANES), 1)
     for j in range(16):
-        start = OWN_LANES + EDGE_LANES * ((15 - j) % MERGED)
+        start = OWN_LANES + EDGE_LANES * MERGE[j]
         halo_ref[j] = jnp.where(lane < EDGE_LANES, pltpu.roll(o_ref[48 + j // MERGED], LANES - start, 1), 0.0)
     lines = o_ref[:48].reshape(16, 3, 8, LANES)
     for s in (0, 2):
@@ -186,10 +187,12 @@
 
 
 def steering(wavenumbers):
-    waves = jnp.broadcast_to(wavenumbers.reshape(16, 1, 4)[::-1], (16, 2, 4)).reshape(LANES)
-    real = (jnp.arange(LANES) // 4) % 2 == 0
-    heights = jnp.arange(HEIGHTS, dtype=jnp.int32).astype(jnp.float32) - jnp.float32(HEIGHTS // 2)
-    phases = heights[:, None] * waves[None, :]
+    source = np.array([4 * acq + k for acq in PLACE for _ in range(2) for k in range(4)])
+    chosen = np.arange(len(source) // 2)[:, None] == source[None, :]
+    waves = jnp.sum(jnp.where(chosen, wavenumbers[:, None], 0.0), axis=0)
+    real = (np.arange(LANES) // 4) % 2 == 0
+    heights = np.arange(HEIGHTS, dtype=np.float32) - np.float32(HEIGHTS // 2)
+    phases = jnp.asarray(heights)[:, None] * waves[None, :]
     cosine, sine = jnp.cos(phases), jnp.sin(phases)
     full = jnp.concatenate([jnp.where(real, cosine, sine), jnp.where(real, -sine, cosine)], axis=0)
     high = lax.reduce_precision(full, 8, 7)
@@ -218,16 +221,17 @@
 
 
 def spectrum(slc_stack, wavenumbers):
-    lines, acqs = lax.axis_size("line"), lax.axis_size("acq")
+    lines = lax.axis_size("line")
     outer = [pair for i in range(1, lines - 1, 2) for pair in ((i, i + 1), (i + 1, i))]
     inner = [pair for i in range(0, lines, 2) for pair in ((i, i + 1), (i + 1, i))]
     beams = pltpu.VMEM((2 * HEIGHTS, 2 * LANES), jnp.float32)
     stack = slc_stack.reshape(8, 8, -1, LANES).transpose(0, 2, 1, 3).reshape(-1, LANES)
-    (packed,) = call(pack_kernel, [(16, 9, 8, LANES)], 4, 1000000)(stack)
-    gathered = lax.all_to_all(packed, "acq", 0, 0, tiled=True, axis_index_groups=[list(range(acqs))[::-1]])
-    steer = steering(wavenumbers)
+    (packed,) = call(pack_kernel, [(16, 9, 8, LANES)], 2, 1000000)(stack)
+    gathered = lax.all_to_all(packed, "acq", 0, 0, tiled=True, axis_index_groups=[PLACE])
     mid, mo, me = spread()
     to_o, to_e = call(edge_kernel, [(EDGE_TILES, 8, LANES), (16, 4, 8, LANES)], 4, 1000000)(gathered)
+    to_o, to_e, wavenumbers = lax.optimization_barrier((to_o, to_e, wavenumbers))
+    steer = steering(wavenumbers)
     side_o = lax.ppermute(to_o, "line", outer)
     side_e = lax.ppermute(to_e, "line", inner)
     (own,) = call(own_kernel, [(9, ROWS, LANES)], 10, 1000000000, [beams])(gathered, steer)

time: 48.9 us -> 44.8 us (0.916)
  blocking collectives: 0 us -> 27.5 us
  waiting for transfers between devices: 19.5 us -> 2.93 us
  starting transfers between devices: 21.4 us -> 7.35 us
  Pallas kernels: 5.47 us -> 4.63 us
    all_to_all x0 -> x1, blocking collectives: none -> 27.5 us  [spectrum(): lax.all_to_all(packed, 'acq', 0, 0, tiled=True, axis_index_groups=[PLACE])]
    all_to_all x1 -> x0, starting transfers between devices: 13.2 us -> none  [spectrum(): lax.all_to_all(packed, 'acq', 0, 0, tiled=True, axis_index_groups=[list(r...]
    all_to_all x1 -> x0, waiting for transfers between devices: 13 us -> none  [spectrum(): lax.all_to_all(packed, 'acq', 0, 0, tiled=True, axis_index_groups=[list(r...]
    ppermute x1, waiting for transfers between devices: 6.5 us -> 2.93 us  [spectrum(): side_o = lax.ppermute(to_o, 'line', outer)]
    ppermute x1, starting transfers between devices: 3.79 us -> 1.92 us  [spectrum(): side_e = lax.ppermute(to_e, 'line', inner)]
    ppermute x1, starting transfers between devices: 4.34 us -> 5.43 us  [spectrum(): side_o = lax.ppermute(to_o, 'line', outer)]
    pallas_call x5, Pallas kernels: 5.47 us -> 4.63 us  [on(): pl.pallas_call(kernel, out_shape=[jax.ShapeDtypeStruct(shape, dtype) for...]
    unnamed x10 -> x16, local copies, waits for them, and re-layouts: 1.25 us -> 1.25 us
  transfers between devices with their start and end apart: 3 -> 2, of which waited for: 2 -> 1; matrix products, arithmetic and copies ran while one was open for 2% -> 2% of each run, Pallas kernels for 5% -> 5%
where the time goes in v5:
time: 44.8 us; the launch traced here: 44.5 us
  blocking collectives  27.5 us (61%)
  starting transfers between devices  7.35 us (16%)
  Pallas kernels  4.63 us (10%)
  waiting for transfers between devices  2.93 us (7%)
  local copies, waits for them, and re-layouts  1.25 us (3%)
  other arithmetic  0.73 us (2%)
    all_to_all x1, blocking collectives, spectrum(): lax.all_to_all(packed, 'acq', 0, 0, tiled=True, axis_index_groups=[PLACE])  27.5 us
    ppermute x1, starting transfers between devices, spectrum(): side_o = lax.ppermute(to_o, 'line', outer)  5.43 us
    pallas_call x5, Pallas kernels, on(): pl.pallas_call(kernel, out_shape=[jax.ShapeDtypeStruct(shape, dtype) for...  4.63 us
    ppermute x1, waiting for transfers between devices, spectrum(): side_o = lax.ppermute(to_o, 'line', outer)  2.93 us
    ppermute x1, starting transfers between devices, spectrum(): side_e = lax.ppermute(to_e, 'line', inner)  1.92 us
    unnamed x16, local copies, waits for them, and re-layouts  1.25 us
  transfers between devices with their start and end apart: 2, of which 1 were waited for; matrix products, arithmetic and copies ran while one was open for 2% of the time, Pallas kernels for 5%

profile of v5, /device:TPU:23, one launch (start us, length us, event | category | flops | bytes accessed | tf_op | source)
XLA Modules:
  0.0 44.5 jit_solution(5892829805287466083)
XLA Ops:
  0.0 0.0 copy-start
  0.0 1.0 %copy-done = f32[2,4,8,2048]{3,2,1,0:T(8,128)S(1)} copy-done((f32[2,4,8,2048]{3,2,1,0:T(8,128)S(1)}, f32[2,4,8,2048]{3,2,1,0:T(8,128)}, u32[]{:S(2)}) %copy-start) | copy-done | bytes 524312
  1.0 0.0 copy-start.4
  1.0 0.0 copy-start.7
  1.0 0.0 copy-start.5
  1.0 0.0 copy-start.6
  1.1 0.4 shard_map.82
  1.4 27.5 %all_to_all.5.r_ref = f32[16,9,8,128]{3,2,1,0:T(8,128)S(1)} all-to-all(f32[16,9,8,128]{3,2,1,0:T(8,128)S(1)} %shard_map.82), channel_id=1, replica_groups={{256,288,192,224,320,352,128,160,384,416,64,96,448,480,0,32},{257,289,1..., dimensions={0} | all-to-all | bytes 1179648 | tf_op jit(solution)/shard_map/all_to_all | solution.py:230
  29.0 5.4 %collective-permute-start = (f32[52,8,128]{2,1,0:T(8,128)S(1)}, f32[52,8,128]{2,1,0:T(8,128)S(1)}, u32[]{:S(2)}, u32[]{:S(2)}) collective-permute-start(f32[52,8,128]{2,1,0:T(8,128)S(1)} %get-tuple-element.15), channel_id=1, source_target_pairs={{1,2},{2,1},{3,4},{4,3},{5,6},{6,5},{7,8},{8,7},{9,10},{10,9},{11,... | collective-permute-start | bytes 638984 | tf_op jit(solution)/shard_map/ppermute | solution.py:235
  34.4 1.9 %collective-permute-start.1 = (f32[16,4,8,128]{3,2,1,0:T(8,128)S(1)}, f32[16,4,8,128]{3,2,1,0:T(8,128)S(1)}, u32[]{:S(2)}, u32[]{:S(2)}) collective-permute-start(f32[16,4,8,128]{3,2,1,0:T(8,128)S(1)} %get-tuple-element.17), channel_id=1, source_target_pairs={{0,1},{1,0},{2,3},{3,2},{4,5},{5,4},{6,7},{7,6},{8,9},{9,8},{10,11... | collective-permute-start | bytes 786440 | tf_op jit(solution)/shard_map/ppermute | solution.py:236
  36.3 0.0 copy-done.4
  36.4 0.0 copy-done.7
  36.4 0.1 select_reduce_fusion
  36.5 0.0 copy-done.5
  36.5 0.0 copy-done.6
  36.5 0.5 %fusion.2 = (f32[256,128]{1,0:T(8,128)S(1)}, f32[256,128]{1,0:T(8,128)S(1)}) fusion(f32[128]{0:T(128)S(1)} %select_reduce_fusion, f32[256]{0:T(256)S(1)} %copy-done.5, pred[128]{0:T(512)(128)(4,1)S(1)} %copy-done.6), kind=kLoop, calls=%fused_computation.8 | loop fusion | flops 131072 | bytes 263808 | tf_op jit(solution)/shard_map/jit(_where)/select_n | solution.py:197
  37.1 0.0 copy-start.1
  37.1 0.0 copy-start.3
  37.2 0.8 %shard_map.84.own_ref = f32[9,264,128]{2,1,0:T(8,128)S(1)} custom-call(f32[16,9,8,128]{3,2,1,0:T(8,128)S(1)} %all_to_all.5.r_ref, bf16[512,384]{1,0:T(8,128)(2,1)S(1)} %pad_maximum_fusion.steer_ref), custom_call_target="tpu_custom_call" | custom-call | flops 1000000000 | bytes 1000000 | tf_op jit(solution)/shard_map/pallas_call | solution.py:210
  38.0 0.0 copy-start.2
  38.0 0.0 collective-permute-done.1.e_ref
  38.0 0.1 copy-done.1
  38.2 0.0 copy-done.3
  38.2 1.5 %shard_map.85 = (f32[2048,128]{1,0:T(8,128)S(1)}, f32[3,264,128]{2,1,0:T(8,128)S(1)}, f32[264,384]{1,0:T(8,128)S(1)}) custom-call(f32[9,264,128]{2,1,0:T(8,128)S(1)} %shard_map.84.own_ref, f32[16,4,8,128]{3,2,1,0:T(8,128)S(1)} %collective-permute-done.1.e_ref, bf16[512,384]{1,0:T(8,128)(2,1)S(1)} %pad_maximum_fusion.steer_ref, ...), custom_call_target="tpu_custom_call" | custom-call | flops 1000000000 | bytes 1000000 | tf_op jit(solution)/shard_map/pallas_call | solution.py:210
  39.7 2.9 %collective-permute-done.o_ref = f32[52,8,128]{2,1,0:T(8,128)S(1)} collective-permute-done((f32[52,8,128]{2,1,0:T(8,128)S(1)}, f32[52,8,128]{2,1,0:T(8,128)S(1)}, u32[]{:S(2)}, u32[]{:S(2)}) %collective-permute-start) | collective-permute-done | bytes 213024 | tf_op jit(solution)/shard_map/ppermute | solution.py:235
  42.6 0.0 copy-done.2
  42.6 1.9 %shard_map.86 = bf16[256,8,128]{2,1,0:T(8,128)(2,1)} custom-call(f32[52,8,128]{2,1,0:T(8,128)S(1)} %collective-permute-done.o_ref, f32[3,264,128]{2,1,0:T(8,128)S(1)} %get-tuple-element.18.part_ref, f32[264,384]{1,0:T(8,128)S(1)} %get-tuple-element.19.cor_ref, f32[2048,128]{1,0:T(8,128)S(1)} %get-tuple-element.20.flat_ref, ...), custom_call_target="tpu_custom_call" | custom-call | flops 1000000000 | bytes 1000000 | tf_op jit(solution)/shard_map/pallas_call | solution.py:210
  (3 shorter events, 0.1 us)
Async XLA Ops:
  0.0 1.0 %copy-start = (f32[2,4,8,2048]{3,2,1,0:T(8,128)S(1)}, f32[2,4,8,2048]{3,2,1,0:T(8,128)}, u32[]{:S(2)}) copy-start(f32[2,4,8,2048]{3,2,1,0:T(8,128)} %param.8) | copy-start | bytes 1572868
  1.0 35.3 %copy-start.4 = (pred[64,128]{1,0:T(32,128)(4,1)S(1)}, pred[64,128]{1,0:T(32,128)(4,1)}, u32[]{:S(2)}) copy-start(pred[64,128]{1,0:T(32,128)(4,1)} %constant.17.clone) | copy-start | bytes 24580
  1.0 35.3 %copy-start.7 = (f32[64]{0:T(128)S(1)}, f32[64]{0:T(128)}, u32[]{:S(2)}) copy-start(f32[64]{0:T(128)} %param.9) | copy-start | bytes 772
  1.0 35.4 %copy-start.5 = (f32[256]{0:T(256)S(1)}, f32[256]{0:T(256)}, u32[]{:S(2)}) copy-start(f32[256]{0:T(256)} %constant.18.clone) | copy-start | bytes 3076
  1.0 35.4 %copy-start.6 = (pred[128]{0:T(512)(128)(4,1)S(1)}, pred[128]{0:T(512)(128)(4,1)}, u32[]{:S(2)}) copy-start(pred[128]{0:T(512)(128)(4,1)} %constant.19.clone) | copy-start | bytes 388
  29.0 13.7 %collective-permute-start = (f32[52,8,128]{2,1,0:T(8,128)S(1)}, f32[52,8,128]{2,1,0:T(8,128)S(1)}, u32[]{:S(2)}, u32[]{:S(2)}) collective-permute-start(f32[52,8,128]{2,1,0:T(8,128)S(1)} %get-tuple-element.15), channel_id=1, source_target_pairs={{1,2},{2,1},{3,4},{4,3},{5,6},{6,5},{7,8},{8,7},{9,10},{10,9},{11,... | collective-permute-start | bytes 638984 | tf_op jit(solution)/shard_map/ppermute | solution.py:235
  34.4 3.6 %collective-permute-start.1 = (f32[16,4,8,128]{3,2,1,0:T(8,128)S(1)}, f32[16,4,8,128]{3,2,1,0:T(8,128)S(1)}, u32[]{:S(2)}, u32[]{:S(2)}) collective-permute-start(f32[16,4,8,128]{3,2,1,0:T(8,128)S(1)} %get-tuple-element.17), channel_id=1, source_target_pairs={{0,1},{1,0},{2,3},{3,2},{4,5},{5,4},{6,7},{7,6},{8,9},{9,8},{10,11... | collective-permute-start | bytes 786440 | tf_op jit(solution)/shard_map/ppermute | solution.py:236
  37.1 1.0 %copy-start.1 = (bf16[256,1024]{1,0:T(8,128)(2,1)S(1)}, bf16[256,1024]{1,0:T(8,128)(2,1)}, u32[]{:S(2)}) copy-start(bf16[256,1024]{1,0:T(8,128)(2,1)} %constant.14.clone.mid_ref) | copy-start | bytes 1572868
  37.1 1.1 %copy-start.3 = (bf16[256,384]{1,0:T(8,128)(2,1)S(1)}, bf16[256,384]{1,0:T(8,128)(2,1)}, u32[]{:S(2)}) copy-start(bf16[256,384]{1,0:T(8,128)(2,1)} %constant.16.clone.me_ref) | copy-start | bytes 589828
  38.0 4.6 %copy-start.2 = (bf16[256,384]{1,0:T(8,128)(2,1)S(1)}, bf16[256,384]{1,0:T(8,128)(2,1)}, u32[]{:S(2)}) copy-start(bf16[256,384]{1,0:T(8,128)(2,1)} %constant.15.clone.mo_ref) | copy-start | bytes 589828

commit v6 on v5

--- a/solution.py
+++ b/solution.py
@@ -12,14 +12,15 @@
 LANES = 128
 epsilon = 1e-06
 
+ROW = {0: 0, 1: 8, 2: 16, 7: 28, 6: 36, 5: 44, 3: 52, 4: 60}
+HALO_ROW = 24
+BLOCK = 68
 SLOT = {0: 0, 1: 1, 2: 2, 7: 4, 6: 5, 5: 6, 3: 7, 4: 8}
 HALO = 3
-OWN_LANES = 48
 EDGE_LANES = 18
-MERGED = 4
-EDGE_TILES = 48 + 16 // MERGED
+MERGED = 7
+EDGE_TILES = 48 + 3
 PLACE = [2 * z + y for z in (4, 3, 5, 2, 6, 1, 7, 0) for y in (0, 1)]
-MERGE = [acq % MERGED for acq in PLACE]
 
 
 def parity():
@@ -29,7 +30,6 @@
 def pack_kernel(x_ref, out_ref):
     blocks = x_ref.shape[0] // 64
     odd = parity()
-    place = OWN_LANES + EDGE_LANES * lax.rem(lax.axis_index("acq"), MERGED)
     lane = lax.broadcasted_iota(jnp.int32, (8, LANES), 1)
     zero = jnp.zeros((8, LANES), jnp.float32)
     halo = [zero, zero]
@@ -38,29 +38,49 @@
         for m in range(8):
             line = m + odd * (7 - 2 * m)
             tile = x_ref[pl.ds(8 * j + line, 8, stride=8 * blocks), :]
-            out_ref[PLACE.index(j), SLOT[m]] = tile
-            for start in (6 * m, place + 6 * m)[: 2 if m < 3 else 1]:
-                left = (lane >= start) & (lane < start + 3)
-                right = (lane >= start + 3) & (lane < start + 6)
-                moved = pltpu.roll(tile, start + 3, 1)
-                halo[j + 2] = jnp.where(left, moved, halo[j + 2])
-                halo[j] = jnp.where(right, moved, halo[j])
+            out_ref[pl.ds(BLOCK * PLACE.index(j) + ROW[m], 8), :] = tile
+            left = (lane >= 6 * m) & (lane < 6 * m + 3)
+            right = (lane >= 6 * m + 3) & (lane < 6 * m + 6)
+            moved = pltpu.roll(tile, 6 * m + 3, 1)
+            halo[j + 2] = jnp.where(left, moved, halo[j + 2])
+            halo[j] = jnp.where(right, moved, halo[j])
     for j in range(blocks):
-        out_ref[PLACE.index(j), HALO] = halo[j + 1]
-
-
-def edge_kernel(r_ref, o_ref, e_ref):
+        tile = halo[j + 1]
+        tile = tile + pltpu.roll(pltpu.roll(tile, 4, 0), LANES // 2, 1)
+        out_ref[pl.ds(BLOCK * PLACE.index(j) + HALO_ROW, 4), :] = tile[:4]
+
+
+def edge_kernel(r_ref, o_ref, e_ref, halo_ref):
+    lane = lax.broadcasted_iota(jnp.int32, (8, LANES), 1)
+    sub = lax.broadcasted_iota(jnp.int32, (8, LANES), 0)
+    for g in range(3):
+        sums = [jnp.zeros((8, LANES), jnp.float32) for _ in range(2)]
+        for i in range(min(MERGED, 16 - MERGED * g)):
+            j = MERGED * g + i
+            tile = r_ref[pl.ds(BLOCK * j + HALO_ROW, 8), :]
+            tile = jnp.where(sub < 4, tile, pltpu.roll(pltpu.roll(tile, 4, 0), LANES // 2, 1))
+            tile = jnp.where(lane < 48, tile, 0.0)
+            halo_ref[j] = tile
+            here = (lane >= EDGE_LANES * i) & (lane < EDGE_LANES * (i + 1))
+            for k, start in enumerate((0, 30)):
+                sums[k] = jnp.where(here, pltpu.roll(tile, (EDGE_LANES * i - start) % LANES, 1), sums[k])
+            for k, ref in enumerate((o_ref, e_ref)):
+                for s in range(3):
+                    ref[3 * j + s] = r_ref[pl.ds(BLOCK * j + (0, 28)[k] + 8 * s, 8), :]
+        o_ref[48 + g] = sums[0]
+        e_ref[48 + g] = sums[1]
+
+
+def side_beams(ref, steer_ref, beams_ref, halo_ref, side_ref):
     lane = lax.broadcasted_iota(jnp.int32, (8, LANES), 1)
     for j in range(16):
-        for s in range(3):
-            o_ref[3 * j + s] = r_ref[j, s]
-        for s in range(4):
-            e_ref[j, s] = r_ref[j, HALO + s]
-    for g in range(16 // MERGED):
-        total = r_ref[MERGED * g, HALO]
-        for j in range(1, MERGED):
-            total = total + r_ref[MERGED * g + j, HALO]
-        o_ref[48 + g] = jnp.where(lane < OWN_LANES, 0.0, total)
+        tile = pltpu.roll(ref[48 + j // MERGED], -EDGE_LANES * (j % MERGED) % LANES, 1)
+        halo_ref[j] = jnp.where(lane < EDGE_LANES, tile, 0.0)
+    lines = ref[:48].reshape(16, 3, 8, LANES)
+    for s in (0, 2):
+        both = beam_pair(lines[:, s], lines[:, 1] if s == 0 else halo_ref[...], steer_ref, beams_ref)
+        side_ref[s] = both[:, :LANES]
+        side_ref[s + 1] = both[:, LANES:]
 
 
 def beam_pair(first, second, steer_ref, beams_ref):
@@ -75,10 +95,16 @@
     return jnp.concatenate([power, squares], axis=0)
 
 
-def own_kernel(r_ref, steer_ref, out_ref, beams_ref):
+def own_kernel(r_ref, halo_ref, steer_ref, out_ref, beams_ref):
+    def block(s):
+        if s == HALO:
+            return halo_ref[...]
+        (m,) = [m for m in SLOT if SLOT[m] == s]
+        return jnp.concatenate([r_ref[pl.ds(BLOCK * j + ROW[m], 8), :] for j in range(16)], axis=0)
+
     for s in (0, 2, 4, 6, 8):
         t = min(s + 1, 8)
-        both = beam_pair(r_ref[:, s], r_ref[:, t], steer_ref, beams_ref)
+        both = beam_pair(block(s), block(t), steer_ref, beams_ref)
         out_ref[s] = both[:, :LANES]
         if t != s:
             out_ref[t] = both[:, LANES:]
@@ -107,19 +133,16 @@
         flat_ref[pl.ds(8 * k + line, 64, stride=8), :] = box_of(m, slice(k, k + 64)) * inverse
 
 
-def inner_kernel(own_ref, e_ref, steer_ref, mid_ref, me_ref, flat_ref, part_ref, cor_ref, beams_ref, side_ref, all_ref):
-    for s in (0, 2):
-        both = beam_pair(e_ref[:, s], e_ref[:, s + 1], steer_ref, beams_ref)
-        side_ref[s] = both[:, :LANES]
-        side_ref[s + 1] = both[:, LANES:]
+def inner_kernel(own_ref, e_ref, steer_ref, mid_ref, me_ref, flat_ref, part_ref, cor_ref, beams_ref, halo_ref, side_ref, all_ref):
+    side_beams(e_ref, steer_ref, beams_ref, halo_ref, side_ref)
     all_ref[...] = jnp.dot(halves(own_ref[HALO]), mid_ref[...], preferred_element_type=jnp.float32)
-    all_ref[:, 5 * LANES :] += jnp.dot(halves(side_ref[0]), me_ref[...], preferred_element_type=jnp.float32)
+    all_ref[:, 5 * LANES :] += jnp.dot(halves(side_ref[3]), me_ref[...], preferred_element_type=jnp.float32)
     cor_ref[...] = all_ref[:, : 3 * LANES]
 
     def summed(m, rows):
         total = None
         for position in range(max(m - 3, 0), m + 4):
-            term = side_ref[position - 7, rows] if position > 7 else own_ref[SLOT[position], rows]
+            term = side_ref[position - 8, rows] if position > 7 else own_ref[SLOT[position], rows]
             total = term if total is None else total + term
         return total
 
@@ -131,16 +154,8 @@
         normalize(m, odd, lambda m, rows: boxed(summed(m, rows), all_ref[rows, m * LANES : (m + 1) * LANES]), flat_ref)
 
 
-def outer_kernel(o_ref, part_ref, cor_ref, flat_ref, steer_ref, mo_ref, out_ref, beams_ref, side_ref, halo_ref, all_ref, edge_ref, done_ref, sems):
-    lane = lax.broadcasted_iota(jnp.int32, (8, LANES), 1)
-    for j in range(16):
-        start = OWN_LANES + EDGE_LANES * MERGE[j]
-        halo_ref[j] = jnp.where(lane < EDGE_LANES, pltpu.roll(o_ref[48 + j // MERGED], LANES - start, 1), 0.0)
-    lines = o_ref[:48].reshape(16, 3, 8, LANES)
-    for s in (0, 2):
-        both = beam_pair(lines[:, s], lines[:, 1] if s == 0 else halo_ref[...], steer_ref, beams_ref)
-        side_ref[s] = both[:, :LANES]
-        side_ref[s + 1] = both[:, LANES:]
+def outer_kernel(o_ref, part_ref, cor_ref, flat_ref, steer_ref, mo_ref, out_ref, beams_ref, halo_ref, side_ref, all_ref, edge_ref, done_ref, sems):
+    side_beams(o_ref, steer_ref, beams_ref, halo_ref, side_ref)
     all_ref[...] = cor_ref[...] + jnp.dot(halves(side_ref[3]), mo_ref[...], preferred_element_type=jnp.float32)
 
     def box_of(m, rows):
@@ -171,18 +186,18 @@
     column = np.array([-3, -2, -1, 128, 129, 130])
     near = np.abs(column[:, None] - np.arange(LANES)[None, :]) <= 3
 
-    def matrix(position_of, lines, used):
+    def matrix(position_of, lines, used, first=0):
         full = np.zeros((LANES, len(lines), LANES), np.float32)
         for n in used:
             for i, m in enumerate(lines):
                 if abs(position_of(n) - m) <= 3:
-                    full[6 * n : 6 * n + 6, i] = near
+                    full[6 * (n - first) : 6 * (n - first) + 6, i] = near
         full = full.reshape(LANES, -1)
         return jnp.asarray(np.concatenate([full, full], axis=0), jnp.bfloat16)
 
     mid = matrix(lambda n: n, range(8), range(8))
     mo = matrix(lambda n: -1 - n, (0, 1, 2), (0, 1, 2))
-    me = matrix(lambda n: 15 - n, (5, 6, 7), (5, 6, 7))
+    me = matrix(lambda n: 15 - n, (5, 6, 7), (5, 6, 7), 5)
     return mid, mo, me
 
 
@@ -225,22 +240,27 @@
     outer = [pair for i in range(1, lines - 1, 2) for pair in ((i, i + 1), (i + 1, i))]
     inner = [pair for i in range(0, lines, 2) for pair in ((i, i + 1), (i + 1, i))]
     beams = pltpu.VMEM((2 * HEIGHTS, 2 * LANES), jnp.float32)
+    strip = pltpu.VMEM((16, 8, LANES), jnp.float32)
+    quad = pltpu.VMEM((4, ROWS, LANES), jnp.float32)
     stack = slc_stack.reshape(8, 8, -1, LANES).transpose(0, 2, 1, 3).reshape(-1, LANES)
-    (packed,) = call(pack_kernel, [(16, 9, 8, LANES)], 2, 1000000)(stack)
+    (packed,) = call(pack_kernel, [(16 * BLOCK, LANES)], 2, 1000000)(stack)
+    packed = packed.reshape(16, BLOCK, 1, LANES)
     gathered = lax.all_to_all(packed, "acq", 0, 0, tiled=True, axis_index_groups=[PLACE])
+    gathered = gathered.reshape(16 * BLOCK, LANES)
+    sides = (EDGE_TILES, 8, LANES)
+    to_o, to_e, halo = call(edge_kernel, [sides, sides, (16, 8, LANES)], 4, 1000000)(gathered)
     mid, mo, me = spread()
-    to_o, to_e = call(edge_kernel, [(EDGE_TILES, 8, LANES), (16, 4, 8, LANES)], 4, 1000000)(gathered)
     to_o, to_e, wavenumbers = lax.optimization_barrier((to_o, to_e, wavenumbers))
     steer = steering(wavenumbers)
     side_o = lax.ppermute(to_o, "line", outer)
     side_e = lax.ppermute(to_e, "line", inner)
-    (own,) = call(own_kernel, [(9, ROWS, LANES)], 10, 1000000000, [beams])(gathered, steer)
+    (own,) = call(own_kernel, [(9, ROWS, LANES)], 10, 1000000000, [beams])(gathered, halo, steer)
     flat, part, cor = call(
         inner_kernel,
         [(8 * HEIGHTS, LANES), (3, ROWS, LANES), (ROWS, 3 * LANES)],
         14,
         1000000000,
-        [beams, pltpu.VMEM((4, ROWS, LANES), jnp.float32), pltpu.VMEM((ROWS, 8 * LANES), jnp.float32)],
+        [beams, strip, quad, pltpu.VMEM((ROWS, 8 * LANES), jnp.float32)],
     )(own, side_e, steer, mid, me)
     (result,) = call(
         outer_kernel,
@@ -249,8 +269,8 @@
         1000000000,
         [
             beams,
-            pltpu.VMEM((4, ROWS, LANES), jnp.float32),
-            pltpu.VMEM((16, 8, LANES), jnp.float32),
+            strip,
+            quad,
             pltpu.VMEM((ROWS, 3 * LANES), jnp.float32),
             pltpu.VMEM((8 * HEIGHTS, LANES), jnp.float32),
             pltpu.VMEM((HEIGHTS, 8, LANES), jnp.bfloat16),

time: 44.8 us -> 44.2 us (0.987)
  blocking collectives: 27.5 us -> 26.9 us
    all_to_all x1, blocking collectives: 27.5 us -> 26.9 us  [spectrum(): lax.all_to_all(packed, 'acq', 0, 0, tiled=True, axis_index_groups=[PLACE])]
where the time goes in v6:
time: 44.2 us; the launch traced here: 44 us
  blocking collectives  26.9 us (61%)
  starting transfers between devices  7.25 us (16%)
  Pallas kernels  4.78 us (11%)
  waiting for transfers between devices  3 us (7%)
  local copies, waits for them, and re-layouts  1.26 us (3%)
  other arithmetic  0.73 us (2%)
    all_to_all x1, blocking collectives, spectrum(): lax.all_to_all(packed, 'acq', 0, 0, tiled=True, axis_index_groups=[PLACE])  26.9 us
    ppermute x1, starting transfers between devices, spectrum(): side_o = lax.ppermute(to_o, 'line', outer)  5.33 us
    pallas_call x5, Pallas kernels, on(): pl.pallas_call(kernel, out_shape=[jax.ShapeDtypeStruct(shape, dtype) for...  4.78 us
    ppermute x1, waiting for transfers between devices, spectrum(): side_o = lax.ppermute(to_o, 'line', outer)  2.99 us
    ppermute x1, starting transfers between devices, spectrum(): side_e = lax.ppermute(to_e, 'line', inner)  1.92 us
    unnamed x16, local copies, waits for them, and re-layouts  1.26 us
  transfers between devices with their start and end apart: 2, of which 1 were waited for; matrix products, arithmetic and copies ran while one was open for 2% of the time, Pallas kernels for 5%

profile of v6, /device:TPU:23, one launch (start us, length us, event | category | flops | bytes accessed | tf_op | source)
XLA Modules:
  0.0 44.0 jit_solution(11853081033007329149)
XLA Ops:
  0.0 0.0 copy-start
  0.0 1.0 %copy-done = f32[2,4,8,2048]{3,2,1,0:T(8,128)S(1)} copy-done((f32[2,4,8,2048]{3,2,1,0:T(8,128)S(1)}, f32[2,4,8,2048]{3,2,1,0:T(8,128)}, u32[]{:S(2)}) %copy-start) | copy-done | bytes 524312
  1.0 0.0 copy-start.4
  1.0 0.0 copy-start.7
  1.0 0.0 copy-start.5
  1.0 0.0 copy-start.6
  1.1 0.5 %shard_map.82 = f32[1088,128]{1,0:T(8,128)S(1)} custom-call(f32[1024,128]{1,0:T(8,128)S(1)} %bitcast.10), custom_call_target="tpu_custom_call" | custom-call | flops 1000000 | bytes 1000000 | tf_op jit(solution)/shard_map/pallas_call | solution.py:225
  1.5 26.9 %all_to_all.5 = f32[16,68,1,128]{3,2,1,0:T(1,128)S(1)} all-to-all(f32[16,68,1,128]{3,2,1,0:T(1,128)S(1)} %bitcast.9), channel_id=1, replica_groups={{256,288,192,224,320,352,128,160,384,416,64,96,448,480,0,32},{257,289,1..., dimensions={0} | all-to-all | bytes 1114112 | tf_op jit(solution)/shard_map/all_to_all | solution.py:248
  28.4 0.2 shard_map.83
  28.6 5.3 %collective-permute-start = (f32[51,8,128]{2,1,0:T(8,128)S(1)}, f32[51,8,128]{2,1,0:T(8,128)S(1)}, u32[]{:S(2)}, u32[]{:S(2)}) collective-permute-start(f32[51,8,128]{2,1,0:T(8,128)S(1)} %get-tuple-element.16), channel_id=1, source_target_pairs={{1,2},{2,1},{3,4},{4,3},{5,6},{6,5},{7,8},{8,7},{9,10},{10,9},{11,... | collective-permute-start | bytes 626696 | tf_op jit(solution)/shard_map/ppermute | solution.py:255
  33.9 1.9 %collective-permute-start.1 = (f32[51,8,128]{2,1,0:T(8,128)S(1)}, f32[51,8,128]{2,1,0:T(8,128)S(1)}, u32[]{:S(2)}, u32[]{:S(2)}) collective-permute-start(f32[51,8,128]{2,1,0:T(8,128)S(1)} %get-tuple-element.19), channel_id=1, source_target_pairs={{0,1},{1,0},{2,3},{3,2},{4,5},{5,4},{6,7},{7,6},{8,9},{9,8},{10,11... | collective-permute-start | bytes 626696 | tf_op jit(solution)/shard_map/ppermute | solution.py:256
  35.8 0.0 copy-done.4
  35.8 0.0 copy-done.7
  35.9 0.1 select_reduce_fusion
  35.9 0.0 copy-done.5
  35.9 0.0 copy-done.6
  36.0 0.5 %fusion.2 = (f32[256,128]{1,0:T(8,128)S(1)}, f32[256,128]{1,0:T(8,128)S(1)}) fusion(f32[128]{0:T(128)S(1)} %select_reduce_fusion, f32[256]{0:T(256)S(1)} %copy-done.5, pred[128]{0:T(512)(128)(4,1)S(1)} %copy-done.6), kind=kLoop, calls=%fused_computation.8 | loop fusion | flops 131072 | bytes 263808 | tf_op jit(solution)/shard_map/jit(_where)/select_n | solution.py:212
  36.6 0.0 copy-start.1
  36.6 0.0 copy-start.3
  36.6 0.8 %shard_map.84.own_ref = f32[9,264,128]{2,1,0:T(8,128)S(1)} custom-call(f32[1088,128]{1,0:T(8,128)S(1)} %bitcast.8, f32[16,8,128]{2,1,0:T(8,128)S(1)} %get-tuple-element.17.halo_ref, bf16[512,384]{1,0:T(8,128)(2,1)S(1)} %pad_maximum_fusion.steer_ref), custom_call_target="tpu_custom_call" | custom-call | flops 1000000000 | bytes 1000000 | tf_op jit(solution)/shard_map/pallas_call | solution.py:225
  37.5 0.0 copy-start.2
  37.5 0.0 collective-permute-done.1.e_ref
  37.5 0.1 copy-done.1
  37.7 0.0 copy-done.3
  37.7 1.4 %shard_map.85 = (f32[2048,128]{1,0:T(8,128)S(1)}, f32[3,264,128]{2,1,0:T(8,128)S(1)}, f32[264,384]{1,0:T(8,128)S(1)}) custom-call(f32[9,264,128]{2,1,0:T(8,128)S(1)} %shard_map.84.own_ref, f32[51,8,128]{2,1,0:T(8,128)S(1)} %collective-permute-done.1.e_ref, bf16[512,384]{1,0:T(8,128)(2,1)S(1)} %pad_maximum_fusion.steer_ref, bf16[256,1024]{1,0:T(8,128)(2,1)S(1)} %copy-done.1, ...), custom_call_target="tpu_custom_call" | custom-call | flops 1000000000 | bytes 1000000 | tf_op jit(solution)/shard_map/pallas_call | solution.py:225
  39.1 3.0 %collective-permute-done.o_ref = f32[51,8,128]{2,1,0:T(8,128)S(1)} collective-permute-done((f32[51,8,128]{2,1,0:T(8,128)S(1)}, f32[51,8,128]{2,1,0:T(8,128)S(1)}, u32[]{:S(2)}, u32[]{:S(2)}) %collective-permute-start) | collective-permute-done | bytes 208928 | tf_op jit(solution)/shard_map/ppermute | solution.py:255
  42.1 0.0 copy-done.2
  42.1 1.9 %shard_map.86 = bf16[256,8,128]{2,1,0:T(8,128)(2,1)} custom-call(f32[51,8,128]{2,1,0:T(8,128)S(1)} %collective-permute-done.o_ref, f32[3,264,128]{2,1,0:T(8,128)S(1)} %get-tuple-element.20.part_ref, f32[264,384]{1,0:T(8,128)S(1)} %get-tuple-element.21.cor_ref, f32[2048,128]{1,0:T(8,128)S(1)} %get-tuple-element.22.flat_ref, ...), custom_call_target="tpu_custom_call" | custom-call | flops 1000000000 | bytes 1000000 | tf_op jit(solution)/shard_map/pallas_call | solution.py:225
  (2 shorter events, 0.1 us)
Async XLA Ops:
  0.0 1.0 %copy-start = (f32[2,4,8,2048]{3,2,1,0:T(8,128)S(1)}, f32[2,4,8,2048]{3,2,1,0:T(8,128)}, u32[]{:S(2)}) copy-start(f32[2,4,8,2048]{3,2,1,0:T(8,128)} %param.8) | copy-start | bytes 1572868
  1.0 34.8 %copy-start.4 = (pred[64,128]{1,0:T(32,128)(4,1)S(1)}, pred[64,128]{1,0:T(32,128)(4,1)}, u32[]{:S(2)}) copy-start(pred[64,128]{1,0:T(32,128)(4,1)} %constant.17.clone) | copy-start | bytes 24580
  1.0 34.8 %copy-start.7 = (f32[64]{0:T(128)S(1)}, f32[64]{0:T(128)}, u32[]{:S(2)}) copy-start(f32[64]{0:T(128)} %param.9) | copy-start | bytes 772
  1.0 34.9 %copy-start.5 = (f32[256]{0:T(256)S(1)}, f32[256]{0:T(256)}, u32[]{:S(2)}) copy-start(f32[256]{0:T(256)} %constant.18.clone) | copy-start | bytes 3076
  1.0 34.9 %copy-start.6 = (pred[128]{0:T(512)(128)(4,1)S(1)}, pred[128]{0:T(512)(128)(4,1)}, u32[]{:S(2)}) copy-start(pred[128]{0:T(512)(128)(4,1)} %constant.19.clone) | copy-start | bytes 388
  28.6 13.6 %collective-permute-start = (f32[51,8,128]{2,1,0:T(8,128)S(1)}, f32[51,8,128]{2,1,0:T(8,128)S(1)}, u32[]{:S(2)}, u32[]{:S(2)}) collective-permute-start(f32[51,8,128]{2,1,0:T(8,128)S(1)} %get-tuple-element.16), channel_id=1, source_target_pairs={{1,2},{2,1},{3,4},{4,3},{5,6},{6,5},{7,8},{8,7},{9,10},{10,9},{11,... | collective-permute-start | bytes 626696 | tf_op jit(solution)/shard_map/ppermute | solution.py:255
  33.9 3.6 %collective-permute-start.1 = (f32[51,8,128]{2,1,0:T(8,128)S(1)}, f32[51,8,128]{2,1,0:T(8,128)S(1)}, u32[]{:S(2)}, u32[]{:S(2)}) collective-permute-start(f32[51,8,128]{2,1,0:T(8,128)S(1)} %get-tuple-element.19), channel_id=1, source_target_pairs={{0,1},{1,0},{2,3},{3,2},{4,5},{5,4},{6,7},{7,6},{8,9},{9,8},{10,11... | collective-permute-start | bytes 626696 | tf_op jit(solution)/shard_map/ppermute | solution.py:256
  36.6 1.0 %copy-start.1 = (bf16[256,1024]{1,0:T(8,128)(2,1)S(1)}, bf16[256,1024]{1,0:T(8,128)(2,1)}, u32[]{:S(2)}) copy-start(bf16[256,1024]{1,0:T(8,128)(2,1)} %constant.14.clone.mid_ref) | copy-start | bytes 1572868
  36.6 1.1 %copy-start.3 = (bf16[256,384]{1,0:T(8,128)(2,1)S(1)}, bf16[256,384]{1,0:T(8,128)(2,1)}, u32[]{:S(2)}) copy-start(bf16[256,384]{1,0:T(8,128)(2,1)} %constant.16.clone.me_ref) | copy-start | bytes 589828
  37.5 4.7 %copy-start.2 = (bf16[256,384]{1,0:T(8,128)(2,1)S(1)}, bf16[256,384]{1,0:T(8,128)(2,1)}, u32[]{:S(2)}) copy-start(bf16[256,384]{1,0:T(8,128)(2,1)} %constant.15.clone.mo_ref) | copy-start | bytes 589828

commit v7 on v6

--- a/solution.py
+++ b/solution.py
@@ -15,6 +15,7 @@
 ROW = {0: 0, 1: 8, 2: 16, 7: 28, 6: 36, 5: 44, 3: 52, 4: 60}
 HALO_ROW = 24
 BLOCK = 68
+HELD = (16, 12)
 SLOT = {0: 0, 1: 1, 2: 2, 7: 4, 6: 5, 5: 6, 3: 7, 4: 8}
 HALO = 3
 EDGE_LANES = 18
@@ -27,7 +28,7 @@
     return lax.rem(lax.axis_index("line"), 2)
 
 
-def pack_kernel(x_ref, out_ref):
+def pack(x_ref, out_ref):
     blocks = x_ref.shape[0] // 64
     odd = parity()
     lane = lax.broadcasted_iota(jnp.int32, (8, LANES), 1)
@@ -48,6 +49,17 @@
         tile = halo[j + 1]
         tile = tile + pltpu.roll(pltpu.roll(tile, 4, 0), LANES // 2, 1)
         out_ref[pl.ds(BLOCK * PLACE.index(j) + HALO_ROW, 4), :] = tile[:4]
+
+
+def pack_kernel(x_ref, out_ref):
+    row = lax.rem(lax.axis_index("line"), 8)
+    times = 1 + jnp.where(row == 1, HELD[0], jnp.where(row == 6, HELD[1], 0))
+
+    def once(_, carry):
+        pack(x_ref, out_ref)
+        return carry
+
+    lax.fori_loop(0, times, once, 0)
 
 
 def edge_kernel(r_ref, o_ref, e_ref, halo_ref):

time: 44.2 us -> 41 us (0.928)
  the two profiles are of different devices: /device:TPU:23 before, /device:TPU:232 now
where the time goes in v7:
time: 41 us; the launch traced here: 40.7 us
  blocking collectives  25.2 us (61%)
  starting transfers between devices  5.73 us (14%)
  Pallas kernels  4.78 us (12%)
  waiting for transfers between devices  2.88 us (7%)
  local copies, waits for them, and re-layouts  1.26 us (3%)
  other arithmetic  0.73 us (2%)
    all_to_all x1, blocking collectives, spectrum(): lax.all_to_all(packed, 'acq', 0, 0, tiled=True, axis_index_groups=[PLACE])  25.2 us
    pallas_call x5, Pallas kernels, on(): pl.pallas_call(kernel, out_shape=[jax.ShapeDtypeStruct(shape, dtype) for...  4.78 us
    ppermute x1, starting transfers between devices, spectrum(): side_e = lax.ppermute(to_e, 'line', inner)  3.81 us
    ppermute x1, waiting for transfers between devices, spectrum(): side_o = lax.ppermute(to_o, 'line', outer)  2.88 us
    ppermute x1, starting transfers between devices, spectrum(): side_o = lax.ppermute(to_o, 'line', outer)  1.92 us
    unnamed x16, local copies, waits for them, and re-layouts  1.26 us
  transfers between devices with their start and end apart: 2, of which 1 were waited for; matrix products, arithmetic and copies ran while one was open for 2% of the time, Pallas kernels for 6%

profile of v7, /device:TPU:232, one launch (start us, length us, event | category | flops | bytes accessed | tf_op | source)
XLA Modules:
  0.0 40.7 jit_solution(13405155294547159097)
XLA Ops:
  0.0 0.0 copy-start
  0.0 1.0 %copy-done = f32[2,4,8,2048]{3,2,1,0:T(8,128)S(1)} copy-done((f32[2,4,8,2048]{3,2,1,0:T(8,128)S(1)}, f32[2,4,8,2048]{3,2,1,0:T(8,128)}, u32[]{:S(2)}) %copy-start) | copy-done | bytes 524312
  1.0 0.0 copy-start.4
  1.0 0.0 copy-start.7
  1.0 0.0 copy-start.5
  1.0 0.0 copy-start.6
  1.1 0.5 %shard_map.82 = f32[1088,128]{1,0:T(8,128)S(1)} custom-call(f32[1024,128]{1,0:T(8,128)S(1)} %bitcast.10), custom_call_target="tpu_custom_call" | custom-call | flops 1000000 | bytes 1000000 | tf_op jit(solution)/shard_map/pallas_call | solution.py:237
  1.5 25.2 %all_to_all.5 = f32[16,68,1,128]{3,2,1,0:T(1,128)S(1)} all-to-all(f32[16,68,1,128]{3,2,1,0:T(1,128)S(1)} %bitcast.9), channel_id=1, replica_groups={{256,288,192,224,320,352,128,160,384,416,64,96,448,480,0,32},{257,289,1..., dimensions={0} | all-to-all | bytes 1114112 | tf_op jit(solution)/shard_map/all_to_all | solution.py:260
  26.8 0.2 shard_map.83
  26.9 1.9 %collective-permute-start = (f32[51,8,128]{2,1,0:T(8,128)S(1)}, f32[51,8,128]{2,1,0:T(8,128)S(1)}, u32[]{:S(2)}, u32[]{:S(2)}) collective-permute-start(f32[51,8,128]{2,1,0:T(8,128)S(1)} %get-tuple-element.16), channel_id=1, source_target_pairs={{1,2},{2,1},{3,4},{4,3},{5,6},{6,5},{7,8},{8,7},{9,10},{10,9},{11,... | collective-permute-start | bytes 626696 | tf_op jit(solution)/shard_map/ppermute | solution.py:267
  28.9 3.8 %collective-permute-start.1 = (f32[51,8,128]{2,1,0:T(8,128)S(1)}, f32[51,8,128]{2,1,0:T(8,128)S(1)}, u32[]{:S(2)}, u32[]{:S(2)}) collective-permute-start(f32[51,8,128]{2,1,0:T(8,128)S(1)} %get-tuple-element.19), channel_id=1, source_target_pairs={{0,1},{1,0},{2,3},{3,2},{4,5},{5,4},{6,7},{7,6},{8,9},{9,8},{10,11... | collective-permute-start | bytes 626696 | tf_op jit(solution)/shard_map/ppermute | solution.py:268
  32.7 0.0 copy-done.4
  32.7 0.0 copy-done.7
  32.7 0.1 select_reduce_fusion
  32.8 0.0 copy-done.5
  32.8 0.0 copy-done.6
  32.8 0.5 %fusion.2 = (f32[256,128]{1,0:T(8,128)S(1)}, f32[256,128]{1,0:T(8,128)S(1)}) fusion(f32[128]{0:T(128)S(1)} %select_reduce_fusion, f32[256]{0:T(256)S(1)} %copy-done.5, pred[128]{0:T(512)(128)(4,1)S(1)} %copy-done.6), kind=kLoop, calls=%fused_computation.8 | loop fusion | flops 131072 | bytes 263808 | tf_op jit(solution)/shard_map/jit(_where)/select_n | solution.py:224
  33.5 0.0 copy-start.1
  33.5 0.0 copy-start.3
  33.5 0.8 %shard_map.84.own_ref = f32[9,264,128]{2,1,0:T(8,128)S(1)} custom-call(f32[1088,128]{1,0:T(8,128)S(1)} %bitcast.8, f32[16,8,128]{2,1,0:T(8,128)S(1)} %get-tuple-element.17.halo_ref, bf16[512,384]{1,0:T(8,128)(2,1)S(1)} %pad_maximum_fusion.steer_ref), custom_call_target="tpu_custom_call" | custom-call | flops 1000000000 | bytes 1000000 | tf_op jit(solution)/shard_map/pallas_call | solution.py:237
  34.3 0.0 copy-start.2
  34.4 0.0 collective-permute-done.1.e_ref
  34.4 0.1 copy-done.1
  34.5 0.0 copy-done.3
  34.5 1.4 %shard_map.85 = (f32[2048,128]{1,0:T(8,128)S(1)}, f32[3,264,128]{2,1,0:T(8,128)S(1)}, f32[264,384]{1,0:T(8,128)S(1)}) custom-call(f32[9,264,128]{2,1,0:T(8,128)S(1)} %shard_map.84.own_ref, f32[51,8,128]{2,1,0:T(8,128)S(1)} %collective-permute-done.1.e_ref, bf16[512,384]{1,0:T(8,128)(2,1)S(1)} %pad_maximum_fusion.steer_ref, bf16[256,1024]{1,0:T(8,128)(2,1)S(1)} %copy-done.1, ...), custom_call_target="tpu_custom_call" | custom-call | flops 1000000000 | bytes 1000000 | tf_op jit(solution)/shard_map/pallas_call | solution.py:237
  36.0 2.9 %collective-permute-done.o_ref = f32[51,8,128]{2,1,0:T(8,128)S(1)} collective-permute-done((f32[51,8,128]{2,1,0:T(8,128)S(1)}, f32[51,8,128]{2,1,0:T(8,128)S(1)}, u32[]{:S(2)}, u32[]{:S(2)}) %collective-permute-start) | collective-permute-done | bytes 208928 | tf_op jit(solution)/shard_map/ppermute | solution.py:267
  38.9 0.0 copy-done.2
  38.9 1.9 %shard_map.86 = bf16[256,8,128]{2,1,0:T(8,128)(2,1)} custom-call(f32[51,8,128]{2,1,0:T(8,128)S(1)} %collective-permute-done.o_ref, f32[3,264,128]{2,1,0:T(8,128)S(1)} %get-tuple-element.20.part_ref, f32[264,384]{1,0:T(8,128)S(1)} %get-tuple-element.21.cor_ref, f32[2048,128]{1,0:T(8,128)S(1)} %get-tuple-element.22.flat_ref, ...), custom_call_target="tpu_custom_call" | custom-call | flops 1000000000 | bytes 1000000 | tf_op jit(solution)/shard_map/pallas_call | solution.py:237
  (2 shorter events, 0.1 us)
Async XLA Ops:
  0.0 1.0 %copy-start = (f32[2,4,8,2048]{3,2,1,0:T(8,128)S(1)}, f32[2,4,8,2048]{3,2,1,0:T(8,128)}, u32[]{:S(2)}) copy-start(f32[2,4,8,2048]{3,2,1,0:T(8,128)} %param.8) | copy-start | bytes 1572868
  1.0 31.6 %copy-start.4 = (pred[64,128]{1,0:T(32,128)(4,1)S(1)}, pred[64,128]{1,0:T(32,128)(4,1)}, u32[]{:S(2)}) copy-start(pred[64,128]{1,0:T(32,128)(4,1)} %constant.17.clone) | copy-start | bytes 24580
  1.0 31.6 %copy-start.7 = (f32[64]{0:T(128)S(1)}, f32[64]{0:T(128)}, u32[]{:S(2)}) copy-start(f32[64]{0:T(128)} %param.9) | copy-start | bytes 772
  1.0 31.7 %copy-start.5 = (f32[256]{0:T(256)S(1)}, f32[256]{0:T(256)}, u32[]{:S(2)}) copy-start(f32[256]{0:T(256)} %constant.18.clone) | copy-start | bytes 3076
  1.0 31.7 %copy-start.6 = (pred[128]{0:T(512)(128)(4,1)S(1)}, pred[128]{0:T(512)(128)(4,1)}, u32[]{:S(2)}) copy-start(pred[128]{0:T(512)(128)(4,1)} %constant.19.clone) | copy-start | bytes 388
  26.9 11.9 %collective-permute-start = (f32[51,8,128]{2,1,0:T(8,128)S(1)}, f32[51,8,128]{2,1,0:T(8,128)S(1)}, u32[]{:S(2)}, u32[]{:S(2)}) collective-permute-start(f32[51,8,128]{2,1,0:T(8,128)S(1)} %get-tuple-element.16), channel_id=1, source_target_pairs={{1,2},{2,1},{3,4},{4,3},{5,6},{6,5},{7,8},{8,7},{9,10},{10,9},{11,... | collective-permute-start | bytes 626696 | tf_op jit(solution)/shard_map/ppermute | solution.py:267
  28.9 5.5 %collective-permute-start.1 = (f32[51,8,128]{2,1,0:T(8,128)S(1)}, f32[51,8,128]{2,1,0:T(8,128)S(1)}, u32[]{:S(2)}, u32[]{:S(2)}) collective-permute-start(f32[51,8,128]{2,1,0:T(8,128)S(1)} %get-tuple-element.19), channel_id=1, source_target_pairs={{0,1},{1,0},{2,3},{3,2},{4,5},{5,4},{6,7},{7,6},{8,9},{9,8},{10,11... | collective-permute-start | bytes 626696 | tf_op jit(solution)/shard_map/ppermute | solution.py:268
  33.5 1.0 %copy-start.1 = (bf16[256,1024]{1,0:T(8,128)(2,1)S(1)}, bf16[256,1024]{1,0:T(8,128)(2,1)}, u32[]{:S(2)}) copy-start(bf16[256,1024]{1,0:T(8,128)(2,1)} %constant.14.clone.mid_ref) | copy-start | bytes 1572868
  33.5 1.1 %copy-start.3 = (bf16[256,384]{1,0:T(8,128)(2,1)S(1)}, bf16[256,384]{1,0:T(8,128)(2,1)}, u32[]{:S(2)}) copy-start(bf16[256,384]{1,0:T(8,128)(2,1)} %constant.16.clone.me_ref) | copy-start | bytes 589828
  34.3 4.5 %copy-start.2 = (bf16[256,384]{1,0:T(8,128)(2,1)S(1)}, bf16[256,384]{1,0:T(8,128)(2,1)}, u32[]{:S(2)}) copy-start(bf16[256,384]{1,0:T(8,128)(2,1)} %constant.15.clone.mo_ref) | copy-start | bytes 589828

commit v8 on v7

--- a/solution.py
+++ b/solution.py
@@ -15,7 +15,7 @@
 ROW = {0: 0, 1: 8, 2: 16, 7: 28, 6: 36, 5: 44, 3: 52, 4: 60}
 HALO_ROW = 24
 BLOCK = 68
-HELD = (16, 12)
+HELD = (26, 17)
 SLOT = {0: 0, 1: 1, 2: 2, 7: 4, 6: 5, 5: 6, 3: 7, 4: 8}
 HALO = 3
 EDGE_LANES = 18
@@ -28,17 +28,33 @@
     return lax.rem(lax.axis_index("line"), 2)
 
 
+def transposed(tiles):
+    sub = lax.broadcasted_iota(jnp.int32, (8, LANES), 0)
+    tiles = list(tiles)
+    for d in (4, 2, 1):
+        low = (sub & d) == 0
+        for i in range(8):
+            if i & d == 0:
+                a, b = tiles[i], tiles[i + d]
+                tiles[i] = jnp.where(low, a, pltpu.roll(b, d, 0))
+                tiles[i + d] = jnp.where(low, pltpu.roll(a, 8 - d, 0), b)
+    return tiles
+
+
+def turned(tiles, odd):
+    return [jnp.where(odd, tiles[-1 - i], tile) for i, tile in enumerate(tiles)]
+
+
 def pack(x_ref, out_ref):
     blocks = x_ref.shape[0] // 64
-    odd = parity()
+    odd = parity() == 1
     lane = lax.broadcasted_iota(jnp.int32, (8, LANES), 1)
     zero = jnp.zeros((8, LANES), jnp.float32)
     halo = [zero, zero]
     for j in range(blocks):
         halo.append(zero)
-        for m in range(8):
-            line = m + odd * (7 - 2 * m)
-            tile = x_ref[pl.ds(8 * j + line, 8, stride=8 * blocks), :]
+        rows = [slice(8 * (blocks * channel + j), 8 * (blocks * channel + j) + 8) for channel in range(8)]
+        for m, tile in enumerate(turned(transposed([x_ref[r] for r in rows]), odd)):
             out_ref[pl.ds(BLOCK * PLACE.index(j) + ROW[m], 8), :] = tile
             left = (lane >= 6 * m) & (lane < 6 * m + 3)
             right = (lane >= 6 * m + 3) & (lane < 6 * m + 6)
@@ -52,8 +68,10 @@
 
 
 def pack_kernel(x_ref, out_ref):
-    row = lax.rem(lax.axis_index("line"), 8)
-    times = 1 + jnp.where(row == 1, HELD[0], jnp.where(row == 6, HELD[1], 0))
+    line, lines = lax.axis_index("line"), lax.axis_size("line")
+    row = lax.rem(line, 8)
+    first, last = (row == 1) & (line > 1), (row == 6) & (line < lines - 2)
+    times = 1 + jnp.where(first, HELD[0], jnp.where(last, HELD[1], 0))
 
     def once(_, carry):
         pack(x_ref, out_ref)
@@ -83,31 +101,31 @@
         e_ref[48 + g] = sums[1]
 
 
-def side_beams(ref, steer_ref, beams_ref, halo_ref, side_ref):
+def side_beams(ref, steer_ref, halo_ref, side_ref):
     lane = lax.broadcasted_iota(jnp.int32, (8, LANES), 1)
     for j in range(16):
         tile = pltpu.roll(ref[48 + j // MERGED], -EDGE_LANES * (j % MERGED) % LANES, 1)
         halo_ref[j] = jnp.where(lane < EDGE_LANES, tile, 0.0)
     lines = ref[:48].reshape(16, 3, 8, LANES)
     for s in (0, 2):
-        both = beam_pair(lines[:, s], lines[:, 1] if s == 0 else halo_ref[...], steer_ref, beams_ref)
+        both = beam_pair(lines[:, s], lines[:, 1] if s == 0 else halo_ref[...], steer_ref)
         side_ref[s] = both[:, :LANES]
         side_ref[s + 1] = both[:, LANES:]
 
 
-def beam_pair(first, second, steer_ref, beams_ref):
+def beam_pair(first, second, steer_ref):
     both = jnp.concatenate([first.reshape(LANES, LANES), second.reshape(LANES, LANES)], axis=1)
     high = both.astype(jnp.bfloat16)
     low = (both - high.astype(jnp.float32)).astype(jnp.bfloat16)
     stacked = jnp.concatenate([high, low, high], axis=0)
-    beams_ref[...] = jnp.dot(steer_ref[...], stacked, preferred_element_type=jnp.float32)
-    re, im = beams_ref[:HEIGHTS], beams_ref[HEIGHTS:]
-    power = re * re + im * im
+    beams = jnp.dot(steer_ref[...], stacked, preferred_element_type=jnp.float32)
+    beams = beams.reshape(HEIGHTS // 8, 2, 8, 2 * LANES)
+    power = beams[:, 0] * beams[:, 0] + beams[:, 1] * beams[:, 1]
     squares = (both * both).reshape(16, 8, 2 * LANES).sum(axis=0)
-    return jnp.concatenate([power, squares], axis=0)
-
-
-def own_kernel(r_ref, halo_ref, steer_ref, out_ref, beams_ref):
+    return jnp.concatenate([power.reshape(HEIGHTS, 2 * LANES), squares], axis=0)
+
+
+def own_kernel(r_ref, halo_ref, steer_ref, out_ref):
     def block(s):
         if s == HALO:
             return halo_ref[...]
@@ -116,7 +134,7 @@
 
     for s in (0, 2, 4, 6, 8):
         t = min(s + 1, 8)
-        both = beam_pair(block(s), block(t), steer_ref, beams_ref)
+        both = beam_pair(block(s), block(t), steer_ref)
         out_ref[s] = both[:, :LANES]
         if t != s:
             out_ref[t] = both[:, LANES:]
@@ -128,65 +146,66 @@
     return jnp.concatenate([high, low], axis=1)
 
 
-def boxed(total, correction):
+def boxed(total, correction, few):
     lane = lax.broadcasted_iota(jnp.int32, total.shape, 1)
+
+    def after(field, d):
+        return jnp.where(lane >= d, pltpu.roll(field, d, 1), 0.0)
+
+    def before(field, d):
+        return jnp.where(lane < LANES - d, pltpu.roll(field, LANES - d, 1), 0.0)
+
+    if few:
+        right, left = total + after(total, 1), before(total, 1)
+        return (right + after(right, 2)) + (left + before(total + left, 2)) + correction
     box = total + correction
     for d in (1, 2, 3):
-        box = box + jnp.where(lane >= d, pltpu.roll(total, d, 1), 0.0)
-        box = box + jnp.where(lane < LANES - d, pltpu.roll(total, LANES - d, 1), 0.0)
+        box = (box + after(total, d)) + before(total, d)
     return box
 
 
-def normalize(m, odd, box_of, flat_ref):
-    line = m + odd * (7 - 2 * m)
-    energy = box_of(m, slice(HEIGHTS, ROWS)).sum(axis=0, keepdims=True)
-    inverse = 1.0 / (energy + epsilon)
-    for k in range(0, HEIGHTS, 64):
-        flat_ref[pl.ds(8 * k + line, 64, stride=8), :] = box_of(m, slice(k, k + 64)) * inverse
-
-
-def inner_kernel(own_ref, e_ref, steer_ref, mid_ref, me_ref, flat_ref, part_ref, cor_ref, beams_ref, halo_ref, side_ref, all_ref):
-    side_beams(e_ref, steer_ref, beams_ref, halo_ref, side_ref)
+def normalize(box_of, ref):
+    inverse = [1.0 / (box.sum(axis=0, keepdims=True) + epsilon) for box in box_of(slice(HEIGHTS, ROWS))]
+    for k in range(0, HEIGHTS, 8):
+        for n, box in enumerate(box_of(slice(k, k + 8))):
+            ref[n, k : k + 8] = box * inverse[n]
+
+
+def inner_kernel(own_ref, e_ref, steer_ref, mid_ref, me_ref, done_ref, part_ref, cor_ref, halo_ref, side_ref, all_ref):
+    side_beams(e_ref, steer_ref, halo_ref, side_ref)
     all_ref[...] = jnp.dot(halves(own_ref[HALO]), mid_ref[...], preferred_element_type=jnp.float32)
     all_ref[:, 5 * LANES :] += jnp.dot(halves(side_ref[3]), me_ref[...], preferred_element_type=jnp.float32)
     cor_ref[...] = all_ref[:, : 3 * LANES]
 
-    def summed(m, rows):
-        total = None
-        for position in range(max(m - 3, 0), m + 4):
-            term = side_ref[position - 8, rows] if position > 7 else own_ref[SLOT[position], rows]
-            total = term if total is None else total + term
-        return total
-
-    for m in range(3):
-        for k in range(0, ROWS, 88):
-            part_ref[m, k : k + 88] = summed(m, slice(k, k + 88))
-    odd = parity()
-    for m in range(3, 8):
-        normalize(m, odd, lambda m, rows: boxed(summed(m, rows), all_ref[rows, m * LANES : (m + 1) * LANES]), flat_ref)
-
-
-def outer_kernel(o_ref, part_ref, cor_ref, flat_ref, steer_ref, mo_ref, out_ref, beams_ref, halo_ref, side_ref, all_ref, edge_ref, done_ref, sems):
-    side_beams(o_ref, steer_ref, beams_ref, halo_ref, side_ref)
+    def box_of(rows):
+        ones = [own_ref[SLOT[m], rows] for m in range(8)] + [side_ref[n, rows] for n in range(3)]
+        twos = [a + b for a, b in zip(ones[:-1], ones[1:])]
+        fours = [a + b for a, b in zip(twos[:-2], twos[2:])]
+        for m, total in enumerate((fours[0], fours[0] + ones[4], fours[0] + twos[4])):
+            part_ref[m, rows] = total
+        sums = [fours[n] + (twos[n + 4] + ones[n + 6]) for n in range(5)]
+        return [boxed(total, all_ref[rows, (n + 3) * LANES : (n + 4) * LANES], False) for n, total in enumerate(sums)]
+
+    normalize(box_of, done_ref)
+
+
+def outer_kernel(o_ref, part_ref, cor_ref, lines_ref, steer_ref, mo_ref, out_ref, halo_ref, side_ref, all_ref, edge_ref, done_ref, sems):
+    side_beams(o_ref, steer_ref, halo_ref, side_ref)
     all_ref[...] = cor_ref[...] + jnp.dot(halves(side_ref[3]), mo_ref[...], preferred_element_type=jnp.float32)
 
-    def box_of(m, rows):
-        total = part_ref[m, rows]
-        for i in range(3 - m):
-            total = total + side_ref[i, rows]
-        return boxed(total, all_ref[rows, m * LANES : (m + 1) * LANES])
-
-    odd = parity()
-    for m in range(3):
-        normalize(m, odd, box_of, edge_ref)
-    sub = lax.broadcasted_iota(jnp.int32, (16, 8, LANES), 1)
-    edge = jnp.where(odd == 1, 7 - sub, sub) < 3
+    def box_of(rows):
+        near, next_, far = (side_ref[n, rows] for n in range(3))
+        two = near + next_
+        sums = (part_ref[0, rows] + (two + far), part_ref[1, rows] + two, part_ref[2, rows] + near)
+        return [boxed(total, all_ref[rows, n * LANES : (n + 1) * LANES], True) for n, total in enumerate(sums)]
+
+    normalize(box_of, edge_ref)
+    odd = parity() == 1
     copies = []
     for q in range(4):
-        for k in range(64 * q, 64 * q + 64, 16):
-            rows = slice(8 * k, 8 * k + 128)
-            merged = jnp.where(edge, edge_ref[rows].reshape(16, 8, LANES), flat_ref[rows].reshape(16, 8, LANES))
-            done_ref[k : k + 16] = merged.astype(jnp.bfloat16)
+        for k in range(64 * q, 64 * q + 64, 8):
+            tiles = [edge_ref[m, k : k + 8] for m in range(3)] + [lines_ref[m, k : k + 8] for m in range(5)]
+            done_ref[k : k + 8] = jnp.stack(transposed(turned(tiles, odd))).astype(jnp.bfloat16)
         copy = pltpu.make_async_copy(done_ref.at[pl.ds(64 * q, 64)], out_ref.at[pl.ds(64 * q, 64)], sems.at[q])
         copy.start()
         copies.append(copy)
@@ -222,6 +241,7 @@
     phases = jnp.asarray(heights)[:, None] * waves[None, :]
     cosine, sine = jnp.cos(phases), jnp.sin(phases)
     full = jnp.concatenate([jnp.where(real, cosine, sine), jnp.where(real, -sine, cosine)], axis=0)
+    full = full.reshape(2, HEIGHTS // 8, 8, LANES).transpose(1, 0, 2, 3).reshape(2 * HEIGHTS, LANES)
     high = lax.reduce_precision(full, 8, 7)
     low = (full - high).astype(jnp.bfloat16)
     high = high.astype(jnp.bfloat16)
@@ -251,7 +271,6 @@
     lines = lax.axis_size("line")
     outer = [pair for i in range(1, lines - 1, 2) for pair in ((i, i + 1), (i + 1, i))]
     inner = [pair for i in range(0, lines, 2) for pair in ((i, i + 1), (i + 1, i))]
-    beams = pltpu.VMEM((2 * HEIGHTS, 2 * LANES), jnp.float32)
     strip = pltpu.VMEM((16, 8, LANES), jnp.float32)
     quad = pltpu.VMEM((4, ROWS, LANES), jnp.float32)
     stack = slc_stack.reshape(8, 8, -1, LANES).transpose(0, 2, 1, 3).reshape(-1, LANES)
@@ -266,13 +285,13 @@
     steer = steering(wavenumbers)
     side_o = lax.ppermute(to_o, "line", outer)
     side_e = lax.ppermute(to_e, "line", inner)
-    (own,) = call(own_kernel, [(9, ROWS, LANES)], 10, 1000000000, [beams])(gathered, halo, steer)
-    flat, part, cor = call(
+    (own,) = call(own_kernel, [(9, ROWS, LANES)], 10, 1000000000)(gathered, halo, steer)
+    rest, part, cor = call(
         inner_kernel,
-        [(8 * HEIGHTS, LANES), (3, ROWS, LANES), (ROWS, 3 * LANES)],
+        [(5, HEIGHTS, LANES), (3, ROWS, LANES), (ROWS, 3 * LANES)],
         14,
         1000000000,
-        [beams, strip, quad, pltpu.VMEM((ROWS, 8 * LANES), jnp.float32)],
+        [strip, quad, pltpu.VMEM((ROWS, 8 * LANES), jnp.float32)],
     )(own, side_e, steer, mid, me)
     (result,) = call(
         outer_kernel,
@@ -280,17 +299,16 @@
         12,
         1000000000,
         [
-            beams,
             strip,
             quad,
             pltpu.VMEM((ROWS, 3 * LANES), jnp.float32),
-            pltpu.VMEM((8 * HEIGHTS, LANES), jnp.float32),
+            pltpu.VMEM((3, HEIGHTS, LANES), jnp.float32),
             pltpu.VMEM((HEIGHTS, 8, LANES), jnp.bfloat16),
             pltpu.SemaphoreType.DMA((4,)),
         ],
         out=ANY,
         dtype=jnp.bfloat16,
-    )(side_o, part, cor, flat, steer, mo)
+    )(side_o, part, cor, rest, steer, mo)
     return result
 
 

time: 41 us -> 40.4 us (0.985)
  the two profiles are of different devices: /device:TPU:232 before, /device:TPU:1 now
where the time goes in v8:
time: 40.4 us; the launch traced here: 40.2 us
  blocking collectives  27.7 us (69%)
  starting transfers between devices  5.93 us (15%)
  Pallas kernels  4.37 us (11%)
  local copies, waits for them, and re-layouts  1.28 us (3%)
  other arithmetic  0.75 us (2%)
    all_to_all x1, blocking collectives, spectrum(): lax.all_to_all(packed, 'acq', 0, 0, tiled=True, axis_index_groups=[PLACE])  27.7 us
    pallas_call x5, Pallas kernels, on(): pl.pallas_call(kernel, out_shape=[jax.ShapeDtypeStruct(shape, dtype) for...  4.37 us
    ppermute x1, starting transfers between devices, spectrum(): side_o = lax.ppermute(to_o, 'line', outer)  4.01 us
    ppermute x1, starting transfers between devices, spectrum(): side_e = lax.ppermute(to_e, 'line', inner)  1.92 us
    unnamed x16, local copies, waits for them, and re-layouts  1.26 us
  transfers between devices with their start and end apart: 2, of which 0 were waited for; matrix products, arithmetic and copies ran while one was open for 2% of the time, Pallas kernels for 5%

profile of v8, /device:TPU:1, one launch (start us, length us, event | category | flops | bytes accessed | tf_op | source)
XLA Modules:
  0.0 40.2 jit_solution(4727591804187685134)
XLA Ops:
  0.0 0.0 copy-start
  0.0 1.0 %copy-done = f32[2,4,8,2048]{3,2,1,0:T(8,128)S(1)} copy-done((f32[2,4,8,2048]{3,2,1,0:T(8,128)S(1)}, f32[2,4,8,2048]{3,2,1,0:T(8,128)}, u32[]{:S(2)}) %copy-start) | copy-done | bytes 524312
  1.0 0.0 copy-start.4
  1.0 0.0 copy-start.7
  1.0 0.0 copy-start.5
  1.0 0.0 copy-start.6
  1.1 0.3 shard_map.82
  1.4 27.7 %all_to_all.5 = f32[16,68,1,128]{3,2,1,0:T(1,128)S(1)} all-to-all(f32[16,68,1,128]{3,2,1,0:T(1,128)S(1)} %bitcast.15), channel_id=1, replica_groups={{256,288,192,224,320,352,128,160,384,416,64,96,448,480,0,32},{257,289,1..., dimensions={0} | all-to-all | bytes 1114112 | tf_op jit(solution)/shard_map/all_to_all | solution.py:279
  29.1 0.2 shard_map.83
  29.2 4.0 %collective-permute-start = (f32[51,8,128]{2,1,0:T(8,128)S(1)}, f32[51,8,128]{2,1,0:T(8,128)S(1)}, u32[]{:S(2)}, u32[]{:S(2)}) collective-permute-start(f32[51,8,128]{2,1,0:T(8,128)S(1)} %get-tuple-element.16), channel_id=1, source_target_pairs={{1,2},{2,1},{3,4},{4,3},{5,6},{6,5},{7,8},{8,7},{9,10},{10,9},{11,... | collective-permute-start | bytes 626696 | tf_op jit(solution)/shard_map/ppermute | solution.py:286
  33.2 1.9 %collective-permute-start.1 = (f32[51,8,128]{2,1,0:T(8,128)S(1)}, f32[51,8,128]{2,1,0:T(8,128)S(1)}, u32[]{:S(2)}, u32[]{:S(2)}) collective-permute-start(f32[51,8,128]{2,1,0:T(8,128)S(1)} %get-tuple-element.19), channel_id=1, source_target_pairs={{0,1},{1,0},{2,3},{3,2},{4,5},{5,4},{6,7},{7,6},{8,9},{9,8},{10,11... | collective-permute-start | bytes 626696 | tf_op jit(solution)/shard_map/ppermute | solution.py:287
  35.2 0.0 copy-done.4
  35.2 0.0 copy-done.7
  35.2 0.1 select_reduce_fusion
  35.3 0.0 copy-done.5
  35.3 0.0 copy-done.6
  35.3 0.5 %fusion.2 = (f32[256,128]{1,0:T(8,128)S(1)}, f32[256,128]{1,0:T(8,128)S(1)}) fusion(f32[128]{0:T(128)S(1)} %select_reduce_fusion, f32[256]{0:T(256)S(1)} %copy-done.5, pred[128]{0:T(512)(128)(4,1)S(1)} %copy-done.6), kind=kLoop, calls=%fused_computation.8 | loop fusion | flops 131072 | bytes 263808 | tf_op jit(solution)/shard_map/jit(_where)/select_n | solution.py:243
  36.0 0.0 copy-start.1
  36.0 0.0 copy-start.3
  36.0 0.8 %shard_map.84.own_ref = f32[9,264,128]{2,1,0:T(8,128)S(1)} custom-call(f32[1088,128]{1,0:T(8,128)S(1)} %bitcast.14, f32[16,8,128]{2,1,0:T(8,128)S(1)} %get-tuple-element.17.halo_ref, bf16[512,384]{1,0:T(8,128)(2,1)S(1)} %pad_maximum_fusion.steer_ref), custom_call_target="tpu_custom_call" | custom-call | flops 1000000000 | bytes 1000000 | tf_op jit(solution)/shard_map/pallas_call | solution.py:257
  36.9 0.0 copy-start.2
  36.9 0.0 collective-permute-done.1.e_ref
  36.9 0.1 copy-done.1
  37.1 0.0 copy-done.3
  37.1 1.3 %shard_map.85 = (f32[5,256,128]{2,1,0:T(8,128)S(1)}, f32[3,264,128]{2,1,0:T(8,128)S(1)}, f32[264,384]{1,0:T(8,128)S(1)}) custom-call(f32[9,264,128]{2,1,0:T(8,128)S(1)} %shard_map.84.own_ref, f32[51,8,128]{2,1,0:T(8,128)S(1)} %collective-permute-done.1.e_ref, bf16[512,384]{1,0:T(8,128)(2,1)S(1)} %pad_maximum_fusion.steer_ref, ...), custom_call_target="tpu_custom_call" | custom-call | flops 1000000000 | bytes 1000000 | tf_op jit(solution)/shard_map/pallas_call | solution.py:257
  38.4 0.0 collective-permute-done.o_ref
  38.5 0.0 copy-done.2
  38.5 1.7 %shard_map.86 = bf16[256,8,128]{2,1,0:T(8,128)(2,1)} custom-call(f32[51,8,128]{2,1,0:T(8,128)S(1)} %collective-permute-done.o_ref, f32[3,264,128]{2,1,0:T(8,128)S(1)} %get-tuple-element.20.part_ref, f32[264,384]{1,0:T(8,128)S(1)} %get-tuple-element.21.cor_ref, f32[5,256,128]{2,1,0:T(8,128)S(1)} %get-tuple-element.22.lines_ref, ...), custom_call_target="tpu_custom_call" | custom-call | flops 1000000000 | bytes 1000000 | tf_op jit(solution)/shard_map/pallas_call | solution.py:257
  (4 shorter events, 0.1 us)
Async XLA Ops:
  0.0 1.0 %copy-start = (f32[2,4,8,2048]{3,2,1,0:T(8,128)S(1)}, f32[2,4,8,2048]{3,2,1,0:T(8,128)}, u32[]{:S(2)}) copy-start(f32[2,4,8,2048]{3,2,1,0:T(8,128)} %param.8) | copy-start | bytes 1572868
  1.0 34.1 %copy-start.4 = (pred[64,128]{1,0:T(32,128)(4,1)S(1)}, pred[64,128]{1,0:T(32,128)(4,1)}, u32[]{:S(2)}) copy-start(pred[64,128]{1,0:T(32,128)(4,1)} %constant.17.clone) | copy-start | bytes 24580
  1.0 34.1 %copy-start.7 = (f32[64]{0:T(128)S(1)}, f32[64]{0:T(128)}, u32[]{:S(2)}) copy-start(f32[64]{0:T(128)} %param.9) | copy-start | bytes 772
  1.0 34.2 %copy-start.5 = (f32[256]{0:T(256)S(1)}, f32[256]{0:T(256)}, u32[]{:S(2)}) copy-start(f32[256]{0:T(256)} %constant.18.clone) | copy-start | bytes 3076
  1.0 34.2 %copy-start.6 = (pred[128]{0:T(512)(128)(4,1)S(1)}, pred[128]{0:T(512)(128)(4,1)}, u32[]{:S(2)}) copy-start(pred[128]{0:T(512)(128)(4,1)} %constant.19.clone) | copy-start | bytes 388
  29.2 9.2 %collective-permute-start = (f32[51,8,128]{2,1,0:T(8,128)S(1)}, f32[51,8,128]{2,1,0:T(8,128)S(1)}, u32[]{:S(2)}, u32[]{:S(2)}) collective-permute-start(f32[51,8,128]{2,1,0:T(8,128)S(1)} %get-tuple-element.16), channel_id=1, source_target_pairs={{1,2},{2,1},{3,4},{4,3},{5,6},{6,5},{7,8},{8,7},{9,10},{10,9},{11,... | collective-permute-start | bytes 626696 | tf_op jit(solution)/shard_map/ppermute | solution.py:286
  33.2 3.7 %collective-permute-start.1 = (f32[51,8,128]{2,1,0:T(8,128)S(1)}, f32[51,8,128]{2,1,0:T(8,128)S(1)}, u32[]{:S(2)}, u32[]{:S(2)}) collective-permute-start(f32[51,8,128]{2,1,0:T(8,128)S(1)} %get-tuple-element.19), channel_id=1, source_target_pairs={{0,1},{1,0},{2,3},{3,2},{4,5},{5,4},{6,7},{7,6},{8,9},{9,8},{10,11... | collective-permute-start | bytes 626696 | tf_op jit(solution)/shard_map/ppermute | solution.py:287
  36.0 1.0 %copy-start.1 = (bf16[256,1024]{1,0:T(8,128)(2,1)S(1)}, bf16[256,1024]{1,0:T(8,128)(2,1)}, u32[]{:S(2)}) copy-start(bf16[256,1024]{1,0:T(8,128)(2,1)} %constant.14.clone.mid_ref) | copy-start | bytes 1572868
  36.0 1.1 %copy-start.3 = (bf16[256,384]{1,0:T(8,128)(2,1)S(1)}, bf16[256,384]{1,0:T(8,128)(2,1)}, u32[]{:S(2)}) copy-start(bf16[256,384]{1,0:T(8,128)(2,1)} %constant.16.clone.me_ref) | copy-start | bytes 589828
  36.9 1.6 %copy-start.2 = (bf16[256,384]{1,0:T(8,128)(2,1)S(1)}, bf16[256,384]{1,0:T(8,128)(2,1)}, u32[]{:S(2)}) copy-start(bf16[256,384]{1,0:T(8,128)(2,1)} %constant.15.clone.mo_ref) | copy-start | bytes 589828

commit v9 on v8

--- a/solution.py
+++ b/solution.py
@@ -146,7 +146,13 @@
     return jnp.concatenate([high, low], axis=1)
 
 
-def boxed(total, correction, few):
+def normalized(total, correction, band_ref):
+    box = jnp.dot(halves(total), band_ref[...], preferred_element_type=jnp.float32) + correction
+    energy = box[HEIGHTS:].sum(axis=0, keepdims=True)
+    return box[:HEIGHTS] * (1.0 / (energy + epsilon))
+
+
+def boxed(total, correction):
     lane = lax.broadcasted_iota(jnp.int32, total.shape, 1)
 
     def after(field, d):
@@ -155,13 +161,8 @@
     def before(field, d):
         return jnp.where(lane < LANES - d, pltpu.roll(field, LANES - d, 1), 0.0)
 
-    if few:
-        right, left = total + after(total, 1), before(total, 1)
-        return (right + after(right, 2)) + (left + before(total + left, 2)) + correction
-    box = total + correction
-    for d in (1, 2, 3):
-        box = (box + after(total, d)) + before(total, d)
-    return box
+    right, left = total + after(total, 1), before(total, 1)
+    return (right + after(right, 2)) + (left + before(total + left, 2)) + correction
 
 
 def normalize(box_of, ref):
@@ -171,22 +172,23 @@
             ref[n, k : k + 8] = box * inverse[n]
 
 
-def inner_kernel(own_ref, e_ref, steer_ref, mid_ref, me_ref, done_ref, part_ref, cor_ref, halo_ref, side_ref, all_ref):
+def inner_kernel(own_ref, e_ref, steer_ref, mid_ref, me_ref, band_ref, done_ref, part_ref, cor_ref, halo_ref, side_ref, all_ref):
     side_beams(e_ref, steer_ref, halo_ref, side_ref)
     all_ref[...] = jnp.dot(halves(own_ref[HALO]), mid_ref[...], preferred_element_type=jnp.float32)
     all_ref[:, 5 * LANES :] += jnp.dot(halves(side_ref[3]), me_ref[...], preferred_element_type=jnp.float32)
     cor_ref[...] = all_ref[:, : 3 * LANES]
 
-    def box_of(rows):
-        ones = [own_ref[SLOT[m], rows] for m in range(8)] + [side_ref[n, rows] for n in range(3)]
-        twos = [a + b for a, b in zip(ones[:-1], ones[1:])]
-        fours = [a + b for a, b in zip(twos[:-2], twos[2:])]
-        for m, total in enumerate((fours[0], fours[0] + ones[4], fours[0] + twos[4])):
-            part_ref[m, rows] = total
-        sums = [fours[n] + (twos[n + 4] + ones[n + 6]) for n in range(5)]
-        return [boxed(total, all_ref[rows, (n + 3) * LANES : (n + 4) * LANES], False) for n, total in enumerate(sums)]
-
-    normalize(box_of, done_ref)
+    def summed(m):
+        total = None
+        for position in range(max(m - 3, 0), m + 4):
+            term = side_ref[position - 8] if position > 7 else own_ref[SLOT[position]]
+            total = term if total is None else total + term
+        return total
+
+    for m in range(3, 8):
+        done_ref[m - 3] = normalized(summed(m), all_ref[:, m * LANES : (m + 1) * LANES], band_ref)
+    for m in range(3):
+        part_ref[m] = summed(m)
 
 
 def outer_kernel(o_ref, part_ref, cor_ref, lines_ref, steer_ref, mo_ref, out_ref, halo_ref, side_ref, all_ref, edge_ref, done_ref, sems):
@@ -197,7 +199,7 @@
         near, next_, far = (side_ref[n, rows] for n in range(3))
         two = near + next_
         sums = (part_ref[0, rows] + (two + far), part_ref[1, rows] + two, part_ref[2, rows] + near)
-        return [boxed(total, all_ref[rows, n * LANES : (n + 1) * LANES], True) for n, total in enumerate(sums)]
+        return [boxed(total, all_ref[rows, n * LANES : (n + 1) * LANES]) for n, total in enumerate(sums)]
 
     normalize(box_of, edge_ref)
     odd = parity() == 1
@@ -229,7 +231,9 @@
     mid = matrix(lambda n: n, range(8), range(8))
     mo = matrix(lambda n: -1 - n, (0, 1, 2), (0, 1, 2))
     me = matrix(lambda n: 15 - n, (5, 6, 7), (5, 6, 7), 5)
-    return mid, mo, me
+    cell = np.arange(LANES)
+    band = np.abs(cell[:, None] - cell[None, :]) <= 3
+    return mid, mo, me, jnp.asarray(np.concatenate([band, band], axis=0), jnp.bfloat16)
 
 
 def steering(wavenumbers):
@@ -280,7 +284,7 @@
     gathered = gathered.reshape(16 * BLOCK, LANES)
     sides = (EDGE_TILES, 8, LANES)
     to_o, to_e, halo = call(edge_kernel, [sides, sides, (16, 8, LANES)], 4, 1000000)(gathered)
-    mid, mo, me = spread()
+    mid, mo, me, band = spread()
     to_o, to_e, wavenumbers = lax.optimization_barrier((to_o, to_e, wavenumbers))
     steer = steering(wavenumbers)
     side_o = lax.ppermute(to_o, "line", outer)
@@ -292,7 +296,7 @@
         14,
         1000000000,
         [strip, quad, pltpu.VMEM((ROWS, 8 * LANES), jnp.float32)],
-    )(own, side_e, steer, mid, me)
+    )(own, side_e, steer, mid, me, band)
     (result,) = call(
         outer_kernel,
         [(HEIGHTS, 8, LANES)],

time: 40.4 us -> 40.1 us (level)
    unnamed x16 -> x18, local copies, waits for them, and re-layouts: 1.26 us -> 1.25 us
where the time goes in v9:
time: 40.1 us; the launch traced here: 39.8 us
  blocking collectives  27.7 us (69%)
  starting transfers between devices  5.93 us (15%)
  Pallas kernels  4 us (10%)
  local copies, waits for them, and re-layouts  1.27 us (3%)
  other arithmetic  0.75 us (2%)
    all_to_all x1, blocking collectives, spectrum(): lax.all_to_all(packed, 'acq', 0, 0, tiled=True, axis_index_groups=[PLACE])  27.7 us
    ppermute x1, starting transfers between devices, spectrum(): side_o = lax.ppermute(to_o, 'line', outer)  4.01 us
    pallas_call x5, Pallas kernels, on(): pl.pallas_call(kernel, out_shape=[jax.ShapeDtypeStruct(shape, dtype) for...  4 us
    ppermute x1, starting transfers between devices, spectrum(): side_e = lax.ppermute(to_e, 'line', inner)  1.92 us
    unnamed x18, local copies, waits for them, and re-layouts  1.25 us
  transfers between devices with their start and end apart: 2, of which 0 were waited for; matrix products, arithmetic and copies ran while one was open for 2% of the time, Pallas kernels for 5%

profile of v9, /device:TPU:1, one launch (start us, length us, event | category | flops | bytes accessed | tf_op | source)
XLA Modules:
  0.0 39.8 jit_solution(7919754782283495430)
XLA Ops:
  0.0 0.0 copy-start
  0.0 1.0 %copy-done = f32[2,4,8,2048]{3,2,1,0:T(8,128)S(1)} copy-done((f32[2,4,8,2048]{3,2,1,0:T(8,128)S(1)}, f32[2,4,8,2048]{3,2,1,0:T(8,128)}, u32[]{:S(2)}) %copy-start) | copy-done | bytes 524312
  1.0 0.0 copy-start.5
  1.0 0.0 copy-start.8
  1.0 0.0 copy-start.6
  1.0 0.0 copy-start.7
  1.1 0.3 shard_map.91
  1.4 27.7 %all_to_all.5 = f32[16,68,1,128]{3,2,1,0:T(1,128)S(1)} all-to-all(f32[16,68,1,128]{3,2,1,0:T(1,128)S(1)} %bitcast.15), channel_id=1, replica_groups={{256,288,192,224,320,352,128,160,384,416,64,96,448,480,0,32},{257,289,1..., dimensions={0} | all-to-all | bytes 1114112 | tf_op jit(solution)/shard_map/all_to_all | solution.py:283
  29.1 0.2 shard_map.92
  29.2 4.0 %collective-permute-start = (f32[51,8,128]{2,1,0:T(8,128)S(1)}, f32[51,8,128]{2,1,0:T(8,128)S(1)}, u32[]{:S(2)}, u32[]{:S(2)}) collective-permute-start(f32[51,8,128]{2,1,0:T(8,128)S(1)} %get-tuple-element.16), channel_id=1, source_target_pairs={{1,2},{2,1},{3,4},{4,3},{5,6},{6,5},{7,8},{8,7},{9,10},{10,9},{11,... | collective-permute-start | bytes 626696 | tf_op jit(solution)/shard_map/ppermute | solution.py:290
  33.2 1.9 %collective-permute-start.1 = (f32[51,8,128]{2,1,0:T(8,128)S(1)}, f32[51,8,128]{2,1,0:T(8,128)S(1)}, u32[]{:S(2)}, u32[]{:S(2)}) collective-permute-start(f32[51,8,128]{2,1,0:T(8,128)S(1)} %get-tuple-element.19), channel_id=1, source_target_pairs={{0,1},{1,0},{2,3},{3,2},{4,5},{5,4},{6,7},{7,6},{8,9},{9,8},{10,11... | collective-permute-start | bytes 626696 | tf_op jit(solution)/shard_map/ppermute | solution.py:291
  35.2 0.0 copy-done.5
  35.2 0.0 copy-done.8
  35.2 0.1 select_reduce_fusion
  35.3 0.0 copy-done.6
  35.3 0.0 copy-done.7
  35.3 0.5 %fusion.2 = (f32[256,128]{1,0:T(8,128)S(1)}, f32[256,128]{1,0:T(8,128)S(1)}) fusion(f32[128]{0:T(128)S(1)} %select_reduce_fusion, f32[256]{0:T(256)S(1)} %copy-done.6, pred[128]{0:T(512)(128)(4,1)S(1)} %copy-done.7), kind=kLoop, calls=%fused_computation.8 | loop fusion | flops 131072 | bytes 263808 | tf_op jit(solution)/shard_map/jit(_where)/select_n | solution.py:247
  36.0 0.0 copy-start.1
  36.0 0.0 copy-start.3
  36.0 0.0 copy-start.4
  36.0 0.8 %shard_map.93.own_ref = f32[9,264,128]{2,1,0:T(8,128)S(1)} custom-call(f32[1088,128]{1,0:T(8,128)S(1)} %bitcast.14, f32[16,8,128]{2,1,0:T(8,128)S(1)} %get-tuple-element.17.halo_ref, bf16[512,384]{1,0:T(8,128)(2,1)S(1)} %pad_maximum_fusion.steer_ref), custom_call_target="tpu_custom_call" | custom-call | flops 1000000000 | bytes 1000000 | tf_op jit(solution)/shard_map/pallas_call | solution.py:261
  36.9 0.0 copy-start.2
  36.9 0.0 collective-permute-done.1.e_ref
  36.9 0.1 copy-done.1
  37.1 0.0 copy-done.3
  37.1 0.0 copy-done.4
  37.1 1.0 %shard_map.94 = (f32[5,256,128]{2,1,0:T(8,128)S(1)}, f32[3,264,128]{2,1,0:T(8,128)S(1)}, f32[264,384]{1,0:T(8,128)S(1)}) custom-call(f32[9,264,128]{2,1,0:T(8,128)S(1)} %shard_map.93.own_ref, f32[51,8,128]{2,1,0:T(8,128)S(1)} %collective-permute-done.1.e_ref, bf16[512,384]{1,0:T(8,128)(2,1)S(1)} %pad_maximum_fusion.steer_ref, ...), custom_call_target="tpu_custom_call" | custom-call | flops 1000000000 | bytes 1000000 | tf_op jit(solution)/shard_map/pallas_call | solution.py:261
  38.1 0.0 collective-permute-done.o_ref
  38.1 0.0 copy-done.2
  38.1 1.7 %shard_map.95 = bf16[256,8,128]{2,1,0:T(8,128)(2,1)} custom-call(f32[51,8,128]{2,1,0:T(8,128)S(1)} %collective-permute-done.o_ref, f32[3,264,128]{2,1,0:T(8,128)S(1)} %get-tuple-element.20.part_ref, f32[264,384]{1,0:T(8,128)S(1)} %get-tuple-element.21.cor_ref, f32[5,256,128]{2,1,0:T(8,128)S(1)} %get-tuple-element.22.lines_ref, ...), custom_call_target="tpu_custom_call" | custom-call | flops 1000000000 | bytes 1000000 | tf_op jit(solution)/shard_map/pallas_call | solution.py:261
  (4 shorter events, 0.1 us)
Async XLA Ops:
  0.0 1.0 %copy-start = (f32[2,4,8,2048]{3,2,1,0:T(8,128)S(1)}, f32[2,4,8,2048]{3,2,1,0:T(8,128)}, u32[]{:S(2)}) copy-start(f32[2,4,8,2048]{3,2,1,0:T(8,128)} %param.9) | copy-start | bytes 1572868
  1.0 34.1 %copy-start.5 = (pred[64,128]{1,0:T(32,128)(4,1)S(1)}, pred[64,128]{1,0:T(32,128)(4,1)}, u32[]{:S(2)}) copy-start(pred[64,128]{1,0:T(32,128)(4,1)} %constant.20.clone) | copy-start | bytes 24580
  1.0 34.1 %copy-start.8 = (f32[64]{0:T(128)S(1)}, f32[64]{0:T(128)}, u32[]{:S(2)}) copy-start(f32[64]{0:T(128)} %param.10) | copy-start | bytes 772
  1.0 34.2 %copy-start.6 = (f32[256]{0:T(256)S(1)}, f32[256]{0:T(256)}, u32[]{:S(2)}) copy-start(f32[256]{0:T(256)} %constant.21.clone) | copy-start | bytes 3076
  1.0 34.2 %copy-start.7 = (pred[128]{0:T(512)(128)(4,1)S(1)}, pred[128]{0:T(512)(128)(4,1)}, u32[]{:S(2)}) copy-start(pred[128]{0:T(512)(128)(4,1)} %constant.22.clone) | copy-start | bytes 388
  29.2 8.8 %collective-permute-start = (f32[51,8,128]{2,1,0:T(8,128)S(1)}, f32[51,8,128]{2,1,0:T(8,128)S(1)}, u32[]{:S(2)}, u32[]{:S(2)}) collective-permute-start(f32[51,8,128]{2,1,0:T(8,128)S(1)} %get-tuple-element.16), channel_id=1, source_target_pairs={{1,2},{2,1},{3,4},{4,3},{5,6},{6,5},{7,8},{8,7},{9,10},{10,9},{11,... | collective-permute-start | bytes 626696 | tf_op jit(solution)/shard_map/ppermute | solution.py:290
  33.2 3.7 %collective-permute-start.1 = (f32[51,8,128]{2,1,0:T(8,128)S(1)}, f32[51,8,128]{2,1,0:T(8,128)S(1)}, u32[]{:S(2)}, u32[]{:S(2)}) collective-permute-start(f32[51,8,128]{2,1,0:T(8,128)S(1)} %get-tuple-element.19), channel_id=1, source_target_pairs={{0,1},{1,0},{2,3},{3,2},{4,5},{5,4},{6,7},{7,6},{8,9},{9,8},{10,11... | collective-permute-start | bytes 626696 | tf_op jit(solution)/shard_map/ppermute | solution.py:291
  36.0 1.0 %copy-start.1 = (bf16[256,1024]{1,0:T(8,128)(2,1)S(1)}, bf16[256,1024]{1,0:T(8,128)(2,1)}, u32[]{:S(2)}) copy-start(bf16[256,1024]{1,0:T(8,128)(2,1)} %constant.16.clone.mid_ref) | copy-start | bytes 1572868
  36.0 1.1 %copy-start.3 = (bf16[256,384]{1,0:T(8,128)(2,1)S(1)}, bf16[256,384]{1,0:T(8,128)(2,1)}, u32[]{:S(2)}) copy-start(bf16[256,384]{1,0:T(8,128)(2,1)} %constant.18.clone.me_ref) | copy-start | bytes 589828
  36.0 1.1 %copy-start.4 = (bf16[256,128]{1,0:T(8,128)(2,1)S(1)}, bf16[256,128]{1,0:T(8,128)(2,1)}, u32[]{:S(2)}) copy-start(bf16[256,128]{1,0:T(8,128)(2,1)} %constant.19.clone.band_ref) | copy-start | bytes 196612
  36.9 1.2 %copy-start.2 = (bf16[256,384]{1,0:T(8,128)(2,1)S(1)}, bf16[256,384]{1,0:T(8,128)(2,1)}, u32[]{:S(2)}) copy-start(bf16[256,384]{1,0:T(8,128)(2,1)} %constant.17.clone.mo_ref) | copy-start | bytes 589828

commit v10 on v9

--- a/solution.py
+++ b/solution.py
@@ -215,6 +215,10 @@
         copy.wait()
 
 
+def copy_kernel(x_ref, out_ref):
+    out_ref[...] = x_ref[...]
+
+
 def spread():
     column = np.array([-3, -2, -1, 128, 129, 130])
     near = np.abs(column[:, None] - np.arange(LANES)[None, :]) <= 3
@@ -286,7 +290,8 @@
     to_o, to_e, halo = call(edge_kernel, [sides, sides, (16, 8, LANES)], 4, 1000000)(gathered)
     mid, mo, me, band = spread()
     to_o, to_e, wavenumbers = lax.optimization_barrier((to_o, to_e, wavenumbers))
-    steer = steering(wavenumbers)
+    (wavenumbers,) = call(copy_kernel, [(1, wavenumbers.shape[0])], 1, 1000)(wavenumbers.reshape(1, -1))
+    steer = steering(wavenumbers.reshape(-1))
     side_o = lax.ppermute(to_o, "line", outer)
     side_e = lax.ppermute(to_e, "line", inner)
     (own,) = call(own_kernel, [(9, ROWS, LANES)], 10, 1000000000)(gathered, halo, steer)

time: 40.1 us -> 40.1 us (level)
    pallas_call x5 -> x6, Pallas kernels: 4 us -> 4 us  [on(): pl.pallas_call(kernel, out_shape=[jax.ShapeDtypeStruct(shape, dtype) for...]
where the time goes in v10:
time: 40.1 us; the launch traced here: 39.8 us
  blocking collectives  27.7 us (69%)
  starting transfers between devices  5.93 us (15%)
  Pallas kernels  4 us (10%)
  local copies, waits for them, and re-layouts  1.27 us (3%)
  other arithmetic  0.75 us (2%)
    all_to_all x1, blocking collectives, spectrum(): lax.all_to_all(packed, 'acq', 0, 0, tiled=True, axis_index_groups=[PLACE])  27.7 us
    ppermute x1, starting transfers between devices, spectrum(): side_o = lax.ppermute(to_o, 'line', outer)  4.01 us
    pallas_call x6, Pallas kernels, on(): pl.pallas_call(kernel, out_shape=[jax.ShapeDtypeStruct(shape, dtype) for...  4 us
    ppermute x1, starting transfers between devices, spectrum(): side_e = lax.ppermute(to_e, 'line', inner)  1.92 us
    unnamed x18, local copies, waits for them, and re-layouts  1.26 us
  transfers between devices with their start and end apart: 2, of which 0 were waited for; matrix products, arithmetic and copies ran while one was open for 2% of the time, Pallas kernels for 5%

profile of v10, /device:TPU:1, one launch (start us, length us, event | category | flops | bytes accessed | tf_op | source)
XLA Modules:
  0.0 39.8 jit_solution(11354621559735301274)
XLA Ops:
  0.0 0.0 copy-start
  0.0 1.0 %copy-done = f32[2,4,8,2048]{3,2,1,0:T(8,128)S(1)} copy-done((f32[2,4,8,2048]{3,2,1,0:T(8,128)S(1)}, f32[2,4,8,2048]{3,2,1,0:T(8,128)}, u32[]{:S(2)}) %copy-start) | copy-done | bytes 524312
  1.0 0.0 copy-start.1
  1.0 0.0 copy-start.6
  1.0 0.0 copy-start.7
  1.0 0.0 copy-start.8
  1.1 0.3 shard_map.91
  1.4 27.7 %all_to_all.5 = f32[16,68,1,128]{3,2,1,0:T(1,128)S(1)} all-to-all(f32[16,68,1,128]{3,2,1,0:T(1,128)S(1)} %bitcast.17), channel_id=1, replica_groups={{256,288,192,224,320,352,128,160,384,416,64,96,448,480,0,32},{257,289,1..., dimensions={0} | all-to-all | bytes 1114112 | tf_op jit(solution)/shard_map/all_to_all | solution.py:287
  29.1 0.2 shard_map.92
  29.2 0.0 copy-done.1
  29.2 4.0 %collective-permute-start = (f32[51,8,128]{2,1,0:T(8,128)S(1)}, f32[51,8,128]{2,1,0:T(8,128)S(1)}, u32[]{:S(2)}, u32[]{:S(2)}) collective-permute-start(f32[51,8,128]{2,1,0:T(8,128)S(1)} %get-tuple-element.16), channel_id=1, source_target_pairs={{1,2},{2,1},{3,4},{4,3},{5,6},{6,5},{7,8},{8,7},{9,10},{10,9},{11,... | collective-permute-start | bytes 626696 | tf_op jit(solution)/shard_map/ppermute | solution.py:295
  33.3 1.9 %collective-permute-start.1 = (f32[51,8,128]{2,1,0:T(8,128)S(1)}, f32[51,8,128]{2,1,0:T(8,128)S(1)}, u32[]{:S(2)}, u32[]{:S(2)}) collective-permute-start(f32[51,8,128]{2,1,0:T(8,128)S(1)} %get-tuple-element.19), channel_id=1, source_target_pairs={{0,1},{1,0},{2,3},{3,2},{4,5},{5,4},{6,7},{7,6},{8,9},{9,8},{10,11... | collective-permute-start | bytes 626696 | tf_op jit(solution)/shard_map/ppermute | solution.py:296
  35.2 0.0 copy-done.6
  35.2 0.1 select_reduce_fusion
  35.3 0.0 copy-done.7
  35.3 0.0 copy-done.8
  35.3 0.5 %fusion.2 = (f32[256,128]{1,0:T(8,128)S(1)}, f32[256,128]{1,0:T(8,128)S(1)}) fusion(f32[128]{0:T(128)S(1)} %select_reduce_fusion, f32[256]{0:T(256)S(1)} %copy-done.7, pred[128]{0:T(512)(128)(4,1)S(1)} %copy-done.8), kind=kLoop, calls=%fused_computation.8 | loop fusion | flops 131072 | bytes 263808 | tf_op jit(solution)/shard_map/jit(_where)/select_n | solution.py:251
  36.0 0.0 copy-start.2
  36.0 0.0 copy-start.4
  36.0 0.0 copy-start.5
  36.1 0.8 %shard_map.94.own_ref = f32[9,264,128]{2,1,0:T(8,128)S(1)} custom-call(f32[1088,128]{1,0:T(8,128)S(1)} %bitcast.16, f32[16,8,128]{2,1,0:T(8,128)S(1)} %get-tuple-element.17.halo_ref, bf16[512,384]{1,0:T(8,128)(2,1)S(1)} %pad_maximum_fusion.steer_ref), custom_call_target="tpu_custom_call" | custom-call | flops 1000000000 | bytes 1000000 | tf_op jit(solution)/shard_map/pallas_call | solution.py:265
  36.9 0.0 copy-start.3
  36.9 0.0 collective-permute-done.1.e_ref
  36.9 0.1 copy-done.2
  37.1 0.0 copy-done.4
  37.1 0.0 copy-done.5
  37.1 1.0 %shard_map.95 = (f32[5,256,128]{2,1,0:T(8,128)S(1)}, f32[3,264,128]{2,1,0:T(8,128)S(1)}, f32[264,384]{1,0:T(8,128)S(1)}) custom-call(f32[9,264,128]{2,1,0:T(8,128)S(1)} %shard_map.94.own_ref, f32[51,8,128]{2,1,0:T(8,128)S(1)} %collective-permute-done.1.e_ref, bf16[512,384]{1,0:T(8,128)(2,1)S(1)} %pad_maximum_fusion.steer_ref, ...), custom_call_target="tpu_custom_call" | custom-call | flops 1000000000 | bytes 1000000 | tf_op jit(solution)/shard_map/pallas_call | solution.py:265
  38.1 0.0 collective-permute-done.o_ref
  38.1 0.0 copy-done.3
  38.1 1.7 %shard_map.96 = bf16[256,8,128]{2,1,0:T(8,128)(2,1)} custom-call(f32[51,8,128]{2,1,0:T(8,128)S(1)} %collective-permute-done.o_ref, f32[3,264,128]{2,1,0:T(8,128)S(1)} %get-tuple-element.20.part_ref, f32[264,384]{1,0:T(8,128)S(1)} %get-tuple-element.21.cor_ref, f32[5,256,128]{2,1,0:T(8,128)S(1)} %get-tuple-element.22.lines_ref, ...), custom_call_target="tpu_custom_call" | custom-call | flops 1000000000 | bytes 1000000 | tf_op jit(solution)/shard_map/pallas_call | solution.py:265
  (5 shorter events, 0.1 us)
Async XLA Ops:
  0.0 1.0 %copy-start = (f32[2,4,8,2048]{3,2,1,0:T(8,128)S(1)}, f32[2,4,8,2048]{3,2,1,0:T(8,128)}, u32[]{:S(2)}) copy-start(f32[2,4,8,2048]{3,2,1,0:T(8,128)} %param.9) | copy-start | bytes 1572868
  1.0 28.2 %copy-start.1 = (f32[64]{0:T(128)S(1)}, f32[64]{0:T(128)}, u32[]{:S(2)}) copy-start(f32[64]{0:T(128)} %param.10) | copy-start | bytes 772
  1.0 34.1 %copy-start.6 = (pred[64,128]{1,0:T(32,128)(4,1)S(1)}, pred[64,128]{1,0:T(32,128)(4,1)}, u32[]{:S(2)}) copy-start(pred[64,128]{1,0:T(32,128)(4,1)} %constant.20.clone) | copy-start | bytes 24580
  1.0 34.2 %copy-start.7 = (f32[256]{0:T(256)S(1)}, f32[256]{0:T(256)}, u32[]{:S(2)}) copy-start(f32[256]{0:T(256)} %constant.21.clone) | copy-start | bytes 3076
  1.0 34.3 %copy-start.8 = (pred[128]{0:T(512)(128)(4,1)S(1)}, pred[128]{0:T(512)(128)(4,1)}, u32[]{:S(2)}) copy-start(pred[128]{0:T(512)(128)(4,1)} %constant.22.clone) | copy-start | bytes 388
  29.2 8.8 %collective-permute-start = (f32[51,8,128]{2,1,0:T(8,128)S(1)}, f32[51,8,128]{2,1,0:T(8,128)S(1)}, u32[]{:S(2)}, u32[]{:S(2)}) collective-permute-start(f32[51,8,128]{2,1,0:T(8,128)S(1)} %get-tuple-element.16), channel_id=1, source_target_pairs={{1,2},{2,1},{3,4},{4,3},{5,6},{6,5},{7,8},{8,7},{9,10},{10,9},{11,... | collective-permute-start | bytes 626696 | tf_op jit(solution)/shard_map/ppermute | solution.py:295
  33.3 3.7 %collective-permute-start.1 = (f32[51,8,128]{2,1,0:T(8,128)S(1)}, f32[51,8,128]{2,1,0:T(8,128)S(1)}, u32[]{:S(2)}, u32[]{:S(2)}) collective-permute-start(f32[51,8,128]{2,1,0:T(8,128)S(1)} %get-tuple-element.19), channel_id=1, source_target_pairs={{0,1},{1,0},{2,3},{3,2},{4,5},{5,4},{6,7},{7,6},{8,9},{9,8},{10,11... | collective-permute-start | bytes 626696 | tf_op jit(solution)/shard_map/ppermute | solution.py:296
  36.0 1.0 %copy-start.2 = (bf16[256,1024]{1,0:T(8,128)(2,1)S(1)}, bf16[256,1024]{1,0:T(8,128)(2,1)}, u32[]{:S(2)}) copy-start(bf16[256,1024]{1,0:T(8,128)(2,1)} %constant.16.clone.mid_ref) | copy-start | bytes 1572868
  36.0 1.1 %copy-start.4 = (bf16[256,384]{1,0:T(8,128)(2,1)S(1)}, bf16[256,384]{1,0:T(8,128)(2,1)}, u32[]{:S(2)}) copy-start(bf16[256,384]{1,0:T(8,128)(2,1)} %constant.18.clone.me_ref) | copy-start | bytes 589828
  36.0 1.1 %copy-start.5 = (bf16[256,128]{1,0:T(8,128)(2,1)S(1)}, bf16[256,128]{1,0:T(8,128)(2,1)}, u32[]{:S(2)}) copy-start(bf16[256,128]{1,0:T(8,128)(2,1)} %constant.19.clone.band_ref) | copy-start | bytes 196612
  36.9 1.2 %copy-start.3 = (bf16[256,384]{1,0:T(8,128)(2,1)S(1)}, bf16[256,384]{1,0:T(8,128)(2,1)}, u32[]{:S(2)}) copy-start(bf16[256,384]{1,0:T(8,128)(2,1)} %constant.17.clone.mo_ref) | copy-start | bytes 589828

commit v11 on v10

--- a/solution.py
+++ b/solution.py
@@ -165,13 +165,6 @@
     return (right + after(right, 2)) + (left + before(total + left, 2)) + correction
 
 
-def normalize(box_of, ref):
-    inverse = [1.0 / (box.sum(axis=0, keepdims=True) + epsilon) for box in box_of(slice(HEIGHTS, ROWS))]
-    for k in range(0, HEIGHTS, 8):
-        for n, box in enumerate(box_of(slice(k, k + 8))):
-            ref[n, k : k + 8] = box * inverse[n]
-
-
 def inner_kernel(own_ref, e_ref, steer_ref, mid_ref, me_ref, band_ref, done_ref, part_ref, cor_ref, halo_ref, side_ref, all_ref):
     side_beams(e_ref, steer_ref, halo_ref, side_ref)
     all_ref[...] = jnp.dot(halves(own_ref[HALO]), mid_ref[...], preferred_element_type=jnp.float32)
@@ -191,7 +184,7 @@
         part_ref[m] = summed(m)
 
 
-def outer_kernel(o_ref, part_ref, cor_ref, lines_ref, steer_ref, mo_ref, out_ref, halo_ref, side_ref, all_ref, edge_ref, done_ref, sems):
+def outer_kernel(o_ref, part_ref, cor_ref, lines_ref, steer_ref, mo_ref, out_ref, halo_ref, side_ref, all_ref, done_ref, sems):
     side_beams(o_ref, steer_ref, halo_ref, side_ref)
     all_ref[...] = cor_ref[...] + jnp.dot(halves(side_ref[3]), mo_ref[...], preferred_element_type=jnp.float32)
 
@@ -201,12 +194,13 @@
         sums = (part_ref[0, rows] + (two + far), part_ref[1, rows] + two, part_ref[2, rows] + near)
         return [boxed(total, all_ref[rows, n * LANES : (n + 1) * LANES]) for n, total in enumerate(sums)]
 
-    normalize(box_of, edge_ref)
+    inverse = [1.0 / (box.sum(axis=0, keepdims=True) + epsilon) for box in box_of(slice(HEIGHTS, ROWS))]
     odd = parity() == 1
     copies = []
     for q in range(4):
         for k in range(64 * q, 64 * q + 64, 8):
-            tiles = [edge_ref[m, k : k + 8] for m in range(3)] + [lines_ref[m, k : k + 8] for m in range(5)]
+            near = [box * scale for box, scale in zip(box_of(slice(k, k + 8)), inverse)]
+            tiles = near + [lines_ref[m, k : k + 8] for m in range(5)]
             done_ref[k : k + 8] = jnp.stack(transposed(turned(tiles, odd))).astype(jnp.bfloat16)
         copy = pltpu.make_async_copy(done_ref.at[pl.ds(64 * q, 64)], out_ref.at[pl.ds(64 * q, 64)], sems.at[q])
         copy.start()
@@ -311,7 +305,6 @@
             strip,
             quad,
             pltpu.VMEM((ROWS, 3 * LANES), jnp.float32),
-            pltpu.VMEM((3, HEIGHTS, LANES), jnp.float32),
             pltpu.VMEM((HEIGHTS, 8, LANES), jnp.bfloat16),
             pltpu.SemaphoreType.DMA((4,)),
         ],

time: 40.1 us -> 40.1 us (level)
  no operation moved by 1% of the time
where the time goes in v11:
time: 40.1 us; the launch traced here: 39.8 us
  blocking collectives  27.7 us (69%)
  starting transfers between devices  5.93 us (15%)
  Pallas kernels  4 us (10%)
  local copies, waits for them, and re-layouts  1.27 us (3%)
  other arithmetic  0.75 us (2%)
    all_to_all x1, blocking collectives, spectrum(): lax.all_to_all(packed, 'acq', 0, 0, tiled=True, axis_index_groups=[PLACE])  27.7 us
    ppermute x1, starting transfers between devices, spectrum(): side_o = lax.ppermute(to_o, 'line', outer)  4.01 us
    pallas_call x6, Pallas kernels, on(): pl.pallas_call(kernel, out_shape=[jax.ShapeDtypeStruct(shape, dtype) for...  4 us
    ppermute x1, starting transfers between devices, spectrum(): side_e = lax.ppermute(to_e, 'line', inner)  1.92 us
    unnamed x18, local copies, waits for them, and re-layouts  1.26 us
  transfers between devices with their start and end apart: 2, of which 0 were waited for; matrix products, arithmetic and copies ran while one was open for 2% of the time, Pallas kernels for 5%

profile of v11, /device:TPU:1, one launch (start us, length us, event | category | flops | bytes accessed | tf_op | source)
XLA Modules:
  0.0 39.8 jit_solution(17080703599561067823)
XLA Ops:
  0.0 0.0 copy-start
  0.0 1.0 %copy-done = f32[2,4,8,2048]{3,2,1,0:T(8,128)S(1)} copy-done((f32[2,4,8,2048]{3,2,1,0:T(8,128)S(1)}, f32[2,4,8,2048]{3,2,1,0:T(8,128)}, u32[]{:S(2)}) %copy-start) | copy-done | bytes 524312
  1.0 0.0 copy-start.1
  1.0 0.0 copy-start.6
  1.0 0.0 copy-start.7
  1.0 0.0 copy-start.8
  1.1 0.3 shard_map.91
  1.4 27.7 %all_to_all.5 = f32[16,68,1,128]{3,2,1,0:T(1,128)S(1)} all-to-all(f32[16,68,1,128]{3,2,1,0:T(1,128)S(1)} %bitcast.17), channel_id=1, replica_groups={{256,288,192,224,320,352,128,160,384,416,64,96,448,480,0,32},{257,289,1..., dimensions={0} | all-to-all | bytes 1114112 | tf_op jit(solution)/shard_map/all_to_all | solution.py:281
  29.1 0.2 shard_map.92
  29.2 0.0 copy-done.1
  29.2 4.0 %collective-permute-start = (f32[51,8,128]{2,1,0:T(8,128)S(1)}, f32[51,8,128]{2,1,0:T(8,128)S(1)}, u32[]{:S(2)}, u32[]{:S(2)}) collective-permute-start(f32[51,8,128]{2,1,0:T(8,128)S(1)} %get-tuple-element.16), channel_id=1, source_target_pairs={{1,2},{2,1},{3,4},{4,3},{5,6},{6,5},{7,8},{8,7},{9,10},{10,9},{11,... | collective-permute-start | bytes 626696 | tf_op jit(solution)/shard_map/ppermute | solution.py:289
  33.3 1.9 %collective-permute-start.1 = (f32[51,8,128]{2,1,0:T(8,128)S(1)}, f32[51,8,128]{2,1,0:T(8,128)S(1)}, u32[]{:S(2)}, u32[]{:S(2)}) collective-permute-start(f32[51,8,128]{2,1,0:T(8,128)S(1)} %get-tuple-element.19), channel_id=1, source_target_pairs={{0,1},{1,0},{2,3},{3,2},{4,5},{5,4},{6,7},{7,6},{8,9},{9,8},{10,11... | collective-permute-start | bytes 626696 | tf_op jit(solution)/shard_map/ppermute | solution.py:290
  35.2 0.0 copy-done.6
  35.2 0.1 select_reduce_fusion
  35.3 0.0 copy-done.7
  35.3 0.0 copy-done.8
  35.3 0.5 %fusion.2 = (f32[256,128]{1,0:T(8,128)S(1)}, f32[256,128]{1,0:T(8,128)S(1)}) fusion(f32[128]{0:T(128)S(1)} %select_reduce_fusion, f32[256]{0:T(256)S(1)} %copy-done.7, pred[128]{0:T(512)(128)(4,1)S(1)} %copy-done.8), kind=kLoop, calls=%fused_computation.8 | loop fusion | flops 131072 | bytes 263808 | tf_op jit(solution)/shard_map/jit(_where)/select_n | solution.py:245
  36.0 0.0 copy-start.2
  36.0 0.0 copy-start.4
  36.0 0.0 copy-start.5
  36.1 0.8 %shard_map.94.own_ref = f32[9,264,128]{2,1,0:T(8,128)S(1)} custom-call(f32[1088,128]{1,0:T(8,128)S(1)} %bitcast.16, f32[16,8,128]{2,1,0:T(8,128)S(1)} %get-tuple-element.17.halo_ref, bf16[512,384]{1,0:T(8,128)(2,1)S(1)} %pad_maximum_fusion.steer_ref), custom_call_target="tpu_custom_call" | custom-call | flops 1000000000 | bytes 1000000 | tf_op jit(solution)/shard_map/pallas_call | solution.py:259
  36.9 0.0 copy-start.3
  36.9 0.0 collective-permute-done.1.e_ref
  36.9 0.1 copy-done.2
  37.1 0.0 copy-done.4
  37.1 0.0 copy-done.5
  37.1 1.0 %shard_map.95 = (f32[5,256,128]{2,1,0:T(8,128)S(1)}, f32[3,264,128]{2,1,0:T(8,128)S(1)}, f32[264,384]{1,0:T(8,128)S(1)}) custom-call(f32[9,264,128]{2,1,0:T(8,128)S(1)} %shard_map.94.own_ref, f32[51,8,128]{2,1,0:T(8,128)S(1)} %collective-permute-done.1.e_ref, bf16[512,384]{1,0:T(8,128)(2,1)S(1)} %pad_maximum_fusion.steer_ref, ...), custom_call_target="tpu_custom_call" | custom-call | flops 1000000000 | bytes 1000000 | tf_op jit(solution)/shard_map/pallas_call | solution.py:259
  38.1 0.0 collective-permute-done.o_ref
  38.1 0.0 copy-done.3
  38.1 1.7 %shard_map.96 = bf16[256,8,128]{2,1,0:T(8,128)(2,1)} custom-call(f32[51,8,128]{2,1,0:T(8,128)S(1)} %collective-permute-done.o_ref, f32[3,264,128]{2,1,0:T(8,128)S(1)} %get-tuple-element.20.part_ref, f32[264,384]{1,0:T(8,128)S(1)} %get-tuple-element.21.cor_ref, f32[5,256,128]{2,1,0:T(8,128)S(1)} %get-tuple-element.22.lines_ref, ...), custom_call_target="tpu_custom_call" | custom-call | flops 1000000000 | bytes 1000000 | tf_op jit(solution)/shard_map/pallas_call | solution.py:259
  (5 shorter events, 0.1 us)
Async XLA Ops:
  0.0 1.0 %copy-start = (f32[2,4,8,2048]{3,2,1,0:T(8,128)S(1)}, f32[2,4,8,2048]{3,2,1,0:T(8,128)}, u32[]{:S(2)}) copy-start(f32[2,4,8,2048]{3,2,1,0:T(8,128)} %param.9) | copy-start | bytes 1572868
  1.0 28.2 %copy-start.1 = (f32[64]{0:T(128)S(1)}, f32[64]{0:T(128)}, u32[]{:S(2)}) copy-start(f32[64]{0:T(128)} %param.10) | copy-start | bytes 772
  1.0 34.1 %copy-start.6 = (pred[64,128]{1,0:T(32,128)(4,1)S(1)}, pred[64,128]{1,0:T(32,128)(4,1)}, u32[]{:S(2)}) copy-start(pred[64,128]{1,0:T(32,128)(4,1)} %constant.20.clone) | copy-start | bytes 24580
  1.0 34.2 %copy-start.7 = (f32[256]{0:T(256)S(1)}, f32[256]{0:T(256)}, u32[]{:S(2)}) copy-start(f32[256]{0:T(256)} %constant.21.clone) | copy-start | bytes 3076
  1.0 34.3 %copy-start.8 = (pred[128]{0:T(512)(128)(4,1)S(1)}, pred[128]{0:T(512)(128)(4,1)}, u32[]{:S(2)}) copy-start(pred[128]{0:T(512)(128)(4,1)} %constant.22.clone) | copy-start | bytes 388
  29.2 8.8 %collective-permute-start = (f32[51,8,128]{2,1,0:T(8,128)S(1)}, f32[51,8,128]{2,1,0:T(8,128)S(1)}, u32[]{:S(2)}, u32[]{:S(2)}) collective-permute-start(f32[51,8,128]{2,1,0:T(8,128)S(1)} %get-tuple-element.16), channel_id=1, source_target_pairs={{1,2},{2,1},{3,4},{4,3},{5,6},{6,5},{7,8},{8,7},{9,10},{10,9},{11,... | collective-permute-start | bytes 626696 | tf_op jit(solution)/shard_map/ppermute | solution.py:289
  33.3 3.7 %collective-permute-start.1 = (f32[51,8,128]{2,1,0:T(8,128)S(1)}, f32[51,8,128]{2,1,0:T(8,128)S(1)}, u32[]{:S(2)}, u32[]{:S(2)}) collective-permute-start(f32[51,8,128]{2,1,0:T(8,128)S(1)} %get-tuple-element.19), channel_id=1, source_target_pairs={{0,1},{1,0},{2,3},{3,2},{4,5},{5,4},{6,7},{7,6},{8,9},{9,8},{10,11... | collective-permute-start | bytes 626696 | tf_op jit(solution)/shard_map/ppermute | solution.py:290
  36.0 1.0 %copy-start.2 = (bf16[256,1024]{1,0:T(8,128)(2,1)S(1)}, bf16[256,1024]{1,0:T(8,128)(2,1)}, u32[]{:S(2)}) copy-start(bf16[256,1024]{1,0:T(8,128)(2,1)} %constant.16.clone.mid_ref) | copy-start | bytes 1572868
  36.0 1.1 %copy-start.4 = (bf16[256,384]{1,0:T(8,128)(2,1)S(1)}, bf16[256,384]{1,0:T(8,128)(2,1)}, u32[]{:S(2)}) copy-start(bf16[256,384]{1,0:T(8,128)(2,1)} %constant.18.clone.me_ref) | copy-start | bytes 589828
  36.0 1.1 %copy-start.5 = (bf16[256,128]{1,0:T(8,128)(2,1)S(1)}, bf16[256,128]{1,0:T(8,128)(2,1)}, u32[]{:S(2)}) copy-start(bf16[256,128]{1,0:T(8,128)(2,1)} %constant.19.clone.band_ref) | copy-start | bytes 196612
  36.9 1.2 %copy-start.3 = (bf16[256,384]{1,0:T(8,128)(2,1)S(1)}, bf16[256,384]{1,0:T(8,128)(2,1)}, u32[]{:S(2)}) copy-start(bf16[256,384]{1,0:T(8,128)(2,1)} %constant.17.clone.mo_ref) | copy-start | bytes 589828
